TPU v7x, 128 devices: a whole 4x4x4 slice. The times are simulated.
128 devices in a mesh: own: 32 (over x, z, core), rep: 4 (over y).
Axes of the slice: x: 4, y: 4, z: 4, core: 2. Of those that a mesh axis runs over, the one named last changes fastest.
Arguments:
- block_pool: bfloat16 [8192, 64, 576], P(('own', 'rep')), may hold values from -16 to 16
- sel_index: int32 [4096], P(('own', 'rep')), may hold values from 0 to 63
- sel_layer: int32 [4096], P(('own', 'rep')), may hold values from 0 to 15, as said below
- counts: int32 [128], P(('own', 'rep')), may hold values from 8 to 32, as said below
Outputs:
- quant_codes: bfloat16 [32, 4, 32, 8, 18432], P('own', 'rep')
- quant_steps: float32 [32, 288], P('own')
- clip_error: float32 [32, 288], P('own')
Inputs may be any that keep to these rules, and one draw needn't show every extreme that they name: `sel_layer`: among the 32 entries of one device, at most 8 name any one layer; the first 8 entries of every device all name one and the same layer. `counts`: some device has all 32 entries live.
All inputs are finite; a program needn't handle non-finite values.
Results may differ from a plain program's by a relative error of at most 0.001.
Values may be sent and summed in bfloat16 or wider, within the bound.
No kernel may reach another device: no remote copies, remote signals or barrier semaphores. Data moves between devices by JAX's collectives and lax.ppermute only.
A program may use at most 128 MiB of HBM per device.

v0:
```python
import jax
import jax.numpy as jnp
from jax import lax
from jax.sharding import PartitionSpec as P

SLICES = 2


headroom = 0.5


def sent_to_all(x, axis):
    count = lax.axis_size(axis)
    return lax.all_to_all(jnp.broadcast_to(x[None], (count, *x.shape)), axis, 0, 0, tiled=True)


def of_everyone(x, axis):
    return sent_to_all(x, axis).max(axis=0)


def over_copies(x, axis):
    everything = sent_to_all(x, axis)
    return jnp.sum(everything, axis=0)


def slot_table(index_row, layer_row, live_count, group_layer, capacity):
    n_select = index_row.shape[0]
    is_live = jnp.arange(n_select) < live_count
    matches = (layer_row[None, :] == group_layer[:, None]) & is_live[None, :]
    ranking = jnp.cumsum(matches.astype(jnp.int32), axis=1) - 1
    slot_hit = matches[:, None, :] & (ranking[:, None, :] == jnp.arange(capacity)[None, :, None])
    chosen = jnp.sum(jnp.where(slot_hit, index_row[None, None, :], 0), axis=2)
    filled = jnp.any(slot_hit, axis=2)
    return (chosen, filled)


def body(block_pool, sel_index, sel_layer, counts):
    own_count = lax.axis_size("own")
    rep_count = lax.axis_size("rep")
    n_select = sel_index.shape[0]
    capacity = n_select // 4
    block_tokens = block_pool.shape[1]
    latent_width = block_pool.shape[2]
    half_width = latent_width // SLICES
    flat_width = block_tokens * half_width
    layer_count = own_count // SLICES
    layer_ids = jnp.arange(layer_count)
    chosen, filled = slot_table(sel_index, sel_layer, counts[0], layer_ids, capacity)
    pool_rows = block_pool.reshape(block_pool.shape[0], block_tokens * latent_width)
    picked = jnp.take(pool_rows, chosen.reshape(-1), axis=0)
    picked = jnp.where(filled.reshape(-1)[:, None], picked, jnp.zeros((), picked.dtype))
    picked = picked.reshape(layer_count, capacity, block_tokens, SLICES, half_width)
    parted = picked.transpose(0, 3, 1, 2, 4).reshape(own_count, capacity, flat_width)
    denominator = float(own_count * rep_count * capacity * block_tokens)
    arrived = lax.all_to_all(parted, "own", split_axis=0, concat_axis=0, tiled=True)
    flat_peak = jnp.max(jnp.abs(arrived), axis=(0, 1)).astype(jnp.float32)
    local_peak = jnp.max(flat_peak.reshape(block_tokens, half_width), axis=0)
    peak_abs = of_everyone(local_peak, "rep")
    step_size = headroom * jnp.maximum(peak_abs, 1.0) / 127.0
    step_flat = jnp.tile(step_size, block_tokens)
    values = arrived.astype(jnp.float32)
    encoded = jnp.clip(values / step_flat, -127.0, 127.0).astype(jnp.bfloat16)
    encoded = lax.optimization_barrier(encoded)
    decoded = encoded.astype(jnp.float32) * step_flat
    flat_error = jnp.sum((values - decoded) ** 2, axis=(0, 1))
    sq_error = jnp.sum(flat_error.reshape(block_tokens, half_width), axis=0)
    error_all = over_copies(sq_error, "rep")
    steps_out = step_size[None, :]
    error_out = (error_all / (step_size * step_size * denominator))[None, :]
    return (encoded[None, None], steps_out, error_out)


def solution(mesh):
    return jax.shard_map(
        body,
        mesh=mesh,
        in_specs=(
            P(("own", "rep"), None, None),
            P(("own", "rep")),
            P(("own", "rep")),
            P(("own", "rep")),
        ),
        out_specs=(P("own", "rep", None, None, None), P("own", None), P("own", None)),
        check_vma=False,
    )
```

profile of v0, /device:TPU:32, one launch (start us, length us, event | category | flops | bytes accessed | tf_op | source)
XLA Modules:
  0.0 261.5 jit_solution(13616483861530412258)
XLA Ops:
  1.3 0.7 fusion.7
  2.0 0.2 reduce_window_sum.11
  2.1 0.4 fusion.6
  2.5 1.0 select_reduce_fusion
  3.5 0.1 reshape.175
  3.7 9.9 %reshape.174 = bf16[64,36864]{1,0:T(8,128)(2,1)} reshape(bf16[64,64,576]{2,1,0:T(8,128)(2,1)} %param.4) | data formatting | bytes 9437184 | tf_op jit(solution)/shard_map/reshape | solution.py:49
  13.6 21.4 %gather_fusion = bf16[128,36864]{1,0:T(8,128)(2,1)} fusion(bf16[64,36864]{1,0:T(8,128)(2,1)} %reshape.174, s32[1024]{0:T(1024)S(1)} %pad_clamp_fusion), kind=kCustom, calls=%fused_computation | custom fusion | bytes 18874880 | tf_op jit(solution)/shard_map/jit(_take)/gather | solution.py:50
  35.0 24.6 %gather.7 = bf16[16,8,64,2,288]{4,3,2,1,0:T(2,128)(2,1)} reshape(bf16[128,36864]{1,0:T(8,128)(2,1)} %gather_fusion) | data formatting | bytes 18874368 | tf_op jit(solution)/shard_map/jit(_take)/gather | solution.py:50
  59.6 16.3 %fusion.4 = bf16[16,2,8,64,288]{4,1,3,2,0:T(2,128)(2,1)S(1)} fusion(pred[16,8]{1,0:T(8,128)(4,1)S(1)} %fusion.6, bf16[16,8,64,2,288]{4,3,2,1,0:T(2,128)(2,1)} %gather.7, pred[16,8]{1,0:T(8,128)(4,1)S(1)} %compare_and_fusion), kind=kLoop, calls=%fused_computation.9 | loop fusion | flops 9437184 | bytes 18874624 | tf_op jit(solution)/shard_map/transpose | solution.py:53
  75.9 6.8 %copy.10 = bf16[16,2,8,64,288]{4,3,2,1,0:T(8,128)(2,1)} copy(bf16[16,2,8,64,288]{4,1,3,2,0:T(2,128)(2,1)S(1)} %fusion.4) | data formatting | bytes 18874368 | tf_op jit(solution)/shard_map/transpose | solution.py:53
  82.7 20.9 %reshape.176 = bf16[32,8,18432]{2,1,0:T(8,128)(2,1)} reshape(bf16[16,2,8,64,288]{4,3,2,1,0:T(8,128)(2,1)} %copy.10) | data formatting | bytes 18874368 | tf_op jit(solution)/shard_map/reshape | solution.py:53
  103.6 113.4 %all_to_all.17 = bf16[32,8,18432]{2,1,0:T(8,128)(2,1)S(1)} all-to-all(bf16[32,8,18432]{2,1,0:T(8,128)(2,1)} %reshape.176), channel_id=1, replica_groups=mesh['own'=32,'rep'=4] {'own'}, dimensions={0} | all-to-all | bytes 18874368 | tf_op jit(solution)/shard_map/all_to_all | solution.py:55
  217.1 0.0 copy-start
  217.1 3.6 %copy-done = bf16[32,8,18432]{2,1,0:T(8,128)(2,1)} copy-done((bf16[32,8,18432]{2,1,0:T(8,128)(2,1)}, bf16[32,8,18432]{2,1,0:T(8,128)(2,1)S(1)}, u32[]{:S(2)}) %copy-start) | copy-done | bytes 9437208
  220.7 1.1 abs_reduce_fusion
  221.8 0.1 reduce_max.35
  221.9 9.6 %all_to_all.18 = f32[4,1,288]{2,1,0:T(1,128)S(1)} all-to-all(f32[4,1,288]{2,1,0:T(1,128)S(1)} %broadcast_in_dim.64), channel_id=1, replica_groups=mesh['own'=32,'rep'=4] {'rep'}, dimensions={0} | all-to-all | bytes 9216 | tf_op jit(solution)/shard_map/all_to_all | solution.py:14
  231.6 0.1 div.30
  231.7 9.8 %fusion.1 = bf16[32,8,18432]{2,1,0:T(8,128)(2,1)} fusion(bf16[32,8,18432]{2,1,0:T(8,128)(2,1)} %copy-done, f32[18432]{0:T(1024)S(1)} %div.30), kind=kLoop, calls=%fused_computation.6 | loop fusion | flops 18874368 | bytes 18948096 | tf_op jit(solution)/shard_map/convert_element_type | solution.py:62
  241.5 10.1 %fusion.3 = f32[18432]{0:T(1024)S(1)} fusion(bf16[32,8,18432]{2,1,0:T(8,128)(2,1)} %copy-done, bf16[32,8,18432]{2,1,0:T(8,128)(2,1)} %fusion.1, f32[18432]{0:T(1024)S(1)} %div.30), kind=kLoop, calls=%fused_computation.8 | loop fusion | flops 28293120 | bytes 19021824 | tf_op jit(solution)/shard_map/reduce_sum | solution.py:65
  251.7 0.1 reshape.177
  251.8 0.6 broadcast_in_dim.66
  252.4 3.2 %all-to-all-start.2 = ((f32[4,1,288]{2,1,0:T(1,128)}), f32[4,1,288]{2,1,0:T(1,128)S(1)}, u32[]{:S(2)}, u32[]{:S(2)}) async-start(f32[4,1,288]{2,1,0:T(1,128)} %broadcast_in_dim.66), calls=%async_computation.2 | async-start | bytes 12288 | tf_op jit(solution)/shard_map/all_to_all | solution.py:14
  255.6 0.6 div.33
  256.2 4.7 %all-to-all-done.2 = f32[4,1,288]{2,1,0:T(1,128)S(1)} async-done(((f32[4,1,288]{2,1,0:T(1,128)}), f32[4,1,288]{2,1,0:T(1,128)S(1)}, u32[]{:S(2)}, u32[]{:S(2)}) %all-to-all-start.2) | async-done | bytes 4640 | tf_op jit(solution)/shard_map/all_to_all | solution.py:14
  260.9 0.6 multiply_divide_fusion
  (12 shorter events, 0.2 us)
Async XLA Ops:
  217.1 3.6 %copy-start = (bf16[32,8,18432]{2,1,0:T(8,128)(2,1)}, bf16[32,8,18432]{2,1,0:T(8,128)(2,1)S(1)}, u32[]{:S(2)}) copy-start(bf16[32,8,18432]{2,1,0:T(8,128)(2,1)S(1)} %all_to_all.17) | copy-start | bytes 28311556
  252.4 8.5 %all-to-all-start.2 = ((f32[4,1,288]{2,1,0:T(1,128)}), f32[4,1,288]{2,1,0:T(1,128)S(1)}, u32[]{:S(2)}, u32[]{:S(2)}) async-start(f32[4,1,288]{2,1,0:T(1,128)} %broadcast_in_dim.66), calls=%async_computation.2 | async-start | bytes 12288 | tf_op jit(solution)/shard_map/all_to_all | solution.py:14
where the time goes:
time: 264 us; the launch traced here: 262 us
  blocking collectives  123 us (47%)
  local copies, waits for them, and re-layouts  88.9 us (34%)
  other arithmetic  40.3 us (15%)
  waiting for transfers between devices  4.71 us (2%)
  starting transfers between devices  3.25 us (1%)
    all_to_all x1, blocking collectives, body(): lax.all_to_all(parted, 'own', split_axis=0, concat_axis=0, tiled=True)  113 us
    gather x2, local copies, waits for them, and re-layouts, body(): picked = jnp.take(pool_rows, chosen.reshape(-1), axis=0)  46 us
    reshape x1, local copies, waits for them, and re-layouts, body(): picked.transpose(0, 3, 1, 2, 4).reshape(own_count, capacity, flat_width)  20.9 us
    transpose x1, other arithmetic, body(): picked.transpose(0, 3, 1, 2, 4).reshape(own_count, capacity, flat_width)  16.3 us
    reduce_sum x1, other arithmetic, body(): flat_error = jnp.sum((values - decoded) ** 2, axis=(0, 1))  10.1 us
    reshape x1, local copies, waits for them, and re-layouts, body(): block_pool.reshape(block_pool.shape[0], block_tokens * latent_width)  9.91 us
    convert_element_type x1, other arithmetic, body(): encoded = jnp.clip(values / step_flat, -127.0, 127.0).astype(jnp.bfloat16)  9.83 us
    all_to_all x1, blocking collectives, sent_to_all(): lax.all_to_all(jnp.broadcast_to(x[None], (count, *x.shape)), axis, 0, 0,...  9.57 us
  transfers between devices with their start and end apart: 1, of which 1 were waited for; matrix products, arithmetic and copies ran while one was open for 0% of the time, Pallas kernels for 0%

commit v1 on v0

v1 whole, which is shorter than its diff:
```python
import functools
import jax
import jax.numpy as jnp
from jax import lax
from jax.experimental import pallas as pl
from jax.experimental.pallas import tpu as pltpu
from jax.sharding import PartitionSpec as P

SLICES = 2
CAP = 8
LANES = 128
PITCH = 72
headroom = 0.5


def peak_kernel(layers, index_ref, layer_ref, count_ref, pool_ref, peak_ref, held, acc, sems):
    live = count_ref[0]

    def fetch(j):
        return pltpu.make_async_copy(pool_ref.at[index_ref[j]], held.at[j], sems.at[j])

    def start(j, carry):
        fetch(j).start()
        return carry

    lax.fori_loop(0, live, start, 0)
    acc[...] = jnp.zeros_like(acc)

    def one(j, carry):
        fetch(j).wait()
        layer = layer_ref[j]
        tokens, width = held.shape[1:]
        values = jnp.abs(held[j].astype(jnp.float32)).reshape(tokens // 8, 8, width)
        acc[layer] = jnp.maximum(acc[layer], jnp.max(values, axis=0))
        return carry

    lax.fori_loop(0, live, one, 0)
    peak_ref[...] = jnp.max(acc[...], axis=1)


def encode_kernel(
    layers, index_ref, layer_ref, count_ref, me_ref, pool_ref, peak_ref,
    codes_ref, error_ref, steps_ref, held, spread, slots, filled, sems,
):
    step = pl.program_id(0)
    live = count_ref[0]
    tokens, width = held.shape[1:]
    half = width // SLICES
    tiles = spread.shape[0]

    def fetch(j):
        return pltpu.make_async_copy(pool_ref.at[index_ref[j]], held.at[j], sems.at[j])

    @pl.when(step == 0)
    def _():
        def clear(layer, carry):
            filled[layer] = 0
            return carry

        lax.fori_loop(0, layers, clear, 0)

        def start(j, carry):
            fetch(j).start()
            layer = layer_ref[j]
            at = filled[layer]
            slots[layer * CAP + at] = j
            filled[layer] = at + 1
            return carry

        lax.fori_loop(0, live, start, 0)

        def wait(j, carry):
            fetch(j).wait()
            return carry

        lax.fori_loop(0, live, wait, 0)
        own = peak_ref[pl.ds(me_ref[0] // SLICES, 1), :]
        own = jnp.where(me_ref[0] % SLICES == 0, own[:, :half], own[:, half:])
        steps_ref[...] = headroom * jnp.maximum(own, 1.0) / 127.0

    held_slots = filled[step]
    scale = headroom * jnp.maximum(peak_ref[pl.ds(step, 1), :], 1.0) / 127.0

    @pl.when(held_slots == 0)
    def _():
        codes_ref[...] = jnp.zeros_like(codes_ref)
        error_ref[...] = jnp.zeros_like(error_ref)

    @pl.when(held_slots > 0)
    def _():
        def code(c, total):
            values = held[slots[step * CAP + c]].astype(jnp.float32)
            coded = jnp.clip(values / scale, -127.0, 127.0).astype(jnp.bfloat16).astype(jnp.float32)
            rows = pl.ds(pl.multiple_of(c * PITCH, 8), tokens)
            for j in range(tiles):
                lanes = min(LANES, width - j * LANES)
                spread[j, rows, :lanes] = coded[:, j * LANES : j * LANES + lanes]
            miss = values - coded * scale
            return total + jnp.sum((miss * miss).reshape(tokens // 8, 8, width), axis=0)

        total = lax.fori_loop(0, held_slots, code, jnp.zeros((8, width), jnp.float32))
        error_ref[0] = jnp.sum(total, axis=0, keepdims=True)

        def blank(c, carry):
            for j in range(tiles):
                spread[j, pl.ds(pl.multiple_of(c * PITCH, 8), tokens), :] = jnp.zeros((tokens, LANES), jnp.float32)
            return carry

        lax.fori_loop(held_slots, CAP, blank, 0)

        lane = lax.broadcasted_iota(jnp.int32, (CAP, LANES), 1)
        group = 4 * half

        def four_tokens(u, carry):
            rows = [
                [spread[j, pl.ds(4 * u + q, CAP, stride=PITCH), :] for j in range(tiles)]
                for q in range(4)
            ]
            for h in range(SLICES):
                turned = {}
                for i in range(group // LANES):
                    out, at = None, 0
                    while at < LANES:
                        flat = i * LANES + at
                        q = flat // half
                        source = flat - q * half + h * half
                        j = source // LANES
                        run = min(LANES - source % LANES, (q + 1) * half - flat, LANES - at)
                        if (q, j) not in turned:
                            shift = (at - source) % LANES
                            turned[q, j] = pltpu.roll(rows[q][j], shift, 1) if shift else rows[q][j]
                        piece = turned[q, j]
                        out = piece if out is None else jnp.where(lane >= at, piece, out)
                        at += run
                    place = pl.ds(pl.multiple_of(u * group + i * LANES, LANES), LANES)
                    codes_ref[h, :, place] = out.astype(jnp.bfloat16)
            return carry

        lax.fori_loop(0, tokens // 4, four_tokens, 0)


def local_peaks(block_pool, sel_index, sel_layer, counts, layers):
    n_select = sel_index.shape[0]
    tokens, width = block_pool.shape[1:]
    smem = pl.BlockSpec(memory_space=pltpu.SMEM)
    return pl.pallas_call(
        functools.partial(peak_kernel, layers),
        out_shape=jax.ShapeDtypeStruct((layers, width), jnp.float32),
        in_specs=[smem, smem, smem, pl.BlockSpec(memory_space=pl.ANY)],
        out_specs=pl.BlockSpec(memory_space=pltpu.VMEM),
        scratch_shapes=[
            pltpu.VMEM((n_select, tokens, width), jnp.bfloat16),
            pltpu.VMEM((layers, 8, width), jnp.float32),
            pltpu.SemaphoreType.DMA((n_select,)),
        ],
        name="peaks",
    )(sel_index, sel_layer, counts, block_pool)


def encode(block_pool, sel_index, sel_layer, counts, me, peak, layers):
    n_select = sel_index.shape[0]
    tokens, width = block_pool.shape[1:]
    half = width // SLICES
    tiles = pl.cdiv(width, LANES)
    smem = pl.BlockSpec(memory_space=pltpu.SMEM)
    return pl.pallas_call(
        functools.partial(encode_kernel, layers),
        grid=(layers,),
        out_shape=(
            jax.ShapeDtypeStruct((layers * SLICES, CAP, tokens * half), jnp.bfloat16),
            jax.ShapeDtypeStruct((layers, 1, width), jnp.float32),
            jax.ShapeDtypeStruct((1, half), jnp.float32),
        ),
        in_specs=[smem, smem, smem, smem, pl.BlockSpec(memory_space=pl.ANY), pl.BlockSpec((layers, width), lambda l: (0, 0))],
        out_specs=(
            pl.BlockSpec((SLICES, CAP, tokens * half), lambda l: (l, 0, 0)),
            pl.BlockSpec((1, 1, width), lambda l: (l, 0, 0)),
            pl.BlockSpec((1, half), lambda l: (0, 0)),
        ),
        scratch_shapes=[
            pltpu.VMEM((n_select, tokens, width), jnp.bfloat16),
            pltpu.VMEM((tiles, CAP * PITCH, LANES), jnp.float32),
            pltpu.SMEM((layers * CAP,), jnp.int32),
            pltpu.SMEM((layers,), jnp.int32),
            pltpu.SemaphoreType.DMA((n_select,)),
        ],
        name="encode",
    )(sel_index, sel_layer, counts, me, block_pool, peak)


def body(block_pool, sel_index, sel_layer, counts):
    own_count = lax.axis_size("own")
    rep_count = lax.axis_size("rep")
    layers = own_count // SLICES
    tokens, width = block_pool.shape[1:]
    me = lax.axis_index("own").astype(jnp.int32)
    peak = local_peaks(block_pool, sel_index, sel_layer, counts, layers)
    peak = lax.pmax(peak, ("own", "rep"))
    codes, error, steps = encode(block_pool, sel_index, sel_layer, counts, me[None], peak, layers)
    arrived = lax.all_to_all(codes, "own", split_axis=0, concat_axis=0, tiled=True)
    total = lax.psum(error, ("own", "rep")).reshape(own_count, width // SLICES)
    mine = lax.dynamic_slice_in_dim(total, me, 1, axis=0)
    denominator = float(own_count * rep_count * CAP * tokens)
    return arrived[None, None], steps, mine / (steps * steps * denominator)


def solution(mesh):
    return jax.shard_map(
        body,
        mesh=mesh,
        in_specs=(
            P(("own", "rep"), None, None),
            P(("own", "rep")),
            P(("own", "rep")),
            P(("own", "rep")),
        ),
        out_specs=(P("own", "rep", None, None, None), P("own", None), P("own", None)),
        check_vma=False,
    )
```

time: 264 us -> 314 us (1.19)
  blocking collectives: 123 us -> 268 us
  local copies, waits for them, and re-layouts: 88.9 us -> 8.49 us
  other arithmetic: 40.3 us -> 0.67 us
  Pallas kernels: 0 us -> 18.4 us
  starting transfers between devices: 3.25 us -> 17.4 us
  waiting for transfers between devices: 4.71 us -> 0.01 us
    psum x0 -> x1, blocking collectives: none -> 202 us  [body(): total = lax.psum(error, ('own', 'rep')).reshape(own_count, width // SLICES)]
    all_to_all x2 -> x0, blocking collectives: 123 us -> none  [the longest x1 113 us: body(): lax.all_to_all(parted, 'own', split_axis=0, concat_axis=0, tiled=True)]
    pmax x0 -> x1, blocking collectives: none -> 66.2 us  [body(): peak = lax.pmax(peak, ('own', 'rep'))]
    gather x2 -> x0, local copies, waits for them, and re-layouts: 46 us -> none  [body(): picked = jnp.take(pool_rows, chosen.reshape(-1), axis=0)]
    reshape x4 -> x1, local copies, waits for them, and re-layouts: 31 us -> 0.08 us  [body(): total = lax.psum(error, ('own', 'rep')).reshape(own_count, width // SLICES)]
    pallas_call x0 -> x2, Pallas kernels: none -> 18.4 us  [the longest x1 15.4 us: encode(): pl.pallas_call(functools.partial(encode_kernel, layers), grid=(layers,),...]
    transpose x1 -> x0, other arithmetic: 16.3 us -> none  [body(): picked.transpose(0, 3, 1, 2, 4).reshape(own_count, capacity, flat_width)]
    all_to_all x1, starting transfers between devices: 3.25 us -> 17.4 us  [body(): lax.all_to_all(codes, 'own', split_axis=0, concat_axis=0, tiled=True)]
  transfers between devices with their start and end apart: 1 -> 1, of which waited for: 1 -> 0; matrix products, arithmetic and copies ran while one was open for 0% -> 0% of each run, Pallas kernels for 0% -> 0%
where the time goes in v1:
time: 314 us
  blocking collectives  268 us (85%)
  Pallas kernels  18.4 us (6%)
  starting transfers between devices  17.4 us (6%)
  local copies, waits for them, and re-layouts  8.49 us (3%)
    psum x1, blocking collectives, body(): total = lax.psum(error, ('own', 'rep')).reshape(own_count, width // SLICES)  202 us
    pmax x1, blocking collectives, body(): peak = lax.pmax(peak, ('own', 'rep'))  66.2 us
    all_to_all x1, starting transfers between devices, body(): lax.all_to_all(codes, 'own', split_axis=0, concat_axis=0, tiled=True)  17.4 us
    pallas_call x1, Pallas kernels, encode(): pl.pallas_call(functools.partial(encode_kernel, layers), grid=(layers,),...  15.4 us
    unnamed x5, local copies, waits for them, and re-layouts  8.42 us
  transfers between devices with their start and end apart: 1, of which 0 were waited for; matrix products, arithmetic and copies ran while one was open for 0% of the time, Pallas kernels for 0%

profile of v1, /device:TPU:32, one launch (start us, length us, event | category | flops | bytes accessed | tf_op | source)
XLA Modules:
  0.0 314.2 jit_solution(4008879794146294528)
XLA Ops:
  1.3 2.9 peaks.1
  4.2 66.2 %pmax.7.peak_ref = f32[16,576]{1,0:T(8,128)} all-reduce(f32[16,576]{1,0:T(8,128)} %peaks.1), channel_id=1, replica_groups=mesh['own'=32,'rep'=4] {'own','rep'}, use_global_device_ids=true, to_apply=%region_0.0 | all-reduce | flops 9216 | bytes 73728 | tf_op jit(solution)/shard_map/pmax | solution.py:198
  70.4 15.4 %encode.1 = (bf16[32,8,18432]{2,1,0:T(8,128)(2,1)}, f32[16,1,576]{2,1,0:T(1,128)}, f32[1,288]{1,0:T(1,128)}) custom-call(s32[32]{0:T(128)} %index_ref.3, s32[32]{0:T(128)} %layer_ref.3, s32[1]{0:T(128)S(6)} %copy.8.count_ref, s32[1]{0:T(128)} %bitcast.me_ref, bf16[64,64,576]{2,1,0:T(8,128)(2,1)} %pool_ref.3, f32[16,576]{1,0:T(8,128)} %pmax.7.peak_ref), custom_call_target="tpu_custom_call" | custom-call | tf_op jit(solution)/shard_map/encode/pallas_call | solution.py:166
  85.9 0.0 copy-start
  85.9 0.0 copy-start.1
  85.9 17.4 %all-to-all-start = ((bf16[32,8,18432]{2,1,0:T(8,128)(2,1)}), bf16[32,8,18432]{2,1,0:T(8,128)(2,1)}, u32[]{:S(2)}, u32[]{:S(2)}) async-start(bf16[32,8,18432]{2,1,0:T(8,128)(2,1)} %get-tuple-element.6), calls=%async_computation | async-start | bytes 18874368 | tf_op jit(solution)/shard_map/all_to_all | solution.py:200
  103.2 0.0 copy-done
  103.3 0.1 reduce
  103.4 0.1 reshape.9
  103.4 201.8 %psum.7 = f32[32,288]{1,0:T(8,128)S(1)} all-reduce(f32[32,288]{1,0:T(8,128)S(1)} %reshape.9), channel_id=1, replica_groups=mesh['own'=32,'rep'=4] {'own','rep'}, use_global_device_ids=true, to_apply=%region_1.0 | all-reduce | flops 9216 | bytes 73728 | tf_op jit(solution)/shard_map/psum | solution.py:201
  305.2 0.0 copy-done.1
  305.2 0.6 multiply_divide_fusion
  305.8 0.0 all-to-all-done
  305.8 8.4 %copy.9 = bf16[1,1,32,8,18432]{4,3,2,1,0:T(8,128)(2,1)} copy(bf16[1,1,32,8,18432]{4,3,2,1,0:T(8,128)(2,1)} %bitcast.1) | data formatting | bytes 18874368
Async XLA Ops:
  85.9 17.4 %copy-start = (f32[16,1,576]{2,1,0:T(1,128)S(1)}, f32[16,1,576]{2,1,0:T(1,128)}, u32[]{:S(2)}) copy-start(f32[16,1,576]{2,1,0:T(1,128)} %get-tuple-element.8) | copy-start | bytes 110596
  85.9 219.3 %copy-start.1 = (f32[1,288]{1,0:T(1,128)S(1)}, f32[1,288]{1,0:T(1,128)}, u32[]{:S(2)}) copy-start(f32[1,288]{1,0:T(1,128)} %get-tuple-element.13) | copy-start | bytes 3460
  85.9 219.9 %all-to-all-start = ((bf16[32,8,18432]{2,1,0:T(8,128)(2,1)}), bf16[32,8,18432]{2,1,0:T(8,128)(2,1)}, u32[]{:S(2)}, u32[]{:S(2)}) async-start(bf16[32,8,18432]{2,1,0:T(8,128)(2,1)} %get-tuple-element.6), calls=%async_computation | async-start | bytes 18874368 | tf_op jit(solution)/shard_map/all_to_all | solution.py:200

commit v2 on v0

v2 whole, which is shorter than its diff:
```python
import functools
import jax
import jax.numpy as jnp
from jax import lax
from jax.experimental import pallas as pl
from jax.experimental.pallas import tpu as pltpu
from jax.sharding import PartitionSpec as P

SLICES = 2
CAP = 8
LANES = 128
QUAD = 4
CHUNKS = (4, 8, 4)
headroom = 0.5


def round_up(n, to):
    return -(-n // to) * to


def lay_out_kernel(
    layers, firsts, counts, peaks, index_ref, layer_ref, count_ref, pool_ref, *refs
):
    outs, (held, spread, slots, filled, sems, *acc) = refs[: len(firsts)], refs[len(firsts) :]
    step = pl.program_id(0)
    live = count_ref[0]
    tokens, width = held.shape[1:]
    half = width // SLICES
    tiles = spread.shape[0]
    pitch = spread.shape[1] // CAP
    group = QUAD * half
    first_token, last_token = QUAD * firsts[0], QUAD * (firsts[-1] + counts[-1])
    here = last_token - first_token

    def fetch(j):
        return pltpu.make_async_copy(pool_ref.at[index_ref[j]], held.at[j], sems.at[j])

    @pl.when(step == 0)
    def _():
        def clear(layer, carry):
            filled[layer] = 0
            return carry

        lax.fori_loop(0, layers, clear, 0)

        def start(j, carry):
            fetch(j).start()
            layer = layer_ref[j]
            at = filled[layer]
            slots[layer * CAP + at] = j
            filled[layer] = at + 1
            return carry

        lax.fori_loop(0, live, start, 0)
        if peaks:
            acc[0][...] = jnp.zeros_like(acc[0])

        def wait(j, carry):
            fetch(j).wait()
            if peaks:
                layer = layer_ref[j]
                values = jnp.abs(held[j].astype(jnp.float32)).reshape(tokens // 8, 8, width)
                acc[0][layer] = jnp.maximum(acc[0][layer], jnp.max(values, axis=0))
            return carry

        lax.fori_loop(0, live, wait, 0)

    held_slots = filled[step]

    @pl.when(held_slots == 0)
    def _():
        for out in outs:
            out[...] = jnp.zeros_like(out)

    @pl.when(held_slots > 0)
    def _():
        def place(c, carry):
            values = held[slots[step * CAP + c], first_token:last_token, :].astype(jnp.float32)
            rows = pl.ds(pl.multiple_of(c * pitch, 8), here)
            for j in range(tiles):
                lanes = min(LANES, width - j * LANES)
                spread[j, rows, :lanes] = values[:, j * LANES : j * LANES + lanes]
            return carry

        lax.fori_loop(0, held_slots, place, 0)

        def blank(c, carry):
            for j in range(tiles):
                spread[j, pl.ds(pl.multiple_of(c * pitch, 8), here), :] = jnp.zeros((here, LANES), jnp.float32)
            return carry

        lax.fori_loop(held_slots, CAP, blank, 0)

        lane = lax.broadcasted_iota(jnp.int32, (CAP, LANES), 1)
        if peaks:
            end = counts[0] * group
            outs[0][:, :, end:] = jnp.zeros((SLICES, CAP, outs[0].shape[2] - end), jnp.bfloat16)
            top = jnp.max(acc[0][step], axis=0, keepdims=True)
            for h in range(SLICES):
                one = jnp.broadcast_to(top[:, h * half : (h + 1) * half], (CAP, half))
                outs[0][h, :, end : end + half] = one.astype(jnp.bfloat16)

        for out, first, count in zip(outs, firsts, counts):

            def four_tokens(u, carry, out=out, first=first):
                at_row = QUAD * (u + first) - first_token
                rows = [
                    [spread[j, pl.ds(at_row + q, CAP, stride=pitch), :] for j in range(tiles)]
                    for q in range(QUAD)
                ]
                for h in range(SLICES):
                    turned = {}
                    for i in range(group // LANES):
                        whole, at = None, 0
                        while at < LANES:
                            flat = i * LANES + at
                            q = flat // half
                            source = flat - q * half + h * half
                            j = source // LANES
                            run = min(LANES - source % LANES, (q + 1) * half - flat, LANES - at)
                            if (q, j) not in turned:
                                shift = (at - source) % LANES
                                turned[q, j] = pltpu.roll(rows[q][j], shift, 1) if shift else rows[q][j]
                            piece = turned[q, j]
                            whole = piece if whole is None else jnp.where(lane >= at, piece, whole)
                            at += run
                        where = pl.ds(pl.multiple_of(u * group + i * LANES, LANES), LANES)
                        out[h, :, where] = whole.astype(jnp.bfloat16)
                return carry

            lax.fori_loop(0, count, four_tokens, 0)


def lay_out(block_pool, sel_index, sel_layer, counts, layers, firsts, groups, peaks, after=()):
    n_select = sel_index.shape[0]
    tokens, width = block_pool.shape[1:]
    half = width // SLICES
    tiles = pl.cdiv(width, LANES)
    here = QUAD * sum(groups)
    pitch = here + 8
    smem = pl.BlockSpec(memory_space=pltpu.SMEM)
    sizes = [QUAD * half * n for n in groups]
    if peaks:
        sizes[0] += round_up(half, LANES)
    scratch = [
        pltpu.VMEM((n_select, tokens, width), jnp.bfloat16),
        pltpu.VMEM((tiles, CAP * pitch, LANES), jnp.float32),
        pltpu.SMEM((layers * CAP,), jnp.int32),
        pltpu.SMEM((layers,), jnp.int32),
        pltpu.SemaphoreType.DMA((n_select,)),
    ]
    if peaks:
        scratch.append(pltpu.VMEM((layers, 8, width), jnp.float32))
    return pl.pallas_call(
        functools.partial(lay_out_kernel, layers, firsts, groups, peaks),
        grid=(layers,),
        out_shape=[jax.ShapeDtypeStruct((layers * SLICES, CAP, n), jnp.bfloat16) for n in sizes],
        in_specs=[smem, smem, smem, pl.BlockSpec(memory_space=pl.ANY)],
        out_specs=[pl.BlockSpec((SLICES, CAP, n), lambda l: (l, 0, 0)) for n in sizes],
        scratch_shapes=scratch,
        cost_estimate=pl.CostEstimate(flops=100_000_000, bytes_accessed=20_000_000, transcendentals=0),
        name="lay_out",
    )(sel_index, sel_layer, counts, block_pool)


def encode_kernel(step_ref, inverse_ref, error_in, raw_ref, *refs):
    codes_ref, error_ref = refs[-2:]

    @pl.when(pl.program_id(0) == 0)
    def _():
        error_ref[...] = error_in[...]

    sources, cap, lanes = raw_ref.shape
    tiles = lanes // LANES
    step = [jnp.broadcast_to(step_ref[:, i * LANES : (i + 1) * LANES], (cap, LANES)) for i in range(tiles)]
    inverse = [jnp.broadcast_to(inverse_ref[:, i * LANES : (i + 1) * LANES], (cap, LANES)) for i in range(tiles)]

    def source(s, totals):
        out = []
        for i in range(tiles):
            at = slice(i * LANES, (i + 1) * LANES)
            values = raw_ref[s, :, at].astype(jnp.float32)
            coded = jnp.clip(values * inverse[i], -127.0, 127.0).astype(jnp.bfloat16)
            codes_ref[s, :, at] = coded
            miss = values - coded.astype(jnp.float32) * step[i]
            out.append(totals[i] + miss * miss)
        return tuple(out)

    zeros = tuple(jnp.zeros((cap, LANES), jnp.float32) for _ in range(tiles))
    totals = lax.fori_loop(0, sources, source, zeros)
    for i in range(tiles):
        error_ref[:, i * LANES : (i + 1) * LANES] += totals[i]


def encode(raw, step_row, inverse_row, error, codes, first, groups, all_groups):
    sources, cap, _ = raw.shape
    lanes = step_row.shape[1]
    row = pl.BlockSpec((1, lanes), lambda u: (0, 0))
    total = pl.BlockSpec((cap, lanes), lambda u: (0, 0))
    specs = [row, row, total, pl.BlockSpec((sources, cap, lanes), lambda u: (0, 0, u))]
    args = [step_row, inverse_row, error, raw]
    aliases = {}
    if codes is not None:
        specs.append(pl.BlockSpec(memory_space=pl.ANY))
        args.append(codes)
        aliases = {4: 0}
    return pl.pallas_call(
        encode_kernel,
        grid=(groups,),
        out_shape=(
            jax.ShapeDtypeStruct((sources, cap, lanes * all_groups), jnp.bfloat16),
            jax.ShapeDtypeStruct((cap, lanes), jnp.float32),
        ),
        in_specs=specs,
        out_specs=(pl.BlockSpec((sources, cap, lanes), lambda u: (0, 0, first + u)), total),
        input_output_aliases=aliases,
        cost_estimate=pl.CostEstimate(flops=20_000_000 * groups, bytes_accessed=1_200_000 * groups, transcendentals=0),
        name="encode",
    )(*args)


def over_rep(x, op):
    x = op(x, lax.ppermute(x, "rep", [(0, 1), (1, 0), (2, 3), (3, 2)]))
    return op(x, lax.ppermute(x, "rep", [(0, 3), (3, 0), (1, 2), (2, 1)]))


def body(block_pool, sel_index, sel_layer, counts):
    own_count = lax.axis_size("own")
    rep_count = lax.axis_size("rep")
    layers = own_count // SLICES
    tokens, width = block_pool.shape[1:]
    half = width // SLICES
    firsts = [sum(CHUNKS[:n]) for n in range(len(CHUNKS))]

    def exchange(x):
        return lax.all_to_all(x, "own", split_axis=0, concat_axis=0, tiled=True)

    sent = lay_out(block_pool, sel_index, sel_layer, counts, layers, firsts[:1], CHUNKS[:1], True)
    sent += lay_out(block_pool, sel_index, sel_layer, counts, layers, firsts[1:], CHUNKS[1:], False)
    arrived = [exchange(x) for x in sent]

    at = QUAD * half * CHUNKS[0]
    peak = jnp.max(arrived[0][:, :1, at : at + half], axis=0).astype(jnp.float32)
    peak = over_rep(peak, jnp.maximum)
    steps = headroom * jnp.maximum(peak, 1.0) / 127.0
    step_row = jnp.tile(steps, (1, QUAD))
    inverse_row = 1.0 / step_row
    error = jnp.zeros((CAP, QUAD * half), jnp.float32)
    codes = None
    for n, raw in enumerate(arrived):
        codes, error = encode(
            raw, step_row, inverse_row, error, codes, firsts[n], CHUNKS[n], tokens // QUAD
        )
    error = jnp.sum(jnp.sum(error, axis=0).reshape(QUAD, half), axis=0, keepdims=True)
    error = over_rep(error, jnp.add)
    denominator = float(own_count * rep_count * CAP * tokens)
    return codes[None, None], steps, error / (steps * steps * denominator)


def solution(mesh):
    return jax.shard_map(
        body,
        mesh=mesh,
        in_specs=(
            P(("own", "rep"), None, None),
            P(("own", "rep")),
            P(("own", "rep")),
            P(("own", "rep")),
        ),
        out_specs=(P("own", "rep", None, None, None), P("own", None), P("own", None)),
        check_vma=False,
    )
```

time: 264 us -> 169 us (0.64)
  local copies, waits for them, and re-layouts: 88.9 us -> 0.81 us
  blocking collectives: 123 us -> 61.5 us
  other arithmetic: 40.3 us -> 2.08 us
  Pallas kernels: 0 us -> 38.1 us
  waiting for transfers between devices: 4.71 us -> 38.5 us
  starting transfers between devices: 3.25 us -> 24.1 us
    all_to_all x2 -> x1, blocking collectives: 123 us -> 61.5 us  [exchange(): return lax.all_to_all(x, 'own', split_axis=0, concat_axis=0, tiled=True)]
    gather x2 -> x0, local copies, waits for them, and re-layouts: 46 us -> none  [body(): picked = jnp.take(pool_rows, chosen.reshape(-1), axis=0)]
    pallas_call x0 -> x5, Pallas kernels: none -> 38.1 us  [the longest x3 19.7 us: encode(): pl.pallas_call(encode_kernel, grid=(groups,), out_shape=(jax.ShapeDtypeSt...]
    reshape x4 -> x1, local copies, waits for them, and re-layouts: 31 us -> 0.08 us  [body(): jnp.sum(error, axis=0).reshape(QUAD, half)]
    all_to_all x1 -> x2, waiting for transfers between devices: 4.71 us -> 28 us  [exchange(): return lax.all_to_all(x, 'own', split_axis=0, concat_axis=0, tiled=True)]
    transpose x1 -> x0, other arithmetic: 16.3 us -> none  [body(): picked.transpose(0, 3, 1, 2, 4).reshape(own_count, capacity, flat_width)]
    all_to_all x1 -> x2, starting transfers between devices: 3.25 us -> 17.7 us  [exchange(): return lax.all_to_all(x, 'own', split_axis=0, concat_axis=0, tiled=True)]
    ppermute x0 -> x4, waiting for transfers between devices: none -> 10.4 us  [the longest x2 6.36 us: over_rep(): return op(x, lax.ppermute(x, 'rep', [(0, 3), (3, 0), (1, 2), (2, 1)]))]
  transfers between devices with their start and end apart: 1 -> 6, of which waited for: 1 -> 6; matrix products, arithmetic and copies ran while one was open for 0% -> 1% of each run, Pallas kernels for 0% -> 15%
where the time goes in v2:
time: 169 us; the launch traced here: 166 us
  blocking collectives  61.5 us (36%)
  waiting for transfers between devices  38.5 us (23%)
  Pallas kernels  38.1 us (23%)
  starting transfers between devices  24.1 us (14%)
  other arithmetic  2.08 us (1%)
    all_to_all x1, blocking collectives, exchange(): return lax.all_to_all(x, 'own', split_axis=0, concat_axis=0, tiled=True)  61.5 us
    all_to_all x2, waiting for transfers between devices, exchange(): return lax.all_to_all(x, 'own', split_axis=0, concat_axis=0, tiled=True)  28 us
    pallas_call x3, Pallas kernels, encode(): pl.pallas_call(encode_kernel, grid=(groups,), out_shape=(jax.ShapeDtypeSt...  19.7 us
    pallas_call x2, Pallas kernels, lay_out(): pl.pallas_call(functools.partial(lay_out_kernel, layers, firsts, groups,...  18.4 us
    all_to_all x2, starting transfers between devices, exchange(): return lax.all_to_all(x, 'own', split_axis=0, concat_axis=0, tiled=True)  17.7 us
    ppermute x2, waiting for transfers between devices, over_rep(): return op(x, lax.ppermute(x, 'rep', [(0, 3), (3, 0), (1, 2), (2, 1)]))  6.36 us
    ppermute x2, waiting for transfers between devices, over_rep(): x = op(x, lax.ppermute(x, 'rep', [(0, 1), (1, 0), (2, 3), (3, 2)]))  4.08 us
  transfers between devices with their start and end apart: 6, of which 6 were waited for; matrix products, arithmetic and copies ran while one was open for 1% of the time, Pallas kernels for 15%

profile of v2, /device:TPU:32, one launch (start us, length us, event | category | flops | bytes accessed | tf_op | source)
XLA Modules:
  0.0 166.4 jit_solution(6096436268546437433)
XLA Ops:
  1.3 8.4 %lay_out.2 = bf16[32,8,4992]{2,1,0:T(8,128)(2,1)} custom-call(s32[32]{0:T(128)} %index_ref.3, s32[32]{0:T(128)} %layer_ref.3, s32[1]{0:T(128)S(6)} %copy.11.count_ref, bf16[64,64,576]{2,1,0:T(8,128)(2,1)} %pool_ref.3), custom_call_target="tpu_custom_call" | custom-call | flops 100000000 | bytes 20000000 | tf_op jit(solution)/shard_map/lay_out/pallas_call | solution.py:154
  9.7 12.0 %all-to-all-start = ((bf16[32,8,4992]{2,1,0:T(8,128)(2,1)}), bf16[32,8,4992]{2,1,0:T(8,128)(2,1)S(1)}, u32[]{:S(2)}, u32[]{:S(2)}) async-start(bf16[32,8,4992]{2,1,0:T(8,128)(2,1)} %lay_out.2), calls=%async_computation | async-start | bytes 5111808 | tf_op jit(solution)/shard_map/all_to_all | solution.py:236
  21.7 10.0 %lay_out.3 = (bf16[32,8,9216]{2,1,0:T(8,128)(2,1)}, bf16[32,8,4608]{2,1,0:T(8,128)(2,1)}) custom-call(s32[32]{0:T(128)} %index_ref.3, s32[32]{0:T(128)} %layer_ref.3, s32[1]{0:T(128)S(6)} %copy.11.count_ref, bf16[64,64,576]{2,1,0:T(8,128)(2,1)} %pool_ref.3), custom_call_target="tpu_custom_call" | custom-call | flops 100000000 | bytes 20000000 | tf_op jit(solution)/shard_map/lay_out/pallas_call | solution.py:154
  31.7 22.3 %all-to-all-done.raw_ref = bf16[32,8,4992]{2,1,0:T(8,128)(2,1)S(1)} async-done(((bf16[32,8,4992]{2,1,0:T(8,128)(2,1)}), bf16[32,8,4992]{2,1,0:T(8,128)(2,1)S(1)}, u32[]{:S(2)}, u32[]{:S(2)}) %all-to-all-start) | async-done | bytes 2555936 | tf_op jit(solution)/shard_map/all_to_all | solution.py:236
  53.9 0.0 copy-start
  53.9 61.5 %all_to_all.15.raw_ref = bf16[32,8,9216]{2,1,0:T(8,128)(2,1)} all-to-all(bf16[32,8,9216]{2,1,0:T(8,128)(2,1)} %get-tuple-element.12), channel_id=1, replica_groups=mesh['own'=32,'rep'=4] {'own'}, dimensions={0} | all-to-all | bytes 9437184 | tf_op jit(solution)/shard_map/all_to_all | solution.py:236
  115.4 5.7 %all-to-all-start.2 = ((bf16[32,8,4608]{2,1,0:T(8,128)(2,1)}), bf16[32,8,4608]{2,1,0:T(8,128)(2,1)}, u32[]{:S(2)}, u32[]{:S(2)}) async-start(bf16[32,8,4608]{2,1,0:T(8,128)(2,1)} %get-tuple-element.15), calls=%async_computation.2 | async-start | bytes 4718592 | tf_op jit(solution)/shard_map/all_to_all | solution.py:236
  121.1 0.0 copy-done
  121.1 0.1 slice_reduce_fusion
  121.2 1.6 collective-permute-start
  122.8 2.0 %collective-permute-done = f32[1,288]{1,0:T(1,128)S(1)} collective-permute-done((f32[1,288]{1,0:T(1,128)S(1)}, f32[1,288]{1,0:T(1,128)S(1)}, u32[]{:S(2)}, u32[]{:S(2)}) %collective-permute-start) | collective-permute-done | bytes 1184 | tf_op jit(solution)/shard_map/ppermute | solution.py:223
  124.9 1.6 collective-permute-start.1
  126.5 3.2 %collective-permute-done.1 = f32[1,288]{1,0:T(1,128)S(1)} collective-permute-done((f32[1,288]{1,0:T(1,128)S(1)}, f32[1,288]{1,0:T(1,128)S(1)}, u32[]{:S(2)}, u32[]{:S(2)}) %collective-permute-start.1) | collective-permute-done | bytes 1184 | tf_op jit(solution)/shard_map/ppermute | solution.py:224
  129.7 0.0 copy-start.2
  129.7 0.1 tile.13.step_ref
  129.8 0.0 copy-start.1
  129.8 0.6 broadcast_divide_fusion.inverse_ref
  130.4 0.6 broadcast_in_dim.9.error_in
  131.0 0.0 copy-done.1
  131.0 5.2 %encode.3 = (bf16[32,8,18432]{2,1,0:T(8,128)(2,1)}, f32[8,1152]{1,0:T(8,128)}) custom-call(f32[1,1152]{1,0:T(1,128)} %copy-done.1, f32[1,1152]{1,0:T(1,128)} %broadcast_divide_fusion.inverse_ref, f32[8,1152]{1,0:T(8,128)} %broadcast_in_dim.9.error_in, bf16[32,8,4992]{2,1,0:T(8,128)(2,1)} %copy-done), custom_call_target="tpu_custom_call" | custom-call | flops 80000000 | bytes 4800000 | tf_op jit(solution)/shard_map/encode/pallas_call | solution.py:207
  136.3 9.2 %encode.4 = (bf16[32,8,18432]{2,1,0:T(8,128)(2,1)}, f32[8,1152]{1,0:T(8,128)}) custom-call(f32[1,1152]{1,0:T(1,128)} %copy-done.1, f32[1,1152]{1,0:T(1,128)} %broadcast_divide_fusion.inverse_ref, f32[8,1152]{1,0:T(8,128)} %get-tuple-element.11.error_in, bf16[32,8,9216]{2,1,0:T(8,128)(2,1)} %all_to_all.15.raw_ref, ...), custom_call_target="tpu_custom_call", output_to_operand_aliasing={{0}: (4, {})} | custom-call | flops 160000000 | bytes 9600000 | tf_op jit(solution)/shard_map/encode/pallas_call | solution.py:207
  145.5 5.8 %all-to-all-done.2.raw_ref = bf16[32,8,4608]{2,1,0:T(8,128)(2,1)} async-done(((bf16[32,8,4608]{2,1,0:T(8,128)(2,1)}), bf16[32,8,4608]{2,1,0:T(8,128)(2,1)}, u32[]{:S(2)}, u32[]{:S(2)}) %all-to-all-start.2) | async-done | bytes 2359328 | tf_op jit(solution)/shard_map/all_to_all | solution.py:236
  151.3 5.2 %encode.5 = (bf16[32,8,18432]{2,1,0:T(8,128)(2,1)}, f32[8,1152]{1,0:T(8,128)}) custom-call(f32[1,1152]{1,0:T(1,128)} %copy-done.1, f32[1,1152]{1,0:T(1,128)} %broadcast_divide_fusion.inverse_ref, f32[8,1152]{1,0:T(8,128)} %get-tuple-element.14.error_in, bf16[32,8,4608]{2,1,0:T(8,128)(2,1)} %all-to-all-done.2.raw_ref, ...), custom_call_target="tpu_custom_call", output_to_operand_aliasing={{0}: (4, {})} | custom-call | flops 80000000 | bytes 4800000 | tf_op jit(solution)/shard_map/encode/pallas_call | solution.py:207
  156.5 0.8 reduce_sum.18
  157.3 0.1 reshape.41
  157.4 1.6 collective-permute-start.2
  159.0 2.0 %collective-permute-done.2 = f32[1,288]{1,0:T(1,128)S(1)} collective-permute-done((f32[1,288]{1,0:T(1,128)S(1)}, f32[1,288]{1,0:T(1,128)S(1)}, u32[]{:S(2)}, u32[]{:S(2)}) %collective-permute-start.2) | collective-permute-done | bytes 1184 | tf_op jit(solution)/shard_map/ppermute | solution.py:223
  161.1 1.6 collective-permute-start.3
  162.7 3.2 %collective-permute-done.3 = f32[1,288]{1,0:T(1,128)S(1)} collective-permute-done((f32[1,288]{1,0:T(1,128)S(1)}, f32[1,288]{1,0:T(1,128)S(1)}, u32[]{:S(2)}, u32[]{:S(2)}) %collective-permute-start.3) | collective-permute-done | bytes 1184 | tf_op jit(solution)/shard_map/ppermute | solution.py:224
  165.8 0.0 copy-done.2
  165.8 0.6 multiply_divide_fusion
  (7 shorter events, 0.1 us)
Async XLA Ops:
  9.7 44.2 %all-to-all-start = ((bf16[32,8,4992]{2,1,0:T(8,128)(2,1)}), bf16[32,8,4992]{2,1,0:T(8,128)(2,1)S(1)}, u32[]{:S(2)}, u32[]{:S(2)}) async-start(bf16[32,8,4992]{2,1,0:T(8,128)(2,1)} %lay_out.2), calls=%async_computation | async-start | bytes 5111808 | tf_op jit(solution)/shard_map/all_to_all | solution.py:236
  53.9 67.2 %copy-start = (bf16[32,8,4992]{2,1,0:T(8,128)(2,1)}, bf16[32,8,4992]{2,1,0:T(8,128)(2,1)S(1)}, u32[]{:S(2)}) copy-start(bf16[32,8,4992]{2,1,0:T(8,128)(2,1)S(1)} %all-to-all-done.raw_ref) | copy-start | bytes 7667716
  115.4 35.8 %all-to-all-start.2 = ((bf16[32,8,4608]{2,1,0:T(8,128)(2,1)}), bf16[32,8,4608]{2,1,0:T(8,128)(2,1)}, u32[]{:S(2)}, u32[]{:S(2)}) async-start(bf16[32,8,4608]{2,1,0:T(8,128)(2,1)} %get-tuple-element.15), calls=%async_computation.2 | async-start | bytes 4718592 | tf_op jit(solution)/shard_map/all_to_all | solution.py:236
  121.2 3.7 %collective-permute-start = (f32[1,288]{1,0:T(1,128)S(1)}, f32[1,288]{1,0:T(1,128)S(1)}, u32[]{:S(2)}, u32[]{:S(2)}) collective-permute-start(f32[1,288]{1,0:T(1,128)S(1)} %reshape.42), channel_id=1, source_target_pairs={{0,1},{1,0},{2,3},{3,2},{4,5},{5,4},{6,7},{7,6},{8,9},{9,8},{10,11... | collective-permute-start | bytes 3464 | tf_op jit(solution)/shard_map/ppermute | solution.py:223
  124.9 4.8 %collective-permute-start.1 = (f32[1,288]{1,0:T(1,128)S(1)}, f32[1,288]{1,0:T(1,128)S(1)}, u32[]{:S(2)}, u32[]{:S(2)}) collective-permute-start(f32[1,288]{1,0:T(1,128)S(1)} %reshape_maximum_fusion), channel_id=1, source_target_pairs={{0,3},{3,0},{1,2},{2,1},{4,7},{7,4},{5,6},{6,5},{8,11},{11,8},{9,1... | collective-permute-start | bytes 3464 | tf_op jit(solution)/shard_map/ppermute | solution.py:224
  129.7 36.2 %copy-start.2 = (f32[1,288]{1,0:T(1,128)}, f32[1,288]{1,0:T(1,128)S(1)}, u32[]{:S(2)}) copy-start(f32[1,288]{1,0:T(1,128)S(1)} %get-tuple-element.20) | copy-start | bytes 3460
  129.8 1.2 copy-start.1
  157.4 3.7 %collective-permute-start.2 = (f32[1,288]{1,0:T(1,128)S(1)}, f32[1,288]{1,0:T(1,128)S(1)}, u32[]{:S(2)}, u32[]{:S(2)}) collective-permute-start(f32[1,288]{1,0:T(1,128)S(1)} %broadcast_in_dim.11), channel_id=1, source_target_pairs={{0,1},{1,0},{2,3},{3,2},{4,5},{5,4},{6,7},{7,6},{8,9},{9,8},{10,11... | collective-permute-start | bytes 3464 | tf_op jit(solution)/shard_map/ppermute | solution.py:223
  161.1 4.8 %collective-permute-start.3 = (f32[1,288]{1,0:T(1,128)S(1)}, f32[1,288]{1,0:T(1,128)S(1)}, u32[]{:S(2)}, u32[]{:S(2)}) collective-permute-start(f32[1,288]{1,0:T(1,128)S(1)} %reshape_add_fusion), channel_id=1, source_target_pairs={{0,3},{3,0},{1,2},{2,1},{4,7},{7,4},{5,6},{6,5},{8,11},{11,8},{9,1... | collective-permute-start | bytes 3464 | tf_op jit(solution)/shard_map/ppermute | solution.py:224

commit v3 on v2

--- a/solution.py
+++ b/solution.py
@@ -10,7 +10,7 @@
 CAP = 8
 LANES = 128
 QUAD = 4
-CHUNKS = (4, 8, 4)
+CHUNKS = (4, 12)
 headroom = 0.5
 
 
@@ -21,7 +21,7 @@
 def lay_out_kernel(
     layers, firsts, counts, peaks, index_ref, layer_ref, count_ref, pool_ref, *refs
 ):
-    outs, (held, spread, slots, filled, sems, *acc) = refs[: len(firsts)], refs[len(firsts) :]
+    outs, (held, spread, slots, filled, dirty, sems, *tops) = refs[: len(firsts)], refs[len(firsts) :]
     step = pl.program_id(0)
     live = count_ref[0]
     tokens, width = held.shape[1:]
@@ -31,6 +31,7 @@
     group = QUAD * half
     first_token, last_token = QUAD * firsts[0], QUAD * (firsts[-1] + counts[-1])
     here = last_token - first_token
+    pieces = pl.cdiv(half, LANES)
 
     def fetch(j):
         return pltpu.make_async_copy(pool_ref.at[index_ref[j]], held.at[j], sems.at[j])
@@ -42,6 +43,7 @@
             return carry
 
         lax.fori_loop(0, layers, clear, 0)
+        dirty[0] = CAP
 
         def start(j, carry):
             fetch(j).start()
@@ -53,17 +55,26 @@
 
         lax.fori_loop(0, live, start, 0)
         if peaks:
-            acc[0][...] = jnp.zeros_like(acc[0])
+            acc, top = tops
+            acc[...] = jnp.zeros_like(acc)
+            top[...] = jnp.zeros_like(top)
 
         def wait(j, carry):
             fetch(j).wait()
             if peaks:
                 layer = layer_ref[j]
                 values = jnp.abs(held[j].astype(jnp.float32)).reshape(tokens // 8, 8, width)
-                acc[0][layer] = jnp.maximum(acc[0][layer], jnp.max(values, axis=0))
+                acc[layer] = jnp.maximum(acc[layer], jnp.max(values, axis=0))
             return carry
 
         lax.fori_loop(0, live, wait, 0)
+        if peaks:
+            whole = jnp.max(acc[...], axis=1)
+            for h in range(SLICES):
+                for n in range(pieces):
+                    lanes = min(LANES, half - n * LANES)
+                    at = h * half + n * LANES
+                    top[h * pieces + n, :, :lanes] = whole[:, at : at + lanes]
 
     held_slots = filled[step]
 
@@ -89,16 +100,19 @@
                 spread[j, pl.ds(pl.multiple_of(c * pitch, 8), here), :] = jnp.zeros((here, LANES), jnp.float32)
             return carry
 
-        lax.fori_loop(held_slots, CAP, blank, 0)
+        lax.fori_loop(held_slots, dirty[0], blank, 0)
+        dirty[0] = held_slots
 
         lane = lax.broadcasted_iota(jnp.int32, (CAP, LANES), 1)
         if peaks:
-            end = counts[0] * group
-            outs[0][:, :, end:] = jnp.zeros((SLICES, CAP, outs[0].shape[2] - end), jnp.bfloat16)
-            top = jnp.max(acc[0][step], axis=0, keepdims=True)
+            top = tops[1]
+            row = lax.broadcasted_iota(jnp.int32, (CAP, LANES), 0)
             for h in range(SLICES):
-                one = jnp.broadcast_to(top[:, h * half : (h + 1) * half], (CAP, half))
-                outs[0][h, :, end : end + half] = one.astype(jnp.bfloat16)
+                tile = jnp.zeros((CAP, LANES), jnp.float32)
+                for n in range(pieces):
+                    one = jnp.broadcast_to(top[h * pieces + n, pl.ds(step, 1), :], (CAP, LANES))
+                    tile = jnp.where(row == n, one, tile)
+                outs[0][h, :, counts[0] * group :] = tile.astype(jnp.bfloat16)
 
         for out, first, count in zip(outs, firsts, counts):
 
@@ -128,10 +142,10 @@
                         out[h, :, where] = whole.astype(jnp.bfloat16)
                 return carry
 
-            lax.fori_loop(0, count, four_tokens, 0)
-
-
-def lay_out(block_pool, sel_index, sel_layer, counts, layers, firsts, groups, peaks, after=()):
+            lax.fori_loop(0, count, four_tokens, 0, unroll=4)
+
+
+def lay_out(block_pool, sel_index, sel_layer, counts, layers, firsts, groups, peaks):
     n_select = sel_index.shape[0]
     tokens, width = block_pool.shape[1:]
     half = width // SLICES
@@ -140,17 +154,18 @@
     pitch = here + 8
     smem = pl.BlockSpec(memory_space=pltpu.SMEM)
     sizes = [QUAD * half * n for n in groups]
-    if peaks:
-        sizes[0] += round_up(half, LANES)
     scratch = [
         pltpu.VMEM((n_select, tokens, width), jnp.bfloat16),
         pltpu.VMEM((tiles, CAP * pitch, LANES), jnp.float32),
         pltpu.SMEM((layers * CAP,), jnp.int32),
         pltpu.SMEM((layers,), jnp.int32),
+        pltpu.SMEM((1,), jnp.int32),
         pltpu.SemaphoreType.DMA((n_select,)),
     ]
     if peaks:
+        sizes[0] += LANES
         scratch.append(pltpu.VMEM((layers, 8, width), jnp.float32))
+        scratch.append(pltpu.VMEM((SLICES * pl.cdiv(half, LANES), layers, LANES), jnp.float32))
     return pl.pallas_call(
         functools.partial(lay_out_kernel, layers, firsts, groups, peaks),
         grid=(layers,),
@@ -163,59 +178,67 @@
     )(sel_index, sel_layer, counts, block_pool)
 
 
-def encode_kernel(step_ref, inverse_ref, error_in, raw_ref, *refs):
-    codes_ref, error_ref = refs[-2:]
-
-    @pl.when(pl.program_id(0) == 0)
-    def _():
-        error_ref[...] = error_in[...]
-
+def code_kernel(coding, measuring, inverse_ref, raw_ref, *refs):
     sources, cap, lanes = raw_ref.shape
     tiles = lanes // LANES
-    step = [jnp.broadcast_to(step_ref[:, i * LANES : (i + 1) * LANES], (cap, LANES)) for i in range(tiles)]
+    codes_ref = refs[-1 - measuring] if coding else None
+    total_ref = refs[-1] if measuring else None
     inverse = [jnp.broadcast_to(inverse_ref[:, i * LANES : (i + 1) * LANES], (cap, LANES)) for i in range(tiles)]
 
     def source(s, totals):
         out = []
         for i in range(tiles):
             at = slice(i * LANES, (i + 1) * LANES)
-            values = raw_ref[s, :, at].astype(jnp.float32)
-            coded = jnp.clip(values * inverse[i], -127.0, 127.0).astype(jnp.bfloat16)
-            codes_ref[s, :, at] = coded
-            miss = values - coded.astype(jnp.float32) * step[i]
-            out.append(totals[i] + miss * miss)
+            exact = raw_ref[s, :, at].astype(jnp.float32) * inverse[i]
+            coded = jnp.clip(exact, -127.0, 127.0).astype(jnp.bfloat16)
+            if coding:
+                codes_ref[s, :, at] = coded
+            if measuring:
+                miss = exact - coded.astype(jnp.float32)
+                out.append(totals[i] + miss * miss)
         return tuple(out)
 
-    zeros = tuple(jnp.zeros((cap, LANES), jnp.float32) for _ in range(tiles))
-    totals = lax.fori_loop(0, sources, source, zeros)
-    for i in range(tiles):
-        error_ref[:, i * LANES : (i + 1) * LANES] += totals[i]
-
-
-def encode(raw, step_row, inverse_row, error, codes, first, groups, all_groups):
+    zeros = tuple(jnp.zeros((cap, LANES), jnp.float32) for _ in range(tiles)) if measuring else ()
+    totals = lax.fori_loop(0, sources, source, zeros, unroll=2)
+    if measuring:
+
+        @pl.when(pl.program_id(0) == 0)
+        def _():
+            total_ref[...] = jnp.zeros_like(total_ref)
+
+        for i in range(tiles):
+            total_ref[:, i * LANES : (i + 1) * LANES] += totals[i]
+
+
+def code(raw, inverse, codes, start, first, groups, all_groups, coding, measuring):
     sources, cap, _ = raw.shape
-    lanes = step_row.shape[1]
-    row = pl.BlockSpec((1, lanes), lambda u: (0, 0))
-    total = pl.BlockSpec((cap, lanes), lambda u: (0, 0))
-    specs = [row, row, total, pl.BlockSpec((sources, cap, lanes), lambda u: (0, 0, u))]
-    args = [step_row, inverse_row, error, raw]
+    lanes = inverse.shape[1]
+    specs = [
+        pl.BlockSpec((1, lanes), lambda u: (0, 0)),
+        pl.BlockSpec((sources, cap, lanes), lambda u: (0, 0, start + u)),
+    ]
+    args = [inverse, raw]
     aliases = {}
-    if codes is not None:
-        specs.append(pl.BlockSpec(memory_space=pl.ANY))
-        args.append(codes)
-        aliases = {4: 0}
+    shapes, out_specs = [], []
+    if coding:
+        if codes is not None:
+            specs.append(pl.BlockSpec(memory_space=pl.ANY))
+            args.append(codes)
+            aliases = {2: 0}
+        shapes.append(jax.ShapeDtypeStruct((sources, cap, lanes * all_groups), jnp.bfloat16))
+        out_specs.append(pl.BlockSpec((sources, cap, lanes), lambda u: (0, 0, first + u)))
+    if measuring:
+        shapes.append(jax.ShapeDtypeStruct((cap, lanes), jnp.float32))
+        out_specs.append(pl.BlockSpec((cap, lanes), lambda u: (0, 0)))
     return pl.pallas_call(
-        encode_kernel,
+        functools.partial(code_kernel, coding, measuring),
         grid=(groups,),
-        out_shape=(
-            jax.ShapeDtypeStruct((sources, cap, lanes * all_groups), jnp.bfloat16),
-            jax.ShapeDtypeStruct((cap, lanes), jnp.float32),
-        ),
+        out_shape=shapes,
         in_specs=specs,
-        out_specs=(pl.BlockSpec((sources, cap, lanes), lambda u: (0, 0, first + u)), total),
+        out_specs=out_specs,
         input_output_aliases=aliases,
         cost_estimate=pl.CostEstimate(flops=20_000_000 * groups, bytes_accessed=1_200_000 * groups, transcendentals=0),
-        name="encode",
+        name="code" if coding else "measure",
     )(*args)
 
 
@@ -237,24 +260,22 @@
 
     sent = lay_out(block_pool, sel_index, sel_layer, counts, layers, firsts[:1], CHUNKS[:1], True)
     sent += lay_out(block_pool, sel_index, sel_layer, counts, layers, firsts[1:], CHUNKS[1:], False)
-    arrived = [exchange(x) for x in sent]
-
-    at = QUAD * half * CHUNKS[0]
-    peak = jnp.max(arrived[0][:, :1, at : at + half], axis=0).astype(jnp.float32)
-    peak = over_rep(peak, jnp.maximum)
+    early, late = [exchange(x) for x in sent]
+
+    peak = jnp.max(early[:, :, QUAD * half * CHUNKS[0] :], axis=0).astype(jnp.float32)
+    peak = over_rep(peak, jnp.maximum).reshape(1, CAP * LANES)[:, :half]
     steps = headroom * jnp.maximum(peak, 1.0) / 127.0
-    step_row = jnp.tile(steps, (1, QUAD))
-    inverse_row = 1.0 / step_row
-    error = jnp.zeros((CAP, QUAD * half), jnp.float32)
-    codes = None
-    for n, raw in enumerate(arrived):
-        codes, error = encode(
-            raw, step_row, inverse_row, error, codes, firsts[n], CHUNKS[n], tokens // QUAD
-        )
-    error = jnp.sum(jnp.sum(error, axis=0).reshape(QUAD, half), axis=0, keepdims=True)
+    inverse = jnp.tile(1.0 / steps, (1, QUAD))
+    every = tokens // QUAD
+    codes, error = code(early, inverse, None, 0, 0, CHUNKS[0], every, True, True)
+    (more,) = code(late, inverse, None, 0, 0, CHUNKS[1], every, False, True)
+    error = jnp.sum(error + more, axis=0).reshape(QUAD, half).sum(axis=0, keepdims=True)
+    split = CHUNKS[1] // 2
+    (codes,) = code(late, inverse, codes, 0, CHUNKS[0], split, every, True, False)
+    (codes,) = code(late, inverse, codes, split, CHUNKS[0] + split, CHUNKS[1] - split, every, True, False)
     error = over_rep(error, jnp.add)
     denominator = float(own_count * rep_count * CAP * tokens)
-    return codes[None, None], steps, error / (steps * steps * denominator)
+    return codes[None, None], steps, error / denominator
 
 
 def solution(mesh):

time: 169 us -> 187 us (1.11)
  waiting for transfers between devices: 38.5 us -> 113 us
  blocking collectives: 61.5 us -> 0 us
  Pallas kernels: 38.1 us -> 44.6 us
    all_to_all x2, waiting for transfers between devices: 28 us -> 109 us  [exchange(): return lax.all_to_all(x, 'own', split_axis=0, concat_axis=0, tiled=True)]
    all_to_all x1 -> x0, blocking collectives: 61.5 us -> none  [exchange(): return lax.all_to_all(x, 'own', split_axis=0, concat_axis=0, tiled=True)]
    pallas_call x3 -> x4, Pallas kernels: 19.7 us -> 26.9 us  [code(): pl.pallas_call(functools.partial(code_kernel, coding, measuring), grid=(g...]
    ppermute x2, waiting for transfers between devices: 6.36 us -> 1.59 us  [over_rep(): return op(x, lax.ppermute(x, 'rep', [(0, 3), (3, 0), (1, 2), (2, 1)]))]
    ppermute x2, waiting for transfers between devices: 4.08 us -> 1.85 us  [over_rep(): x = op(x, lax.ppermute(x, 'rep', [(0, 1), (1, 0), (2, 3), (3, 2)]))]
    all_to_all x2, starting transfers between devices: 17.7 us -> 15.5 us  [exchange(): return lax.all_to_all(x, 'own', split_axis=0, concat_axis=0, tiled=True)]
  transfers between devices with their start and end apart: 6 -> 6, of which waited for: 6 -> 4; matrix products, arithmetic and copies ran while one was open for 1% -> 1% of each run, Pallas kernels for 15% -> 14%
where the time goes in v3:
time: 187 us; the launch traced here: 186 us
  waiting for transfers between devices  113 us (60%)
  Pallas kernels  44.6 us (24%)
  starting transfers between devices  24.2 us (13%)
  other arithmetic  2 us (1%)
    all_to_all x2, waiting for transfers between devices, exchange(): return lax.all_to_all(x, 'own', split_axis=0, concat_axis=0, tiled=True)  109 us
    pallas_call x4, Pallas kernels, code(): pl.pallas_call(functools.partial(code_kernel, coding, measuring), grid=(g...  26.9 us
    pallas_call x2, Pallas kernels, lay_out(): pl.pallas_call(functools.partial(lay_out_kernel, layers, firsts, groups,...  17.7 us
    all_to_all x2, starting transfers between devices, exchange(): return lax.all_to_all(x, 'own', split_axis=0, concat_axis=0, tiled=True)  15.5 us
    ppermute x2, starting transfers between devices, over_rep(): return op(x, lax.ppermute(x, 'rep', [(0, 3), (3, 0), (1, 2), (2, 1)]))  5.05 us
  transfers between devices with their start and end apart: 6, of which 4 were waited for; matrix products, arithmetic and copies ran while one was open for 1% of the time, Pallas kernels for 14%

profile of v3, /device:TPU:32, one launch (start us, length us, event | category | flops | bytes accessed | tf_op | source)
XLA Modules:
  0.0 185.8 jit_solution(122677069011248853)
XLA Ops:
  1.3 8.2 %lay_out.2 = bf16[32,8,4736]{2,1,0:T(8,128)(2,1)} custom-call(s32[32]{0:T(128)} %index_ref.3, s32[32]{0:T(128)} %layer_ref.3, s32[1]{0:T(128)S(6)} %copy.11.count_ref, bf16[64,64,576]{2,1,0:T(8,128)(2,1)} %pool_ref.3), custom_call_target="tpu_custom_call" | custom-call | flops 100000000 | bytes 20000000 | tf_op jit(solution)/shard_map/lay_out/pallas_call | solution.py:169
  9.5 8.9 %all-to-all-start = ((bf16[32,8,4736]{2,1,0:T(8,128)(2,1)}), bf16[32,8,4736]{2,1,0:T(8,128)(2,1)S(1)}, u32[]{:S(2)}, u32[]{:S(2)}) async-start(bf16[32,8,4736]{2,1,0:T(8,128)(2,1)} %lay_out.2), calls=%async_computation | async-start | bytes 4849664 | tf_op jit(solution)/shard_map/all_to_all | solution.py:259
  18.4 9.5 %lay_out.3 = bf16[32,8,13824]{2,1,0:T(8,128)(2,1)} custom-call(s32[32]{0:T(128)} %index_ref.3, s32[32]{0:T(128)} %layer_ref.3, s32[1]{0:T(128)S(6)} %copy.11.count_ref, bf16[64,64,576]{2,1,0:T(8,128)(2,1)} %pool_ref.3), custom_call_target="tpu_custom_call" | custom-call | flops 100000000 | bytes 20000000 | tf_op jit(solution)/shard_map/lay_out/pallas_call | solution.py:169
  27.9 21.1 %all-to-all-done.raw_ref = bf16[32,8,4736]{2,1,0:T(8,128)(2,1)S(1)} async-done(((bf16[32,8,4736]{2,1,0:T(8,128)(2,1)}), bf16[32,8,4736]{2,1,0:T(8,128)(2,1)S(1)}, u32[]{:S(2)}, u32[]{:S(2)}) %all-to-all-start) | async-done | bytes 2424864 | tf_op jit(solution)/shard_map/all_to_all | solution.py:259
  49.0 0.0 copy-start
  49.0 6.6 %all-to-all-start.1 = ((bf16[32,8,13824]{2,1,0:T(8,128)(2,1)}), bf16[32,8,13824]{2,1,0:T(8,128)(2,1)}, u32[]{:S(2)}, u32[]{:S(2)}) async-start(bf16[32,8,13824]{2,1,0:T(8,128)(2,1)} %lay_out.3), calls=%async_computation.1 | async-start | bytes 14155776 | tf_op jit(solution)/shard_map/all_to_all | solution.py:259
  55.6 0.0 copy-done
  55.7 1.8 collective-permute-start
  57.5 1.9 collective-permute-done
  59.4 3.3 %collective-permute-start.1 = (f32[8,128]{1,0:T(8,128)S(1)}, f32[8,128]{1,0:T(8,128)S(1)}, u32[]{:S(2)}, u32[]{:S(2)}) collective-permute-start(f32[8,128]{1,0:T(8,128)S(1)} %convert_maximum_fusion), channel_id=1, source_target_pairs={{0,3},{3,0},{1,2},{2,1},{4,7},{7,4},{5,6},{6,5},{8,11},{11,8},{9,1... | collective-permute-start | bytes 12296 | tf_op jit(solution)/shard_map/ppermute | solution.py:247
  62.7 1.6 collective-permute-done.1
  64.3 0.6 divide_reduce_fusion
  64.9 0.7 tile.13.inverse_ref
  65.5 4.7 %code.3 = (bf16[32,8,18432]{2,1,0:T(8,128)(2,1)}, f32[8,1152]{1,0:T(8,128)}) custom-call(f32[1,1152]{1,0:T(1,128)} %tile.13.inverse_ref, bf16[32,8,4736]{2,1,0:T(8,128)(2,1)} %copy-done), custom_call_target="tpu_custom_call" | custom-call | flops 80000000 | bytes 4800000 | tf_op jit(solution)/shard_map/code/pallas_call | solution.py:233
  70.2 0.0 copy-start.1
  70.2 88.3 %all-to-all-done.1.raw_ref = bf16[32,8,13824]{2,1,0:T(8,128)(2,1)} async-done(((bf16[32,8,13824]{2,1,0:T(8,128)(2,1)}), bf16[32,8,13824]{2,1,0:T(8,128)(2,1)}, u32[]{:S(2)}, u32[]{:S(2)}) %all-to-all-start.1) | async-done | bytes 7077920 | tf_op jit(solution)/shard_map/all_to_all | solution.py:259
  158.5 10.2 %measure.1 = f32[8,1152]{1,0:T(8,128)} custom-call(f32[1,1152]{1,0:T(1,128)} %tile.13.inverse_ref, bf16[32,8,13824]{2,1,0:T(8,128)(2,1)} %all-to-all-done.1.raw_ref), custom_call_target="tpu_custom_call" | custom-call | flops 240000000 | bytes 14400000 | tf_op jit(solution)/shard_map/measure/pallas_call | solution.py:233
  168.8 0.0 copy-done.1
  168.8 0.8 add_reduce_fusion
  169.6 0.1 reshape.19
  169.7 1.8 collective-permute-start.2
  171.5 6.0 %code.4.refs_0_ = bf16[32,8,18432]{2,1,0:T(8,128)(2,1)} custom-call(f32[1,1152]{1,0:T(1,128)} %tile.13.inverse_ref, bf16[32,8,13824]{2,1,0:T(8,128)(2,1)} %all-to-all-done.1.raw_ref, bf16[32,8,18432]{2,1,0:T(8,128)(2,1)} %get-tuple-element.5.refs_0_), custom_call_target="tpu_custom_call", output_to_operand_aliasing={{}: (2, {})} | custom-call | flops 120000000 | bytes 7200000 | tf_op jit(solution)/shard_map/code/pallas_call | solution.py:233
  177.5 0.0 collective-permute-done.2
  177.5 1.7 collective-permute-start.3
  179.3 6.0 %code.5 = bf16[32,8,18432]{2,1,0:T(8,128)(2,1)} custom-call(f32[1,1152]{1,0:T(1,128)} %tile.13.inverse_ref, bf16[32,8,13824]{2,1,0:T(8,128)(2,1)} %all-to-all-done.1.raw_ref, bf16[32,8,18432]{2,1,0:T(8,128)(2,1)} %code.4.refs_0_), custom_call_target="tpu_custom_call", output_to_operand_aliasing={{}: (2, {})} | custom-call | flops 120000000 | bytes 7200000 | tf_op jit(solution)/shard_map/code/pallas_call | solution.py:233
  185.3 0.0 collective-permute-done.3
  185.3 0.6 add_multiply_fusion
  (8 shorter events, 0.1 us)
Async XLA Ops:
  9.5 39.5 %all-to-all-start = ((bf16[32,8,4736]{2,1,0:T(8,128)(2,1)}), bf16[32,8,4736]{2,1,0:T(8,128)(2,1)S(1)}, u32[]{:S(2)}, u32[]{:S(2)}) async-start(bf16[32,8,4736]{2,1,0:T(8,128)(2,1)} %lay_out.2), calls=%async_computation | async-start | bytes 4849664 | tf_op jit(solution)/shard_map/all_to_all | solution.py:259
  49.0 6.6 %copy-start = (bf16[32,8,4736]{2,1,0:T(8,128)(2,1)}, bf16[32,8,4736]{2,1,0:T(8,128)(2,1)S(1)}, u32[]{:S(2)}) copy-start(bf16[32,8,4736]{2,1,0:T(8,128)(2,1)S(1)} %all-to-all-done.raw_ref) | copy-start | bytes 7274500
  49.0 109.5 %all-to-all-start.1 = ((bf16[32,8,13824]{2,1,0:T(8,128)(2,1)}), bf16[32,8,13824]{2,1,0:T(8,128)(2,1)}, u32[]{:S(2)}, u32[]{:S(2)}) async-start(bf16[32,8,13824]{2,1,0:T(8,128)(2,1)} %lay_out.3), calls=%async_computation.1 | async-start | bytes 14155776 | tf_op jit(solution)/shard_map/all_to_all | solution.py:259
  55.7 3.7 %collective-permute-start = (f32[8,128]{1,0:T(8,128)S(1)}, f32[8,128]{1,0:T(8,128)S(1)}, u32[]{:S(2)}, u32[]{:S(2)}) collective-permute-start(f32[8,128]{1,0:T(8,128)S(1)} %convert_element_type.3), channel_id=1, source_target_pairs={{0,1},{1,0},{2,3},{3,2},{4,5},{5,4},{6,7},{7,6},{8,9},{9,8},{10,11... | collective-permute-start | bytes 12296 | tf_op jit(solution)/shard_map/ppermute | solution.py:246
  59.4 4.9 %collective-permute-start.1 = (f32[8,128]{1,0:T(8,128)S(1)}, f32[8,128]{1,0:T(8,128)S(1)}, u32[]{:S(2)}, u32[]{:S(2)}) collective-permute-start(f32[8,128]{1,0:T(8,128)S(1)} %convert_maximum_fusion), channel_id=1, source_target_pairs={{0,3},{3,0},{1,2},{2,1},{4,7},{7,4},{5,6},{6,5},{8,11},{11,8},{9,1... | collective-permute-start | bytes 12296 | tf_op jit(solution)/shard_map/ppermute | solution.py:247
  70.2 98.6 %copy-start.1 = (f32[8,1152]{1,0:T(8,128)S(1)}, f32[8,1152]{1,0:T(8,128)}, u32[]{:S(2)}) copy-start(f32[8,1152]{1,0:T(8,128)} %get-tuple-element.6) | copy-start | bytes 110596
  169.7 7.8 %collective-permute-start.2 = (f32[1,288]{1,0:T(1,128)S(1)}, f32[1,288]{1,0:T(1,128)S(1)}, u32[]{:S(2)}, u32[]{:S(2)}) collective-permute-start(f32[1,288]{1,0:T(1,128)S(1)} %broadcast_in_dim.7), channel_id=1, source_target_pairs={{0,1},{1,0},{2,3},{3,2},{4,5},{5,4},{6,7},{7,6},{8,9},{9,8},{10,11... | collective-permute-start | bytes 3464 | tf_op jit(solution)/shard_map/ppermute | solution.py:246
  177.5 7.7 %collective-permute-start.3 = (f32[1,288]{1,0:T(1,128)S(1)}, f32[1,288]{1,0:T(1,128)S(1)}, u32[]{:S(2)}, u32[]{:S(2)}) collective-permute-start(f32[1,288]{1,0:T(1,128)S(1)} %reshape_add_fusion), channel_id=1, source_target_pairs={{0,3},{3,0},{1,2},{2,1},{4,7},{7,4},{5,6},{6,5},{8,11},{11,8},{9,1... | collective-permute-start | bytes 3464 | tf_op jit(solution)/shard_map/ppermute | solution.py:247

commit v4 on v0

v4 whole, which is shorter than its diff:
```python
import functools
import jax
import jax.numpy as jnp
from jax import lax
from jax.experimental import pallas as pl
from jax.experimental.pallas import tpu as pltpu
from jax.sharding import PartitionSpec as P

SLICES = 2
CAP = 8
LANES = 128
QUAD = 4
headroom = 0.5


def end_to_end(rows, width, start):
    lane = lax.broadcasted_iota(jnp.int32, rows[0][0].shape, 1)
    turned, out = {}, []
    for i in range(len(rows) * width // LANES):
        whole, at = None, 0
        while at < LANES:
            flat = i * LANES + at
            q = flat // width
            source = flat - q * width + start
            j = source // LANES
            run = min(LANES - source % LANES, (q + 1) * width - flat, LANES - at)
            if (q, j) not in turned:
                shift = (at - source) % LANES
                turned[q, j] = pltpu.roll(rows[q][j], shift, 1) if shift else rows[q][j]
            piece = turned[q, j]
            whole = piece if whole is None else jnp.where(lane >= at, piece, whole)
            at += run
        out.append(whole)
    return out


def peak_kernel(index_ref, layer_ref, count_ref, pool_ref, out_ref, held, acc, top, sems):
    live = count_ref[0]
    tokens, width = held.shape[1:]
    layers = acc.shape[0]
    half = width // SLICES
    pieces = top.shape[0] // SLICES

    def fetch(j):
        return pltpu.make_async_copy(pool_ref.at[index_ref[j]], held.at[j], sems.at[j])

    def start(j, carry):
        fetch(j).start()
        return carry

    lax.fori_loop(0, live, start, 0)
    acc[...] = jnp.zeros_like(acc)
    top[...] = jnp.zeros_like(top)

    def wait(j, carry):
        fetch(j).wait()
        layer = layer_ref[j]
        values = jnp.abs(held[j].astype(jnp.float32)).reshape(tokens // 8, 8, width)
        acc[layer] = jnp.maximum(acc[layer], jnp.max(values, axis=0))
        return carry

    lax.fori_loop(0, live, wait, 0)
    whole = jnp.max(acc[...], axis=1)
    for h in range(SLICES):
        for n in range(pieces):
            lanes = min(LANES, half - n * LANES)
            at = h * half + n * LANES
            top[h * pieces + n, :, :lanes] = whole[:, at : at + lanes]
    row = lax.broadcasted_iota(jnp.int32, (CAP, LANES), 0)

    def tiles(layer, carry):
        for h in range(SLICES):
            tile = jnp.zeros((CAP, LANES), jnp.float32)
            for n in range(pieces):
                one = jnp.broadcast_to(top[h * pieces + n, pl.ds(layer, 1), :], (CAP, LANES))
                tile = jnp.where(row == n, one, tile)
            out_ref[layer * SLICES + h] = tile.astype(jnp.bfloat16)
        return carry

    lax.fori_loop(0, layers, tiles, 0, unroll=4)


def local_peaks(block_pool, sel_index, sel_layer, counts, layers):
    n_select = sel_index.shape[0]
    tokens, width = block_pool.shape[1:]
    pieces = pl.cdiv(width // SLICES, LANES)
    smem = pl.BlockSpec(memory_space=pltpu.SMEM)
    return pl.pallas_call(
        peak_kernel,
        out_shape=jax.ShapeDtypeStruct((layers * SLICES, CAP, LANES), jnp.bfloat16),
        in_specs=[smem, smem, smem, pl.BlockSpec(memory_space=pl.ANY)],
        out_specs=pl.BlockSpec(memory_space=pltpu.VMEM),
        scratch_shapes=[
            pltpu.VMEM((n_select, tokens, width), jnp.bfloat16),
            pltpu.VMEM((layers, 8, width), jnp.float32),
            pltpu.VMEM((SLICES * pieces, layers, LANES), jnp.float32),
            pltpu.SemaphoreType.DMA((n_select,)),
        ],
        cost_estimate=pl.CostEstimate(flops=20_000_000, bytes_accessed=2_500_000, transcendentals=0),
        name="peaks",
    )(sel_index, sel_layer, counts, block_pool)


def lay_out_kernel(first, index_ref, layer_ref, count_ref, pool_ref, *refs):
    out, held, spread, slots, filled, dirty, sems = refs[-7:]
    step = pl.program_id(0)
    live = count_ref[0]
    layers = filled.shape[0]
    tokens, width = held.shape[1:]
    half = width // SLICES
    tiles = spread.shape[0]
    pitch = spread.shape[1] // CAP
    group = QUAD * half

    def fetch(j):
        return pltpu.make_async_copy(pool_ref.at[index_ref[j]], held.at[j], sems.at[j])

    @pl.when(step == 0)
    def _():
        for layer in range(layers):
            filled[layer] = 0
        dirty[0] = CAP

        def start(j, carry):
            layer = layer_ref[j] - first

            @pl.when((layer >= 0) & (layer < layers))
            def _():
                fetch(j).start()
                at = filled[layer]
                slots[layer * CAP + at] = j
                filled[layer] = at + 1

            return carry

        lax.fori_loop(0, live, start, 0)

    held_slots = filled[step]

    @pl.when(held_slots == 0)
    def _():
        out[...] = jnp.zeros_like(out)

    @pl.when(held_slots > 0)
    def _():
        def place(c, carry):
            j = slots[step * CAP + c]
            fetch(j).wait()
            values = held[j].astype(jnp.float32)
            rows = pl.ds(pl.multiple_of(c * pitch, 8), tokens)
            for i in range(tiles):
                lanes = min(LANES, width - i * LANES)
                spread[i, rows, :lanes] = values[:, i * LANES : i * LANES + lanes]
            return carry

        lax.fori_loop(0, held_slots, place, 0)

        def blank(c, carry):
            for i in range(tiles):
                spread[i, pl.ds(pl.multiple_of(c * pitch, 8), tokens), :] = jnp.zeros((tokens, LANES), jnp.float32)
            return carry

        lax.fori_loop(held_slots, dirty[0], blank, 0)
        dirty[0] = held_slots

        def four_tokens(u, carry):
            rows = [
                [spread[i, pl.ds(QUAD * u + q, CAP, stride=pitch), :] for i in range(tiles)] for q in range(QUAD)
            ]
            for h in range(SLICES):
                for i, tile in enumerate(end_to_end(rows, half, h * half)):
                    where = pl.ds(pl.multiple_of(u * group + i * LANES, LANES), LANES)
                    out[h, :, where] = tile.astype(jnp.bfloat16)
            return carry

        lax.fori_loop(0, tokens // QUAD, four_tokens, 0, unroll=4)


def lay_out(block_pool, sel_index, sel_layer, counts, out, first, layers, all_layers):
    n_select = sel_index.shape[0]
    tokens, width = block_pool.shape[1:]
    flat = tokens * (width // SLICES)
    pitch = tokens + 8
    smem = pl.BlockSpec(memory_space=pltpu.SMEM)
    specs = [smem, smem, smem, pl.BlockSpec(memory_space=pl.ANY)]
    args = [sel_index, sel_layer, counts, block_pool]
    if out is not None:
        specs.append(pl.BlockSpec(memory_space=pl.ANY))
        args.append(out)
    return pl.pallas_call(
        functools.partial(lay_out_kernel, first),
        grid=(layers,),
        out_shape=jax.ShapeDtypeStruct((all_layers * SLICES, CAP, flat + LANES), jnp.bfloat16),
        in_specs=specs,
        out_specs=pl.BlockSpec((SLICES, CAP, flat), lambda l: (first + l, 0, 0)),
        scratch_shapes=[
            pltpu.VMEM((n_select, tokens, width), jnp.bfloat16),
            pltpu.VMEM((pl.cdiv(width, LANES), CAP * pitch, LANES), jnp.float32),
            pltpu.SMEM((layers * CAP,), jnp.int32),
            pltpu.SMEM((layers,), jnp.int32),
            pltpu.SMEM((1,), jnp.int32),
            pltpu.SemaphoreType.DMA((n_select,)),
        ],
        input_output_aliases={} if out is None else {4: 0},
        cost_estimate=pl.CostEstimate(flops=50_000_000, bytes_accessed=6_000_000, transcendentals=0),
        name="lay_out",
    )(*args)


def append_kernel(tile_ref, _, out_ref):
    out_ref[...] = tile_ref[...]


def append(tile, out):
    groups, cap, lanes = tile.shape
    last = out.shape[2] // lanes - 1
    return pl.pallas_call(
        append_kernel,
        grid=(1,),
        out_shape=jax.ShapeDtypeStruct(out.shape, out.dtype),
        in_specs=[pl.BlockSpec((groups, cap, lanes), lambda i: (0, 0, 0)), pl.BlockSpec(memory_space=pl.ANY)],
        out_specs=pl.BlockSpec((groups, cap, lanes), lambda i: (0, 0, last)),
        input_output_aliases={1: 0},
        name="append",
    )(tile, out)


def measure_kernel(peak_ref, raw_ref, inverse_ref, steps_ref, error_ref, total):
    sources, cap, lanes = raw_ref.shape
    tiles = lanes // LANES
    half = lanes // QUAD
    step = pl.program_id(0)

    @pl.when(step == 0)
    def _():
        peak = jnp.max(peak_ref[...].astype(jnp.float32), axis=0)
        scale = headroom * jnp.maximum(peak, 1.0) / 127.0
        rows = [jnp.broadcast_to(scale[n : n + 1], (cap, LANES)) for n in range(pl.cdiv(half, LANES))]
        for n, row in enumerate(rows):
            size = min(LANES, half - n * LANES)
            steps_ref[:, n * LANES : n * LANES + size] = row[:1, :size]
        for i, tile in enumerate(end_to_end([rows] * QUAD, half, 0)):
            inverse_ref[:, i * LANES : (i + 1) * LANES] = 1.0 / tile
        total[...] = jnp.zeros_like(total)

    inverse = [inverse_ref[:, i * LANES : (i + 1) * LANES] for i in range(tiles)]

    def source(s, totals):
        out = []
        for i in range(tiles):
            exact = raw_ref[s, :, i * LANES : (i + 1) * LANES].astype(jnp.float32) * inverse[i]
            miss = exact - jnp.clip(exact, -127.0, 127.0).astype(jnp.bfloat16).astype(jnp.float32)
            out.append(totals[i] + miss * miss)
        return tuple(out)

    totals = lax.fori_loop(
        0, sources, source, tuple(total[:, i * LANES : (i + 1) * LANES] for i in range(tiles)), unroll=8
    )
    for i in range(tiles):
        total[:, i * LANES : (i + 1) * LANES] = totals[i]

    @pl.when(step == pl.num_programs(0) - 1)
    def _():
        whole = jnp.sum(total[...], axis=0, keepdims=True)
        error = whole[:, :half]
        for q in range(1, QUAD):
            error = error + whole[:, q * half : (q + 1) * half]
        error_ref[...] = error


def measure(raw, groups, half):
    sources, cap, _ = raw.shape
    lanes = QUAD * half
    return pl.pallas_call(
        measure_kernel,
        grid=(groups,),
        out_shape=[
            jax.ShapeDtypeStruct((cap, lanes), jnp.float32),
            jax.ShapeDtypeStruct((1, half), jnp.float32),
            jax.ShapeDtypeStruct((1, half), jnp.float32),
        ],
        in_specs=[
            pl.BlockSpec((sources, cap, LANES), lambda u: (0, 0, groups * lanes // LANES)),
            pl.BlockSpec((sources, cap, lanes), lambda u: (0, 0, u)),
        ],
        out_specs=[
            pl.BlockSpec((cap, lanes), lambda u: (0, 0)),
            pl.BlockSpec((1, half), lambda u: (0, 0)),
            pl.BlockSpec((1, half), lambda u: (0, 0)),
        ],
        scratch_shapes=[pltpu.VMEM((cap, lanes), jnp.float32)],
        cost_estimate=pl.CostEstimate(flops=20_000_000 * groups, bytes_accessed=600_000 * groups, transcendentals=0),
        name="measure",
    )(raw, raw)


def code_kernel(inverse_ref, raw_ref, *refs):
    codes_ref = refs[-1]
    sources, _, lanes = raw_ref.shape
    tiles = lanes // LANES
    inverse = [inverse_ref[:, i * LANES : (i + 1) * LANES] for i in range(tiles)]

    def source(s, carry):
        for i in range(tiles):
            at = slice(i * LANES, (i + 1) * LANES)
            exact = raw_ref[s, :, at].astype(jnp.float32) * inverse[i]
            codes_ref[s, :, at] = jnp.clip(exact, -127.0, 127.0).astype(jnp.bfloat16)
        return carry

    lax.fori_loop(0, sources, source, 0, unroll=8)


def code(raw, inverse, codes, first, groups, all_groups):
    sources, cap, _ = raw.shape
    lanes = inverse.shape[1]
    specs = [
        pl.BlockSpec((cap, lanes), lambda u: (0, 0)),
        pl.BlockSpec((sources, cap, lanes), lambda u: (0, 0, first + u)),
    ]
    args = [inverse, raw]
    if codes is not None:
        specs.append(pl.BlockSpec(memory_space=pl.ANY))
        args.append(codes)
    return pl.pallas_call(
        code_kernel,
        grid=(groups,),
        out_shape=jax.ShapeDtypeStruct((sources, cap, lanes * all_groups), jnp.bfloat16),
        in_specs=specs,
        out_specs=pl.BlockSpec((sources, cap, lanes), lambda u: (0, 0, first + u)),
        input_output_aliases={} if codes is None else {2: 0},
        cost_estimate=pl.CostEstimate(flops=20_000_000 * groups, bytes_accessed=1_200_000 * groups, transcendentals=0),
        name="code",
    )(*args)


def over_rep(x, op, beside):
    done = None
    for pairs, work in zip(([(0, 1), (1, 0), (2, 3), (3, 2)], [(0, 3), (3, 0), (1, 2), (2, 1)]), beside):
        other = lax.ppermute(x, "rep", pairs)
        done = work(done)
        x, done = lax.optimization_barrier((op(x, other), done))
    return x, done


def body(block_pool, sel_index, sel_layer, counts):
    own_count = lax.axis_size("own")
    rep_count = lax.axis_size("rep")
    layers = own_count // SLICES
    tokens, width = block_pool.shape[1:]
    half = width // SLICES
    selection = (block_pool, sel_index, sel_layer, counts)

    upper = layers // 2
    peak, sent = over_rep(
        local_peaks(*selection, layers),
        jnp.maximum,
        (
            lambda out: lay_out(*selection, out, 0, upper, layers),
            lambda out: lay_out(*selection, out, upper, layers - upper, layers),
        ),
    )
    sent = append(peak, sent)
    arrived = lax.all_to_all(sent, "own", split_axis=0, concat_axis=0, tiled=True)

    every = tokens // QUAD
    inverse, steps, error = measure(arrived, every, half)
    split = every // 2
    error, codes = over_rep(
        error,
        jnp.add,
        (
            lambda out: code(arrived, inverse, out, 0, split, every),
            lambda out: code(arrived, inverse, out, split, every - split, every),
        ),
    )
    denominator = float(own_count * rep_count * CAP * tokens)
    return codes[None, None], steps, error / denominator


def solution(mesh):
    return jax.shard_map(
        body,
        mesh=mesh,
        in_specs=(
            P(("own", "rep"), None, None),
            P(("own", "rep")),
            P(("own", "rep")),
            P(("own", "rep")),
        ),
        out_specs=(P("own", "rep", None, None, None), P("own", None), P("own", None)),
        check_vma=False,
    )
```

time: 264 us -> 174 us (0.66)
  local copies, waits for them, and re-layouts: 88.9 us -> 0.01 us
  Pallas kernels: 0 us -> 44.8 us
  other arithmetic: 40.3 us -> 1.25 us
  blocking collectives: 123 us -> 116 us
  waiting for transfers between devices: 4.71 us -> 0.01 us
  starting transfers between devices: 3.25 us -> 7.91 us
    gather x2 -> x0, local copies, waits for them, and re-layouts: 46 us -> none  [body(): picked = jnp.take(pool_rows, chosen.reshape(-1), axis=0)]
    pallas_call x0 -> x7, Pallas kernels: none -> 44.8 us  [the longest x2 14.6 us: code(): pl.pallas_call(code_kernel, grid=(groups,), out_shape=jax.ShapeDtypeStruc...]
    reshape x4 -> x0, local copies, waits for them, and re-layouts: 31 us -> none  [the longest x1 20.9 us: body(): picked.transpose(0, 3, 1, 2, 4).reshape(own_count, capacity, flat_width)]
    transpose x1 -> x0, other arithmetic: 16.3 us -> none  [body(): picked.transpose(0, 3, 1, 2, 4).reshape(own_count, capacity, flat_width)]
    reduce_sum x4 -> x0, other arithmetic: 11.2 us -> none  [the longest x1 10.1 us: body(): flat_error = jnp.sum((values - decoded) ** 2, axis=(0, 1))]
    convert_element_type x1 -> x0, other arithmetic: 9.83 us -> none  [body(): encoded = jnp.clip(values / step_flat, -127.0, 127.0).astype(jnp.bfloat16)]
    ppermute x0 -> x4, starting transfers between devices: none -> 7.91 us  [over_rep(): other = lax.ppermute(x, 'rep', pairs)]
    all_to_all x2 -> x1, blocking collectives: 123 us -> 116 us  [body(): lax.all_to_all(sent, 'own', split_axis=0, concat_axis=0, tiled=True)]
  transfers between devices with their start and end apart: 1 -> 4, of which waited for: 1 -> 0; matrix products, arithmetic and copies ran while one was open for 0% -> 0% of each run, Pallas kernels for 0% -> 16%
where the time goes in v4:
time: 174 us; the launch traced here: 171 us
  blocking collectives  116 us (67%)
  Pallas kernels  44.8 us (26%)
  starting transfers between devices  7.91 us (5%)
    all_to_all x1, blocking collectives, body(): lax.all_to_all(sent, 'own', split_axis=0, concat_axis=0, tiled=True)  116 us
    pallas_call x2, Pallas kernels, code(): pl.pallas_call(code_kernel, grid=(groups,), out_shape=jax.ShapeDtypeStruc...  14.6 us
    pallas_call x2, Pallas kernels, lay_out(): pl.pallas_call(functools.partial(lay_out_kernel, first), grid=(layers,),...  13 us
    pallas_call x1, Pallas kernels, measure(): pl.pallas_call(measure_kernel, grid=(groups,), out_shape=[jax.ShapeDtypeS...  12.7 us
    ppermute x4, starting transfers between devices, over_rep(): other = lax.ppermute(x, 'rep', pairs)  7.91 us
  transfers between devices with their start and end apart: 4, of which 0 were waited for; matrix products, arithmetic and copies ran while one was open for 0% of the time, Pallas kernels for 16%

profile of v4, /device:TPU:32, one launch (start us, length us, event | category | flops | bytes accessed | tf_op | source)
XLA Modules:
  0.0 171.0 jit_solution(13240822277916438372)
XLA Ops:
  1.3 3.0 %peaks.1 = bf16[32,8,128]{2,1,0:T(8,128)(2,1)} custom-call(s32[32]{0:T(128)} %index_ref.5, s32[32]{0:T(128)} %layer_ref.5, s32[1]{0:T(128)S(6)} %copy.13.count_ref, bf16[64,64,576]{2,1,0:T(8,128)(2,1)} %pool_ref.5), custom_call_target="tpu_custom_call" | custom-call | flops 20000000 | bytes 2500000 | tf_op jit(solution)/shard_map/peaks/pallas_call | solution.py:88
  4.3 0.0 copy-start
  4.3 1.6 collective-permute-start
  6.0 6.3 %lay_out.2.refs_0_ = bf16[32,8,18560]{2,1,0:T(8,128)(2,1)} custom-call(s32[32]{0:T(128)} %index_ref.5, s32[32]{0:T(128)} %layer_ref.5, s32[1]{0:T(128)S(6)} %copy.13.count_ref, bf16[64,64,576]{2,1,0:T(8,128)(2,1)} %pool_ref.5), custom_call_target="tpu_custom_call" | custom-call | flops 50000000 | bytes 6000000 | tf_op jit(solution)/shard_map/lay_out/pallas_call | solution.py:190
  12.2 0.0 collective-permute-done
  12.2 0.0 copy-done
  12.3 3.6 %collective-permute-start.1 = (bf16[32,8,128]{2,1,0:T(8,128)(2,1)S(1)}, bf16[32,8,128]{2,1,0:T(8,128)(2,1)S(1)}, u32[]{:S(2)}, u32[]{:S(2)}) collective-permute-start(bf16[32,8,128]{2,1,0:T(8,128)(2,1)S(1)} %max.6), channel_id=1, source_target_pairs={{0,3},{3,0},{1,2},{2,1},{4,7},{7,4},{5,6},{6,5},{8,11},{11,8},{9,1... | collective-permute-start | bytes 196616 | tf_op jit(solution)/shard_map/ppermute | solution.py:339
  15.9 6.7 %lay_out.3._ = bf16[32,8,18560]{2,1,0:T(8,128)(2,1)} custom-call(s32[32]{0:T(128)} %index_ref.5, s32[32]{0:T(128)} %layer_ref.5, s32[1]{0:T(128)S(6)} %copy.13.count_ref, bf16[64,64,576]{2,1,0:T(8,128)(2,1)} %pool_ref.5, bf16[32,8,18560]{2,1,0:T(8,128)(2,1)} %lay_out.2.refs_0_), custom_call_target="tpu_custom_call", output_to_operand_aliasing={{}: (4, {})} | custom-call | flops 50000000 | bytes 6000000 | tf_op jit(solution)/shard_map/lay_out/pallas_call | solution.py:190
  22.6 0.0 collective-permute-done.1
  22.6 0.7 max.7.tile_ref
  23.3 1.5 append.1
  24.8 115.6 %all_to_all.5.peak_ref.raw_ref = bf16[32,8,18560]{2,1,0:T(8,128)(2,1)} all-to-all(bf16[32,8,18560]{2,1,0:T(8,128)(2,1)} %append.1), channel_id=1, replica_groups=mesh['own'=32,'rep'=4] {'own'}, dimensions={0} | all-to-all | bytes 19005440 | tf_op jit(solution)/shard_map/all_to_all | solution.py:363
  140.4 12.7 %measure.1 = (f32[8,1152]{1,0:T(8,128)}, f32[1,288]{1,0:T(1,128)}, f32[1,288]{1,0:T(1,128)}) custom-call(bf16[32,8,18560]{2,1,0:T(8,128)(2,1)} %all_to_all.5.peak_ref.raw_ref, bf16[32,8,18560]{2,1,0:T(8,128)(2,1)} %all_to_all.5.peak_ref.raw_ref), custom_call_target="tpu_custom_call" | custom-call | flops 320000000 | bytes 9600000 | tf_op jit(solution)/shard_map/measure/pallas_call | solution.py:274
  153.1 0.0 copy-start.1
  153.1 1.4 collective-permute-start.2
  154.5 7.3 %code.2.refs_0_ = bf16[32,8,18432]{2,1,0:T(8,128)(2,1)} custom-call(f32[8,1152]{1,0:T(8,128)} %get-tuple-element.19.inverse_ref, bf16[32,8,18560]{2,1,0:T(8,128)(2,1)} %all_to_all.5.peak_ref.raw_ref), custom_call_target="tpu_custom_call" | custom-call | flops 160000000 | bytes 9600000 | tf_op jit(solution)/shard_map/code/pallas_call | solution.py:324
  161.8 0.0 collective-permute-done.2
  161.8 0.0 copy-done.1
  161.8 1.3 collective-permute-start.3
  163.1 7.3 %code.3 = bf16[32,8,18432]{2,1,0:T(8,128)(2,1)} custom-call(f32[8,1152]{1,0:T(8,128)} %get-tuple-element.19.inverse_ref, bf16[32,8,18560]{2,1,0:T(8,128)(2,1)} %all_to_all.5.peak_ref.raw_ref, bf16[32,8,18432]{2,1,0:T(8,128)(2,1)} %code.2.refs_0_), custom_call_target="tpu_custom_call", output_to_operand_aliasing={{}: (2, {})} | custom-call | flops 160000000 | bytes 9600000 | tf_op jit(solution)/shard_map/code/pallas_call | solution.py:324
  170.4 0.0 collective-permute-done.3
  170.4 0.6 broadcast_multiply_fusion
  (3 shorter events, 0.0 us)
Async XLA Ops:
  4.3 7.9 %copy-start = (bf16[32,8,128]{2,1,0:T(8,128)(2,1)S(1)}, bf16[32,8,128]{2,1,0:T(8,128)(2,1)}, u32[]{:S(2)}) copy-start(bf16[32,8,128]{2,1,0:T(8,128)(2,1)} %peaks.1) | copy-start | bytes 196612
  4.3 7.9 %collective-permute-start = (bf16[32,8,128]{2,1,0:T(8,128)(2,1)}, bf16[32,8,128]{2,1,0:T(8,128)(2,1)S(1)}, u32[]{:S(2)}, u32[]{:S(2)}) collective-permute-start(bf16[32,8,128]{2,1,0:T(8,128)(2,1)} %peaks.1), channel_id=1, source_target_pairs={{0,1},{1,0},{2,3},{3,2},{4,5},{5,4},{6,7},{7,6},{8,9},{9,8},{10,11... | collective-permute-start | bytes 196616 | tf_op jit(solution)/shard_map/ppermute | solution.py:339
  12.3 10.4 %collective-permute-start.1 = (bf16[32,8,128]{2,1,0:T(8,128)(2,1)S(1)}, bf16[32,8,128]{2,1,0:T(8,128)(2,1)S(1)}, u32[]{:S(2)}, u32[]{:S(2)}) collective-permute-start(bf16[32,8,128]{2,1,0:T(8,128)(2,1)S(1)} %max.6), channel_id=1, source_target_pairs={{0,3},{3,0},{1,2},{2,1},{4,7},{7,4},{5,6},{6,5},{8,11},{11,8},{9,1... | collective-permute-start | bytes 196616 | tf_op jit(solution)/shard_map/ppermute | solution.py:339
  153.1 8.7 %copy-start.1 = (f32[1,288]{1,0:T(1,128)S(1)}, f32[1,288]{1,0:T(1,128)}, u32[]{:S(2)}) copy-start(f32[1,288]{1,0:T(1,128)} %get-tuple-element.18) | copy-start | bytes 3460
  153.1 8.7 %collective-permute-start.2 = (f32[1,288]{1,0:T(1,128)}, f32[1,288]{1,0:T(1,128)S(1)}, u32[]{:S(2)}, u32[]{:S(2)}) collective-permute-start(f32[1,288]{1,0:T(1,128)} %get-tuple-element.18), channel_id=1, source_target_pairs={{0,1},{1,0},{2,3},{3,2},{4,5},{5,4},{6,7},{7,6},{8,9},{9,8},{10,11... | collective-permute-start | bytes 3464 | tf_op jit(solution)/shard_map/ppermute | solution.py:339
  161.8 8.6 %collective-permute-start.3 = (f32[1,288]{1,0:T(1,128)S(1)}, f32[1,288]{1,0:T(1,128)S(1)}, u32[]{:S(2)}, u32[]{:S(2)}) collective-permute-start(f32[1,288]{1,0:T(1,128)S(1)} %add.6), channel_id=1, source_target_pairs={{0,3},{3,0},{1,2},{2,1},{4,7},{7,4},{5,6},{6,5},{8,11},{11,8},{9,1... | collective-permute-start | bytes 3464 | tf_op jit(solution)/shard_map/ppermute | solution.py:339

commit v5 on v4

v5 whole, which is shorter than its diff:
```python
import functools
import jax
import jax.numpy as jnp
from jax import lax
from jax.experimental import pallas as pl
from jax.experimental.pallas import tpu as pltpu
from jax.sharding import PartitionSpec as P

SLICES = 2
CAP = 8
LANES = 128
QUAD = 4
headroom = 0.5


def end_to_end(rows, width, start):
    lane = lax.broadcasted_iota(jnp.int32, rows[0][0].shape, 1)
    turned, out = {}, []
    for i in range(len(rows) * width // LANES):
        whole, at = None, 0
        while at < LANES:
            flat = i * LANES + at
            q = flat // width
            source = flat - q * width + start
            j = source // LANES
            run = min(LANES - source % LANES, (q + 1) * width - flat, LANES - at)
            if (q, j) not in turned:
                shift = (at - source) % LANES
                turned[q, j] = pltpu.roll(rows[q][j], shift, 1) if shift else rows[q][j]
            piece = turned[q, j]
            whole = piece if whole is None else jnp.where(lane >= at, piece, whole)
            at += run
        out.append(whole)
    return out


def peak_kernel(index_ref, layer_ref, count_ref, pool_ref, out_ref, held, acc, top, sems):
    live = count_ref[0]
    tokens, width = held.shape[1:]
    layers = acc.shape[0]
    half = width // SLICES
    pieces = top.shape[0] // SLICES

    def fetch(j):
        return pltpu.make_async_copy(pool_ref.at[index_ref[j]], held.at[j], sems.at[j])

    def start(j, carry):
        fetch(j).start()
        return carry

    lax.fori_loop(0, live, start, 0)
    acc[...] = jnp.zeros_like(acc)
    top[...] = jnp.zeros_like(top)

    def wait(j, carry):
        fetch(j).wait()
        layer = layer_ref[j]
        values = jnp.abs(held[j].astype(jnp.float32)).reshape(tokens // 8, 8, width)
        acc[layer] = jnp.maximum(acc[layer], jnp.max(values, axis=0))
        return carry

    lax.fori_loop(0, live, wait, 0)
    whole = jnp.max(acc[...], axis=1)
    for h in range(SLICES):
        for n in range(pieces):
            lanes = min(LANES, half - n * LANES)
            at = h * half + n * LANES
            top[h * pieces + n, :, :lanes] = whole[:, at : at + lanes]
    row = lax.broadcasted_iota(jnp.int32, (CAP, LANES), 0)

    def tiles(layer, carry):
        for h in range(SLICES):
            tile = jnp.zeros((CAP, LANES), jnp.float32)
            for n in range(pieces):
                one = jnp.broadcast_to(top[h * pieces + n, pl.ds(layer, 1), :], (CAP, LANES))
                tile = jnp.where(row == n, one, tile)
            out_ref[layer * SLICES + h] = tile.astype(jnp.bfloat16)
        return carry

    lax.fori_loop(0, layers, tiles, 0, unroll=4)


def local_peaks(block_pool, sel_index, sel_layer, counts, layers):
    n_select = sel_index.shape[0]
    tokens, width = block_pool.shape[1:]
    pieces = pl.cdiv(width // SLICES, LANES)
    smem = pl.BlockSpec(memory_space=pltpu.SMEM)
    return pl.pallas_call(
        peak_kernel,
        out_shape=jax.ShapeDtypeStruct((layers * SLICES, CAP, LANES), jnp.bfloat16),
        in_specs=[smem, smem, smem, pl.BlockSpec(memory_space=pl.ANY)],
        out_specs=pl.BlockSpec(memory_space=pltpu.VMEM),
        scratch_shapes=[
            pltpu.VMEM((n_select, tokens, width), jnp.bfloat16),
            pltpu.VMEM((layers, 8, width), jnp.float32),
            pltpu.VMEM((SLICES * pieces, layers, LANES), jnp.float32),
            pltpu.SemaphoreType.DMA((n_select,)),
        ],
        cost_estimate=pl.CostEstimate(flops=20_000_000, bytes_accessed=2_500_000, transcendentals=0),
        name="peaks",
    )(sel_index, sel_layer, counts, block_pool)


def lay_out_kernel(first, index_ref, layer_ref, count_ref, pool_ref, *refs):
    out_ref, built, held, spread, slots, filled, dirty, sems, out_sems = refs[-9:]
    live = count_ref[0]
    layers = filled.shape[0]
    tokens, width = held.shape[1:]
    half = width // SLICES
    tiles = spread.shape[0]
    pitch = spread.shape[1] // CAP
    group = QUAD * half

    def fetch(j):
        return pltpu.make_async_copy(pool_ref.at[index_ref[j]], held.at[j], sems.at[j])

    def send(layer):
        here = pl.ds(SLICES * layer, SLICES)
        there = pl.ds(SLICES * (first + layer), SLICES)
        return pltpu.make_async_copy(
            built.at[here], out_ref.at[there, :, pl.ds(0, tokens * half)], out_sems.at[layer]
        )

    for layer in range(layers):
        filled[layer] = 0
    dirty[0] = CAP

    def start(j, carry):
        layer = layer_ref[j] - first

        @pl.when((layer >= 0) & (layer < layers))
        def _():
            fetch(j).start()
            at = filled[layer]
            slots[layer * CAP + at] = j
            filled[layer] = at + 1

        return carry

    lax.fori_loop(0, live, start, 0)

    def build(layer, carry):
        held_slots = filled[layer]

        @pl.when(held_slots == 0)
        def _():
            built[pl.ds(SLICES * layer, SLICES)] = jnp.zeros((SLICES, *built.shape[1:]), built.dtype)

        @pl.when(held_slots > 0)
        def _():
            def place(c, carry):
                j = slots[layer * CAP + c]
                fetch(j).wait()
                values = held[j].astype(jnp.float32)
                rows = pl.ds(pl.multiple_of(c * pitch, 8), tokens)
                for i in range(tiles):
                    lanes = min(LANES, width - i * LANES)
                    spread[i, rows, :lanes] = values[:, i * LANES : i * LANES + lanes]
                return carry

            lax.fori_loop(0, held_slots, place, 0)

            def blank(c, carry):
                for i in range(tiles):
                    spread[i, pl.ds(pl.multiple_of(c * pitch, 8), tokens), :] = jnp.zeros((tokens, LANES), jnp.float32)
                return carry

            lax.fori_loop(held_slots, dirty[0], blank, 0)
            dirty[0] = held_slots

            def four_tokens(u, carry):
                rows = [
                    [spread[i, pl.ds(QUAD * u + q, CAP, stride=pitch), :] for i in range(tiles)] for q in range(QUAD)
                ]
                for h in range(SLICES):
                    for i, tile in enumerate(end_to_end(rows, half, h * half)):
                        where = pl.ds(pl.multiple_of(u * group + i * LANES, LANES), LANES)
                        built[SLICES * layer + h, :, where] = tile.astype(jnp.bfloat16)
                return carry

            lax.fori_loop(0, tokens // QUAD, four_tokens, 0, unroll=4)

        send(layer).start()
        return carry

    lax.fori_loop(0, layers, build, 0)

    def finish(layer, carry):
        send(layer).wait()
        return carry

    lax.fori_loop(0, layers, finish, 0)


def lay_out(block_pool, sel_index, sel_layer, counts, out, first, layers, all_layers):
    n_select = sel_index.shape[0]
    tokens, width = block_pool.shape[1:]
    flat = tokens * (width // SLICES)
    pitch = tokens + 8
    smem = pl.BlockSpec(memory_space=pltpu.SMEM)
    hbm = pl.BlockSpec(memory_space=pl.ANY)
    specs = [smem, smem, smem, hbm]
    args = [sel_index, sel_layer, counts, block_pool]
    if out is not None:
        specs.append(hbm)
        args.append(out)
    return pl.pallas_call(
        functools.partial(lay_out_kernel, first),
        out_shape=jax.ShapeDtypeStruct((all_layers * SLICES, CAP, flat + LANES), jnp.bfloat16),
        in_specs=specs,
        out_specs=hbm,
        scratch_shapes=[
            pltpu.VMEM((layers * SLICES, CAP, flat), jnp.bfloat16),
            pltpu.VMEM((n_select, tokens, width), jnp.bfloat16),
            pltpu.VMEM((pl.cdiv(width, LANES), CAP * pitch, LANES), jnp.float32),
            pltpu.SMEM((layers * CAP,), jnp.int32),
            pltpu.SMEM((layers,), jnp.int32),
            pltpu.SMEM((1,), jnp.int32),
            pltpu.SemaphoreType.DMA((n_select,)),
            pltpu.SemaphoreType.DMA((layers,)),
        ],
        input_output_aliases={} if out is None else {4: 0},
        cost_estimate=pl.CostEstimate(flops=50_000_000, bytes_accessed=6_000_000, transcendentals=0),
        name="lay_out",
    )(*args)


def append_kernel(mine_ref, other_ref, _, out_ref, tile, sem):
    tile[...] = jnp.maximum(mine_ref[...], other_ref[...])
    lanes = tile.shape[2]
    copy = pltpu.make_async_copy(tile, out_ref.at[:, :, pl.ds(out_ref.shape[2] - lanes, lanes)], sem)
    copy.start()
    copy.wait()


def append(mine, other, out):
    vmem = pl.BlockSpec(memory_space=pltpu.VMEM)
    hbm = pl.BlockSpec(memory_space=pl.ANY)
    return pl.pallas_call(
        append_kernel,
        out_shape=jax.ShapeDtypeStruct(out.shape, out.dtype),
        in_specs=[vmem, vmem, hbm],
        out_specs=hbm,
        scratch_shapes=[pltpu.VMEM(mine.shape, mine.dtype), pltpu.SemaphoreType.DMA],
        input_output_aliases={2: 0},
        name="append",
    )(mine, other, out)


BATCH = 2


def encode_kernel(raw_ref, codes_ref, steps_ref, error_ref, peaks, raw, codes, inverse, peak_sem, in_sems, out_sems):
    sources, cap, _ = raw.shape
    lanes = inverse.shape[1]
    half = lanes // QUAD
    tiles = lanes // LANES
    flat = codes.shape[2]
    batches = sources // BATCH

    def take(b):
        here = pl.ds(b * BATCH, BATCH)
        return pltpu.make_async_copy(raw_ref.at[here, :, pl.ds(0, flat)], raw.at[here], in_sems.at[b])

    def give(b):
        here = pl.ds(b * BATCH, BATCH)
        return pltpu.make_async_copy(codes.at[here], codes_ref.at[here], out_sems.at[b])

    take_peaks = pltpu.make_async_copy(raw_ref.at[:, :, pl.ds(flat, LANES)], peaks, peak_sem)
    take_peaks.start()
    for b in range(batches):
        take(b).start()
    take_peaks.wait()
    peak = jnp.max(peaks[...].astype(jnp.float32), axis=0)
    scale = headroom * jnp.maximum(peak, 1.0) / 127.0
    rows = [jnp.broadcast_to(scale[n : n + 1], (cap, LANES)) for n in range(pl.cdiv(half, LANES))]
    for n, row in enumerate(rows):
        size = min(LANES, half - n * LANES)
        steps_ref[:, n * LANES : n * LANES + size] = row[:1, :size]
    for i, tile in enumerate(end_to_end([rows] * QUAD, half, 0)):
        inverse[:, i * LANES : (i + 1) * LANES] = 1.0 / tile
    by_lane = [inverse[:, i * LANES : (i + 1) * LANES] for i in range(tiles)]

    def batch(b, totals):
        take(b).wait()

        def group(u, totals):
            totals = list(totals)
            for i in range(tiles):
                at = pl.ds(pl.multiple_of(u * lanes + i * LANES, LANES), LANES)
                for s in range(BATCH):
                    exact = raw[b * BATCH + s, :, at].astype(jnp.float32) * by_lane[i]
                    coded = jnp.clip(exact, -127.0, 127.0).astype(jnp.bfloat16)
                    codes[b * BATCH + s, :, at] = coded
                    miss = exact - coded.astype(jnp.float32)
                    totals[i] = totals[i] + miss * miss
            return tuple(totals)

        totals = lax.fori_loop(0, flat // lanes, group, totals, unroll=4)
        give(b).start()
        return totals

    totals = lax.fori_loop(
        0, batches, batch, tuple(jnp.zeros((cap, LANES), jnp.float32) for _ in range(tiles))
    )
    whole = jnp.concatenate([jnp.sum(t, axis=0, keepdims=True) for t in totals], axis=1)
    error = whole[:, :half]
    for q in range(1, QUAD):
        error = error + whole[:, q * half : (q + 1) * half]
    error_ref[...] = error
    for b in range(batches):
        give(b).wait()


def encode(raw, half):
    sources, cap, size = raw.shape
    flat = size - LANES
    vmem = pl.BlockSpec(memory_space=pltpu.VMEM)
    hbm = pl.BlockSpec(memory_space=pl.ANY)
    return pl.pallas_call(
        encode_kernel,
        out_shape=[
            jax.ShapeDtypeStruct((sources, cap, flat), jnp.bfloat16),
            jax.ShapeDtypeStruct((1, half), jnp.float32),
            jax.ShapeDtypeStruct((1, half), jnp.float32),
        ],
        in_specs=[hbm],
        out_specs=[hbm, vmem, vmem],
        scratch_shapes=[
            pltpu.VMEM((sources, cap, LANES), jnp.bfloat16),
            pltpu.VMEM((sources, cap, flat), jnp.bfloat16),
            pltpu.VMEM((sources, cap, flat), jnp.bfloat16),
            pltpu.VMEM((cap, QUAD * half), jnp.float32),
            pltpu.SemaphoreType.DMA,
            pltpu.SemaphoreType.DMA((sources // BATCH,)),
            pltpu.SemaphoreType.DMA((sources // BATCH,)),
        ],
        cost_estimate=pl.CostEstimate(flops=80_000_000, bytes_accessed=19_000_000, transcendentals=0),
        name="encode",
    )(raw)


NEIGHBOURS = ([(0, 1), (1, 0), (2, 3), (3, 2)], [(0, 3), (3, 0), (1, 2), (2, 1)])


def body(block_pool, sel_index, sel_layer, counts):
    own_count = lax.axis_size("own")
    rep_count = lax.axis_size("rep")
    layers = own_count // SLICES
    tokens, width = block_pool.shape[1:]
    half = width // SLICES
    selection = (block_pool, sel_index, sel_layer, counts)

    upper = layers // 2
    peak = local_peaks(*selection, layers)
    other = lax.ppermute(peak, "rep", NEIGHBOURS[0])
    sent = lay_out(*selection, None, 0, upper, layers)
    peak, sent = lax.optimization_barrier((jnp.maximum(peak, other), sent))
    other = lax.ppermute(peak, "rep", NEIGHBOURS[1])
    sent = lay_out(*selection, sent, upper, layers - upper, layers)
    sent = append(peak, other, sent)
    arrived = lax.all_to_all(sent, "own", split_axis=0, concat_axis=0, tiled=True)

    codes, steps, error = encode(arrived, half)
    for pairs in NEIGHBOURS:
        error = error + lax.ppermute(error, "rep", pairs)
    denominator = float(own_count * rep_count * CAP * tokens)
    return codes[None, None], steps, error / denominator


def solution(mesh):
    return jax.shard_map(
        body,
        mesh=mesh,
        in_specs=(
            P(("own", "rep"), None, None),
            P(("own", "rep")),
            P(("own", "rep")),
            P(("own", "rep")),
        ),
        out_specs=(P("own", "rep", None, None, None), P("own", None), P("own", None)),
        check_vma=False,
    )
```

time: 174 us -> 161 us (0.925)
  Pallas kernels: 44.8 us -> 26.2 us
  waiting for transfers between devices: 0.01 us -> 7.13 us
  starting transfers between devices: 7.91 us -> 3.98 us
  blocking collectives: 116 us -> 118 us
    pallas_call x6 -> x4, Pallas kernels: 41.8 us -> 23.1 us  [the longest x1 11.4 us: encode(): pl.pallas_call(encode_kernel, out_shape=[jax.ShapeDtypeStruct((sources, c...]
    ppermute x4, waiting for transfers between devices: 0.01 us -> 7.13 us  [the longest x2 7.12 us: body(): error = error + lax.ppermute(error, 'rep', pairs)]
    ppermute x4, starting transfers between devices: 7.91 us -> 3.98 us  [the longest x1 1.58 us: body(): other = lax.ppermute(peak, 'rep', NEIGHBOURS[0])]
    all_to_all x1, blocking collectives: 116 us -> 118 us  [body(): lax.all_to_all(sent, 'own', split_axis=0, concat_axis=0, tiled=True)]
  transfers between devices with their start and end apart: 4 -> 4, of which waited for: 0 -> 2; matrix products, arithmetic and copies ran while one was open for 0% -> 0% of each run, Pallas kernels for 16% -> 6%
where the time goes in v5:
time: 161 us; the launch traced here: 159 us
  blocking collectives  118 us (73%)
  Pallas kernels  26.2 us (16%)
  waiting for transfers between devices  7.13 us (4%)
  starting transfers between devices  3.98 us (2%)
    all_to_all x1, blocking collectives, body(): lax.all_to_all(sent, 'own', split_axis=0, concat_axis=0, tiled=True)  118 us
    pallas_call x1, Pallas kernels, encode(): pl.pallas_call(encode_kernel, out_shape=[jax.ShapeDtypeStruct((sources, c...  11.4 us
    pallas_call x2, Pallas kernels, lay_out(): pl.pallas_call(functools.partial(lay_out_kernel, first), out_shape=jax.Sh...  10.2 us
    ppermute x2, waiting for transfers between devices, body(): error = error + lax.ppermute(error, 'rep', pairs)  7.12 us
  transfers between devices with their start and end apart: 4, of which 2 were waited for; matrix products, arithmetic and copies ran while one was open for 0% of the time, Pallas kernels for 6%

profile of v5, /device:TPU:32, one launch (start us, length us, event | category | flops | bytes accessed | tf_op | source)
XLA Modules:
  0.0 159.0 jit_solution(1035866430841135558)
XLA Ops:
  1.3 3.1 %peaks.1 = bf16[32,8,128]{2,1,0:T(8,128)(2,1)} custom-call(s32[32]{0:T(128)} %index_ref.5, s32[32]{0:T(128)} %layer_ref.5, s32[1]{0:T(128)S(6)} %copy.11.count_ref, bf16[64,64,576]{2,1,0:T(8,128)(2,1)} %pool_ref.5), custom_call_target="tpu_custom_call" | custom-call | flops 20000000 | bytes 2500000 | tf_op jit(solution)/shard_map/peaks/pallas_call | solution.py:88
  4.3 0.0 copy-start.1
  4.3 1.6 collective-permute-start
  5.9 5.1 %lay_out.2.refs_0_ = bf16[32,8,18560]{2,1,0:T(8,128)(2,1)} custom-call(s32[32]{0:T(128)} %index_ref.5, s32[32]{0:T(128)} %layer_ref.5, s32[1]{0:T(128)S(6)} %copy.11.count_ref, bf16[64,64,576]{2,1,0:T(8,128)(2,1)} %pool_ref.5), custom_call_target="tpu_custom_call" | custom-call | flops 50000000 | bytes 6000000 | tf_op jit(solution)/shard_map/lay_out/pallas_call | solution.py:207
  11.1 0.0 collective-permute-done
  11.1 0.0 copy-done.1
  11.1 0.0 copy-start
  11.1 0.9 collective-permute-start.1
  12.0 5.1 %lay_out.3._ = bf16[32,8,18560]{2,1,0:T(8,128)(2,1)} custom-call(s32[32]{0:T(128)} %index_ref.5, s32[32]{0:T(128)} %layer_ref.5, s32[1]{0:T(128)S(6)} %copy.11.count_ref, bf16[64,64,576]{2,1,0:T(8,128)(2,1)} %pool_ref.5, bf16[32,8,18560]{2,1,0:T(8,128)(2,1)} %lay_out.2.refs_0_), custom_call_target="tpu_custom_call", output_to_operand_aliasing={{}: (4, {})} | custom-call | flops 50000000 | bytes 6000000 | tf_op jit(solution)/shard_map/lay_out/pallas_call | solution.py:207
  17.1 0.0 copy-done
  17.1 0.0 collective-permute-done.1.other_ref
  17.1 0.0 copy-start.2
  17.1 0.6 copy-done.2
  17.7 1.5 append.1
  19.3 118.4 %all_to_all.5.raw_ref = bf16[32,8,18560]{2,1,0:T(8,128)(2,1)} all-to-all(bf16[32,8,18560]{2,1,0:T(8,128)(2,1)} %append.1), channel_id=1, replica_groups=mesh['own'=32,'rep'=4] {'own'}, dimensions={0} | all-to-all | bytes 19005440 | tf_op jit(solution)/shard_map/all_to_all | solution.py:362
  137.7 11.4 %encode.1 = (bf16[32,8,18432]{2,1,0:T(8,128)(2,1)}, f32[1,288]{1,0:T(1,128)}, f32[1,288]{1,0:T(1,128)}) custom-call(bf16[32,8,18560]{2,1,0:T(8,128)(2,1)} %all_to_all.5.raw_ref), custom_call_target="tpu_custom_call" | custom-call | flops 80000000 | bytes 19000000 | tf_op jit(solution)/shard_map/encode/pallas_call | solution.py:320
  149.1 0.1 collective-permute-start.2
  149.2 3.8 %collective-permute-done.2 = f32[1,288]{1,0:T(1,128)S(1)} collective-permute-done((f32[1,288]{1,0:T(1,128)}, f32[1,288]{1,0:T(1,128)S(1)}, u32[]{:S(2)}, u32[]{:S(2)}) %collective-permute-start.2) | collective-permute-done | bytes 1184 | tf_op jit(solution)/shard_map/ppermute | solution.py:366
  153.0 0.7 add.6
  153.6 1.4 collective-permute-start.3
  155.1 3.3 %collective-permute-done.3 = f32[1,288]{1,0:T(1,128)S(1)} collective-permute-done((f32[1,288]{1,0:T(1,128)S(1)}, f32[1,288]{1,0:T(1,128)S(1)}, u32[]{:S(2)}, u32[]{:S(2)}) %collective-permute-start.3) | collective-permute-done | bytes 1184 | tf_op jit(solution)/shard_map/ppermute | solution.py:366
  158.4 0.6 add_multiply_fusion
  (1 shorter events, 0.0 us)
Async XLA Ops:
  4.3 6.8 %copy-start.1 = (bf16[32,8,128]{2,1,0:T(8,128)(2,1)S(1)}, bf16[32,8,128]{2,1,0:T(8,128)(2,1)}, u32[]{:S(2)}) copy-start(bf16[32,8,128]{2,1,0:T(8,128)(2,1)} %peaks.1) | copy-start | bytes 196612
  4.3 6.7 %collective-permute-start = (bf16[32,8,128]{2,1,0:T(8,128)(2,1)}, bf16[32,8,128]{2,1,0:T(8,128)(2,1)S(1)}, u32[]{:S(2)}, u32[]{:S(2)}) collective-permute-start(bf16[32,8,128]{2,1,0:T(8,128)(2,1)} %peaks.1), channel_id=1, source_target_pairs={{0,1},{1,0},{2,3},{3,2},{4,5},{5,4},{6,7},{7,6},{8,9},{9,8},{10,11... | collective-permute-start | bytes 196616 | tf_op jit(solution)/shard_map/ppermute | solution.py:356
  11.1 6.0 %copy-start = (bf16[32,8,128]{2,1,0:T(8,128)(2,1)}, bf16[32,8,128]{2,1,0:T(8,128)(2,1)S(1)}, u32[]{:S(2)}) copy-start(bf16[32,8,128]{2,1,0:T(8,128)(2,1)S(1)} %max.3.mine_ref) | copy-start | bytes 196612
  11.1 6.0 %collective-permute-start.1 = (bf16[32,8,128]{2,1,0:T(8,128)(2,1)S(1)}, bf16[32,8,128]{2,1,0:T(8,128)(2,1)S(1)}, u32[]{:S(2)}, u32[]{:S(2)}) collective-permute-start(bf16[32,8,128]{2,1,0:T(8,128)(2,1)S(1)} %max.3.mine_ref), channel_id=1, source_target_pairs={{0,3},{3,0},{1,2},{2,1},{4,7},{7,4},{5,6},{6,5},{8,11},{11,8},{9,1... | collective-permute-start | bytes 196616 | tf_op jit(solution)/shard_map/ppermute | solution.py:359
  17.1 0.6 copy-start.2
  149.1 3.9 %collective-permute-start.2 = (f32[1,288]{1,0:T(1,128)}, f32[1,288]{1,0:T(1,128)S(1)}, u32[]{:S(2)}, u32[]{:S(2)}) collective-permute-start(f32[1,288]{1,0:T(1,128)} %get-tuple-element.12), channel_id=1, source_target_pairs={{0,1},{1,0},{2,3},{3,2},{4,5},{5,4},{6,7},{7,6},{8,9},{9,8},{10,11... | collective-permute-start | bytes 3464 | tf_op jit(solution)/shard_map/ppermute | solution.py:366
  153.6 4.8 %collective-permute-start.3 = (f32[1,288]{1,0:T(1,128)S(1)}, f32[1,288]{1,0:T(1,128)S(1)}, u32[]{:S(2)}, u32[]{:S(2)}) collective-permute-start(f32[1,288]{1,0:T(1,128)S(1)} %add.6), channel_id=1, source_target_pairs={{0,3},{3,0},{1,2},{2,1},{4,7},{7,4},{5,6},{6,5},{8,11},{11,8},{9,1... | collective-permute-start | bytes 3464 | tf_op jit(solution)/shard_map/ppermute | solution.py:366

commit v6 on v5

--- a/solution.py
+++ b/solution.py
@@ -101,8 +101,9 @@
     )(sel_index, sel_layer, counts, block_pool)
 
 
-def lay_out_kernel(first, index_ref, layer_ref, count_ref, pool_ref, *refs):
-    out_ref, built, held, spread, slots, filled, dirty, sems, out_sems = refs[-9:]
+def lay_out_kernel(
+    index_ref, layer_ref, count_ref, pool_ref, out_ref, built, held, spread, slots, filled, dirty, sems, out_sems
+):
     live = count_ref[0]
     layers = filled.shape[0]
     tokens, width = held.shape[1:]
@@ -116,9 +117,8 @@
 
     def send(layer):
         here = pl.ds(SLICES * layer, SLICES)
-        there = pl.ds(SLICES * (first + layer), SLICES)
         return pltpu.make_async_copy(
-            built.at[here], out_ref.at[there, :, pl.ds(0, tokens * half)], out_sems.at[layer]
+            built.at[here], out_ref.at[here, :, pl.ds(0, tokens * half)], out_sems.at[layer]
         )
 
     for layer in range(layers):
@@ -126,15 +126,11 @@
     dirty[0] = CAP
 
     def start(j, carry):
-        layer = layer_ref[j] - first
-
-        @pl.when((layer >= 0) & (layer < layers))
-        def _():
-            fetch(j).start()
-            at = filled[layer]
-            slots[layer * CAP + at] = j
-            filled[layer] = at + 1
-
+        fetch(j).start()
+        layer = layer_ref[j]
+        at = filled[layer]
+        slots[layer * CAP + at] = j
+        filled[layer] = at + 1
         return carry
 
     lax.fori_loop(0, live, start, 0)
@@ -178,7 +174,7 @@
                         built[SLICES * layer + h, :, where] = tile.astype(jnp.bfloat16)
                 return carry
 
-            lax.fori_loop(0, tokens // QUAD, four_tokens, 0, unroll=4)
+            lax.fori_loop(0, tokens // QUAD, four_tokens, 0, unroll=tokens // QUAD)
 
         send(layer).start()
         return carry
@@ -192,22 +188,17 @@
     lax.fori_loop(0, layers, finish, 0)
 
 
-def lay_out(block_pool, sel_index, sel_layer, counts, out, first, layers, all_layers):
+def lay_out(block_pool, sel_index, sel_layer, counts, layers):
     n_select = sel_index.shape[0]
     tokens, width = block_pool.shape[1:]
     flat = tokens * (width // SLICES)
     pitch = tokens + 8
     smem = pl.BlockSpec(memory_space=pltpu.SMEM)
     hbm = pl.BlockSpec(memory_space=pl.ANY)
-    specs = [smem, smem, smem, hbm]
-    args = [sel_index, sel_layer, counts, block_pool]
-    if out is not None:
-        specs.append(hbm)
-        args.append(out)
     return pl.pallas_call(
-        functools.partial(lay_out_kernel, first),
-        out_shape=jax.ShapeDtypeStruct((all_layers * SLICES, CAP, flat + LANES), jnp.bfloat16),
-        in_specs=specs,
+        lay_out_kernel,
+        out_shape=jax.ShapeDtypeStruct((layers * SLICES, CAP, flat + LANES), jnp.bfloat16),
+        in_specs=[smem, smem, smem, hbm],
         out_specs=hbm,
         scratch_shapes=[
             pltpu.VMEM((layers * SLICES, CAP, flat), jnp.bfloat16),
@@ -219,35 +210,13 @@
             pltpu.SemaphoreType.DMA((n_select,)),
             pltpu.SemaphoreType.DMA((layers,)),
         ],
-        input_output_aliases={} if out is None else {4: 0},
-        cost_estimate=pl.CostEstimate(flops=50_000_000, bytes_accessed=6_000_000, transcendentals=0),
+        cost_estimate=pl.CostEstimate(flops=200_000_000, bytes_accessed=12_000_000, transcendentals=0),
         name="lay_out",
-    )(*args)
-
-
-def append_kernel(mine_ref, other_ref, _, out_ref, tile, sem):
-    tile[...] = jnp.maximum(mine_ref[...], other_ref[...])
-    lanes = tile.shape[2]
-    copy = pltpu.make_async_copy(tile, out_ref.at[:, :, pl.ds(out_ref.shape[2] - lanes, lanes)], sem)
-    copy.start()
-    copy.wait()
-
-
-def append(mine, other, out):
-    vmem = pl.BlockSpec(memory_space=pltpu.VMEM)
-    hbm = pl.BlockSpec(memory_space=pl.ANY)
-    return pl.pallas_call(
-        append_kernel,
-        out_shape=jax.ShapeDtypeStruct(out.shape, out.dtype),
-        in_specs=[vmem, vmem, hbm],
-        out_specs=hbm,
-        scratch_shapes=[pltpu.VMEM(mine.shape, mine.dtype), pltpu.SemaphoreType.DMA],
-        input_output_aliases={2: 0},
-        name="append",
-    )(mine, other, out)
-
-
-BATCH = 2
+    )(sel_index, sel_layer, counts, block_pool)
+
+
+BATCH = 4
+AHEAD = 3
 
 
 def encode_kernel(raw_ref, codes_ref, steps_ref, error_ref, peaks, raw, codes, inverse, peak_sem, in_sems, out_sems):
@@ -268,7 +237,7 @@
 
     take_peaks = pltpu.make_async_copy(raw_ref.at[:, :, pl.ds(flat, LANES)], peaks, peak_sem)
     take_peaks.start()
-    for b in range(batches):
+    for b in range(AHEAD):
         take(b).start()
     take_peaks.wait()
     peak = jnp.max(peaks[...].astype(jnp.float32), axis=0)
@@ -283,6 +252,11 @@
 
     def batch(b, totals):
         take(b).wait()
+
+        @pl.when(b + AHEAD < batches)
+        def _():
+            take(b + AHEAD).start()
+
 
         def group(u, totals):
             totals = list(totals)
@@ -351,14 +325,11 @@
     half = width // SLICES
     selection = (block_pool, sel_index, sel_layer, counts)
 
-    upper = layers // 2
     peak = local_peaks(*selection, layers)
-    other = lax.ppermute(peak, "rep", NEIGHBOURS[0])
-    sent = lay_out(*selection, None, 0, upper, layers)
-    peak, sent = lax.optimization_barrier((jnp.maximum(peak, other), sent))
-    other = lax.ppermute(peak, "rep", NEIGHBOURS[1])
-    sent = lay_out(*selection, sent, upper, layers - upper, layers)
-    sent = append(peak, other, sent)
+    others = [lax.ppermute(peak, "rep", [(r, (r + k) % rep_count) for r in range(rep_count)]) for k in range(1, rep_count)]
+    sent = lay_out(*selection, layers)
+    peak = functools.reduce(jnp.maximum, others, peak)
+    sent = lax.dynamic_update_slice(sent, peak, (0, 0, tokens * half))
     arrived = lax.all_to_all(sent, "own", split_axis=0, concat_axis=0, tiled=True)
 
     codes, steps, error = encode(arrived, half)

time: 161 us -> 154 us (0.957)
  Pallas kernels: 26.2 us -> 18.9 us
  starting transfers between devices: 3.98 us -> 9.93 us
  waiting for transfers between devices: 7.13 us -> 4.68 us
  blocking collectives: 118 us -> 116 us
    pallas_call x3 -> x1, Pallas kernels: 11.8 us -> 6.51 us  [lay_out(): pl.pallas_call(lay_out_kernel, out_shape=jax.ShapeDtypeStruct((layers * S...]
    ppermute x2, starting transfers between devices: 1.53 us -> 5.33 us  [body(): error = error + lax.ppermute(error, 'rep', pairs)]
    all_to_all x1, blocking collectives: 118 us -> 116 us  [body(): lax.all_to_all(sent, 'own', split_axis=0, concat_axis=0, tiled=True)]
    ppermute x2, waiting for transfers between devices: 7.12 us -> 4.67 us  [body(): error = error + lax.ppermute(error, 'rep', pairs)]
    ppermute x2 -> x3, starting transfers between devices: 2.45 us -> 4.6 us  [body(): lax.ppermute(peak, 'rep', [(r, (r + k) % rep_count) for r in range(rep_co...]
    pallas_call x1, Pallas kernels: 11.4 us -> 9.32 us  [encode(): pl.pallas_call(encode_kernel, out_shape=[jax.ShapeDtypeStruct((sources, c...]
  transfers between devices with their start and end apart: 4 -> 5, of which waited for: 2 -> 2; matrix products, arithmetic and copies ran while one was open for 0% -> 0% of each run, Pallas kernels for 6% -> 4%
where the time goes in v6:
time: 154 us; the launch traced here: 153 us
  blocking collectives  116 us (75%)
  Pallas kernels  18.9 us (12%)
  starting transfers between devices  9.93 us (6%)
  waiting for transfers between devices  4.68 us (3%)
  other arithmetic  1.97 us (1%)
    all_to_all x1, blocking collectives, body(): lax.all_to_all(sent, 'own', split_axis=0, concat_axis=0, tiled=True)  116 us
    pallas_call x1, Pallas kernels, encode(): pl.pallas_call(encode_kernel, out_shape=[jax.ShapeDtypeStruct((sources, c...  9.32 us
    pallas_call x1, Pallas kernels, lay_out(): pl.pallas_call(lay_out_kernel, out_shape=jax.ShapeDtypeStruct((layers * S...  6.51 us
    ppermute x2, starting transfers between devices, body(): error = error + lax.ppermute(error, 'rep', pairs)  5.33 us
    ppermute x2, waiting for transfers between devices, body(): error = error + lax.ppermute(error, 'rep', pairs)  4.67 us
    ppermute x3, starting transfers between devices, body(): lax.ppermute(peak, 'rep', [(r, (r + k) % rep_count) for r in range(rep_co...  4.6 us
  transfers between devices with their start and end apart: 5, of which 2 were waited for; matrix products, arithmetic and copies ran while one was open for 0% of the time, Pallas kernels for 4%

profile of v6, /device:TPU:32, one launch (start us, length us, event | category | flops | bytes accessed | tf_op | source)
XLA Modules:
  0.0 152.7 jit_solution(9627883793210772451)
XLA Ops:
  1.3 3.1 %peaks.1 = bf16[32,8,128]{2,1,0:T(8,128)(2,1)} custom-call(s32[32]{0:T(128)} %index_ref.3, s32[32]{0:T(128)} %layer_ref.3, s32[1]{0:T(128)S(6)} %copy.8.count_ref, bf16[64,64,576]{2,1,0:T(8,128)(2,1)} %pool_ref.3), custom_call_target="tpu_custom_call" | custom-call | flops 20000000 | bytes 2500000 | tf_op jit(solution)/shard_map/peaks/pallas_call | solution.py:88
  4.4 0.0 copy-start
  4.4 3.0 %collective-permute-start.2 = (bf16[32,8,128]{2,1,0:T(8,128)(2,1)}, bf16[32,8,128]{2,1,0:T(8,128)(2,1)S(1)}, u32[]{:S(2)}, u32[]{:S(2)}) collective-permute-start(bf16[32,8,128]{2,1,0:T(8,128)(2,1)} %peaks.1), channel_id=1, source_target_pairs={{0,3},{1,0},{2,1},{3,2},{4,7},{5,4},{6,5},{7,6},{8,11},{9,8},{10,9... | collective-permute-start | bytes 196616 | tf_op jit(solution)/shard_map/ppermute | solution.py:329
  7.4 0.6 collective-permute-start.1
  8.0 1.0 collective-permute-start
  9.0 6.5 %lay_out.1 = bf16[32,8,18560]{2,1,0:T(8,128)(2,1)} custom-call(s32[32]{0:T(128)} %index_ref.3, s32[32]{0:T(128)} %layer_ref.3, s32[1]{0:T(128)S(6)} %copy.8.count_ref, bf16[64,64,576]{2,1,0:T(8,128)(2,1)} %pool_ref.3), custom_call_target="tpu_custom_call" | custom-call | flops 200000000 | bytes 12000000 | tf_op jit(solution)/shard_map/lay_out/pallas_call | solution.py:198
  15.5 0.0 collective-permute-done.2
  15.5 0.0 collective-permute-done.1
  15.5 0.0 collective-permute-done
  15.5 0.0 copy-done
  15.5 0.7 maximum_dynamic-update-slice_fusion
  16.3 115.9 %all_to_all.5.raw_ref = bf16[32,8,18560]{2,1,0:T(8,128)(2,1)} all-to-all(bf16[32,8,18560]{2,1,0:T(8,128)(2,1)} %maximum_dynamic-update-slice_fusion), channel_id=1, replica_groups=mesh['own'=32,'rep'=4] {'own'}, dimensions={0} | all-to-all | bytes 19005440 | tf_op jit(solution)/shard_map/all_to_all | solution.py:333
  132.2 9.3 %encode.1 = (bf16[32,8,18432]{2,1,0:T(8,128)(2,1)}, f32[1,288]{1,0:T(1,128)}, f32[1,288]{1,0:T(1,128)}) custom-call(bf16[32,8,18560]{2,1,0:T(8,128)(2,1)} %all_to_all.5.raw_ref), custom_call_target="tpu_custom_call" | custom-call | flops 80000000 | bytes 19000000 | tf_op jit(solution)/shard_map/encode/pallas_call | solution.py:294
  141.5 3.4 %collective-permute-start.3 = (f32[1,288]{1,0:T(1,128)}, f32[1,288]{1,0:T(1,128)S(1)}, u32[]{:S(2)}, u32[]{:S(2)}) collective-permute-start(f32[1,288]{1,0:T(1,128)} %get-tuple-element.8), channel_id=1, source_target_pairs={{0,1},{1,0},{2,3},{3,2},{4,5},{5,4},{6,7},{7,6},{8,9},{9,8},{10,11... | collective-permute-start | bytes 3464 | tf_op jit(solution)/shard_map/ppermute | solution.py:337
  144.9 1.8 %collective-permute-done.3 = f32[1,288]{1,0:T(1,128)S(1)} collective-permute-done((f32[1,288]{1,0:T(1,128)}, f32[1,288]{1,0:T(1,128)S(1)}, u32[]{:S(2)}, u32[]{:S(2)}) %collective-permute-start.3) | collective-permute-done | bytes 1184 | tf_op jit(solution)/shard_map/ppermute | solution.py:337
  146.7 0.7 add.6
  147.4 1.9 %collective-permute-start.4 = (f32[1,288]{1,0:T(1,128)S(1)}, f32[1,288]{1,0:T(1,128)S(1)}, u32[]{:S(2)}, u32[]{:S(2)}) collective-permute-start(f32[1,288]{1,0:T(1,128)S(1)} %add.6), channel_id=1, source_target_pairs={{0,3},{3,0},{1,2},{2,1},{4,7},{7,4},{5,6},{6,5},{8,11},{11,8},{9,1... | collective-permute-start | bytes 3464 | tf_op jit(solution)/shard_map/ppermute | solution.py:337
  149.3 2.9 %collective-permute-done.4 = f32[1,288]{1,0:T(1,128)S(1)} collective-permute-done((f32[1,288]{1,0:T(1,128)S(1)}, f32[1,288]{1,0:T(1,128)S(1)}, u32[]{:S(2)}, u32[]{:S(2)}) %collective-permute-start.4) | collective-permute-done | bytes 1184 | tf_op jit(solution)/shard_map/ppermute | solution.py:337
  152.2 0.6 add_multiply_fusion
Async XLA Ops:
  4.4 11.2 %copy-start = (bf16[32,8,128]{2,1,0:T(8,128)(2,1)S(1)}, bf16[32,8,128]{2,1,0:T(8,128)(2,1)}, u32[]{:S(2)}) copy-start(bf16[32,8,128]{2,1,0:T(8,128)(2,1)} %peaks.1) | copy-start | bytes 196612
  4.4 11.1 %collective-permute-start.2 = (bf16[32,8,128]{2,1,0:T(8,128)(2,1)}, bf16[32,8,128]{2,1,0:T(8,128)(2,1)S(1)}, u32[]{:S(2)}, u32[]{:S(2)}) collective-permute-start(bf16[32,8,128]{2,1,0:T(8,128)(2,1)} %peaks.1), channel_id=1, source_target_pairs={{0,3},{1,0},{2,1},{3,2},{4,7},{5,4},{6,5},{7,6},{8,11},{9,8},{10,9... | collective-permute-start | bytes 196616 | tf_op jit(solution)/shard_map/ppermute | solution.py:329
  7.4 8.1 %collective-permute-start.1 = (bf16[32,8,128]{2,1,0:T(8,128)(2,1)}, bf16[32,8,128]{2,1,0:T(8,128)(2,1)S(1)}, u32[]{:S(2)}, u32[]{:S(2)}) collective-permute-start(bf16[32,8,128]{2,1,0:T(8,128)(2,1)} %peaks.1), channel_id=1, source_target_pairs={{0,2},{1,3},{2,0},{3,1},{4,6},{5,7},{6,4},{7,5},{8,10},{9,11},{10,... | collective-permute-start | bytes 196616 | tf_op jit(solution)/shard_map/ppermute | solution.py:329
  8.0 7.5 %collective-permute-start = (bf16[32,8,128]{2,1,0:T(8,128)(2,1)}, bf16[32,8,128]{2,1,0:T(8,128)(2,1)S(1)}, u32[]{:S(2)}, u32[]{:S(2)}) collective-permute-start(bf16[32,8,128]{2,1,0:T(8,128)(2,1)} %peaks.1), channel_id=1, source_target_pairs={{0,1},{1,2},{2,3},{3,0},{4,5},{5,6},{6,7},{7,4},{8,9},{9,10},{10,1... | collective-permute-start | bytes 196616 | tf_op jit(solution)/shard_map/ppermute | solution.py:329
  141.5 5.2 %collective-permute-start.3 = (f32[1,288]{1,0:T(1,128)}, f32[1,288]{1,0:T(1,128)S(1)}, u32[]{:S(2)}, u32[]{:S(2)}) collective-permute-start(f32[1,288]{1,0:T(1,128)} %get-tuple-element.8), channel_id=1, source_target_pairs={{0,1},{1,0},{2,3},{3,2},{4,5},{5,4},{6,7},{7,6},{8,9},{9,8},{10,11... | collective-permute-start | bytes 3464 | tf_op jit(solution)/shard_map/ppermute | solution.py:337
  147.4 4.8 %collective-permute-start.4 = (f32[1,288]{1,0:T(1,128)S(1)}, f32[1,288]{1,0:T(1,128)S(1)}, u32[]{:S(2)}, u32[]{:S(2)}) collective-permute-start(f32[1,288]{1,0:T(1,128)S(1)} %add.6), channel_id=1, source_target_pairs={{0,3},{3,0},{1,2},{2,1},{4,7},{7,4},{5,6},{6,5},{8,11},{11,8},{9,1... | collective-permute-start | bytes 3464 | tf_op jit(solution)/shard_map/ppermute | solution.py:337

commit v7 on v6

--- a/solution.py
+++ b/solution.py
@@ -11,6 +11,7 @@
 LANES = 128
 QUAD = 4
 headroom = 0.5
+VMEM_LIMIT = 30 * 2**20
 
 
 def end_to_end(rows, width, start):
@@ -34,7 +35,7 @@
     return out
 
 
-def peak_kernel(index_ref, layer_ref, count_ref, pool_ref, out_ref, held, acc, top, sems):
+def peak_kernel(index_ref, layer_ref, count_ref, pool_ref, out_ref, held, slots, filled, acc, top, sems):
     live = count_ref[0]
     tokens, width = held.shape[1:]
     layers = acc.shape[0]
@@ -44,8 +45,15 @@
     def fetch(j):
         return pltpu.make_async_copy(pool_ref.at[index_ref[j]], held.at[j], sems.at[j])
 
+    for layer in range(layers):
+        filled[layer] = 0
+
     def start(j, carry):
         fetch(j).start()
+        layer = layer_ref[j]
+        at = filled[layer]
+        slots[layer * CAP + at] = j
+        filled[layer] = at + 1
         return carry
 
     lax.fori_loop(0, live, start, 0)
@@ -85,69 +93,50 @@
     tokens, width = block_pool.shape[1:]
     pieces = pl.cdiv(width // SLICES, LANES)
     smem = pl.BlockSpec(memory_space=pltpu.SMEM)
+    vmem = pl.BlockSpec(memory_space=pltpu.VMEM)
     return pl.pallas_call(
         peak_kernel,
-        out_shape=jax.ShapeDtypeStruct((layers * SLICES, CAP, LANES), jnp.bfloat16),
-        in_specs=[smem, smem, smem, pl.BlockSpec(memory_space=pl.ANY)],
-        out_specs=pl.BlockSpec(memory_space=pltpu.VMEM),
+        out_shape=[
+            pltpu.VMEM((layers * SLICES, CAP, LANES), jnp.bfloat16),
+            pltpu.VMEM((n_select, tokens, width), jnp.bfloat16),
+            pltpu.SMEM((layers * CAP,), jnp.int32),
+            pltpu.SMEM((layers,), jnp.int32),
+        ],
+        in_specs=[smem, smem, smem, pl.BlockSpec(memory_space=pltpu.HBM)],
+        out_specs=[vmem, vmem, smem, smem],
         scratch_shapes=[
-            pltpu.VMEM((n_select, tokens, width), jnp.bfloat16),
             pltpu.VMEM((layers, 8, width), jnp.float32),
             pltpu.VMEM((SLICES * pieces, layers, LANES), jnp.float32),
             pltpu.SemaphoreType.DMA((n_select,)),
         ],
+        compiler_params=pltpu.CompilerParams(vmem_limit_bytes=2 * VMEM_LIMIT),
         cost_estimate=pl.CostEstimate(flops=20_000_000, bytes_accessed=2_500_000, transcendentals=0),
         name="peaks",
     )(sel_index, sel_layer, counts, block_pool)
 
 
-def lay_out_kernel(
-    index_ref, layer_ref, count_ref, pool_ref, out_ref, built, held, spread, slots, filled, dirty, sems, out_sems
-):
-    live = count_ref[0]
+def lay_out_kernel(slots, filled, held, built, spread, dirty):
     layers = filled.shape[0]
     tokens, width = held.shape[1:]
     half = width // SLICES
     tiles = spread.shape[0]
     pitch = spread.shape[1] // CAP
     group = QUAD * half
-
-    def fetch(j):
-        return pltpu.make_async_copy(pool_ref.at[index_ref[j]], held.at[j], sems.at[j])
-
-    def send(layer):
-        here = pl.ds(SLICES * layer, SLICES)
-        return pltpu.make_async_copy(
-            built.at[here], out_ref.at[here, :, pl.ds(0, tokens * half)], out_sems.at[layer]
-        )
-
-    for layer in range(layers):
-        filled[layer] = 0
     dirty[0] = CAP
-
-    def start(j, carry):
-        fetch(j).start()
-        layer = layer_ref[j]
-        at = filled[layer]
-        slots[layer * CAP + at] = j
-        filled[layer] = at + 1
-        return carry
-
-    lax.fori_loop(0, live, start, 0)
 
     def build(layer, carry):
         held_slots = filled[layer]
 
         @pl.when(held_slots == 0)
         def _():
-            built[pl.ds(SLICES * layer, SLICES)] = jnp.zeros((SLICES, *built.shape[1:]), built.dtype)
+            built[pl.ds(SLICES * layer, SLICES), :, : tokens * half] = jnp.zeros(
+                (SLICES, CAP, tokens * half), built.dtype
+            )
 
         @pl.when(held_slots > 0)
         def _():
             def place(c, carry):
-                j = slots[layer * CAP + c]
-                fetch(j).wait()
-                values = held[j].astype(jnp.float32)
+                values = held[slots[layer * CAP + c]].astype(jnp.float32)
                 rows = pl.ds(pl.multiple_of(c * pitch, 8), tokens)
                 for i in range(tiles):
                     lanes = min(LANES, width - i * LANES)
@@ -176,71 +165,48 @@
 
             lax.fori_loop(0, tokens // QUAD, four_tokens, 0, unroll=tokens // QUAD)
 
-        send(layer).start()
         return carry
 
     lax.fori_loop(0, layers, build, 0)
 
-    def finish(layer, carry):
-        send(layer).wait()
-        return carry
-
-    lax.fori_loop(0, layers, finish, 0)
-
-
-def lay_out(block_pool, sel_index, sel_layer, counts, layers):
-    n_select = sel_index.shape[0]
-    tokens, width = block_pool.shape[1:]
+
+def lay_out(held, slots, filled):
+    layers = filled.shape[0]
+    _, tokens, width = held.shape
     flat = tokens * (width // SLICES)
     pitch = tokens + 8
     smem = pl.BlockSpec(memory_space=pltpu.SMEM)
-    hbm = pl.BlockSpec(memory_space=pl.ANY)
+    vmem = pl.BlockSpec(memory_space=pltpu.VMEM)
     return pl.pallas_call(
         lay_out_kernel,
-        out_shape=jax.ShapeDtypeStruct((layers * SLICES, CAP, flat + LANES), jnp.bfloat16),
-        in_specs=[smem, smem, smem, hbm],
-        out_specs=hbm,
+        out_shape=pltpu.VMEM((layers * SLICES, CAP, flat + LANES), jnp.bfloat16),
+        in_specs=[smem, smem, vmem],
+        out_specs=vmem,
         scratch_shapes=[
-            pltpu.VMEM((layers * SLICES, CAP, flat), jnp.bfloat16),
-            pltpu.VMEM((n_select, tokens, width), jnp.bfloat16),
             pltpu.VMEM((pl.cdiv(width, LANES), CAP * pitch, LANES), jnp.float32),
-            pltpu.SMEM((layers * CAP,), jnp.int32),
-            pltpu.SMEM((layers,), jnp.int32),
             pltpu.SMEM((1,), jnp.int32),
-            pltpu.SemaphoreType.DMA((n_select,)),
-            pltpu.SemaphoreType.DMA((layers,)),
-        ],
+        ],
+        compiler_params=pltpu.CompilerParams(vmem_limit_bytes=VMEM_LIMIT),
         cost_estimate=pl.CostEstimate(flops=200_000_000, bytes_accessed=12_000_000, transcendentals=0),
         name="lay_out",
-    )(sel_index, sel_layer, counts, block_pool)
-
-
-BATCH = 4
-AHEAD = 3
-
-
-def encode_kernel(raw_ref, codes_ref, steps_ref, error_ref, peaks, raw, codes, inverse, peak_sem, in_sems, out_sems):
-    sources, cap, _ = raw.shape
+    )(slots, filled, held)
+
+
+BATCH = 2
+
+
+def encode_kernel(raw_ref, codes_ref, steps_ref, error_ref, codes, inverse, out_sems):
+    sources, cap, flat = codes.shape
     lanes = inverse.shape[1]
     half = lanes // QUAD
     tiles = lanes // LANES
-    flat = codes.shape[2]
     batches = sources // BATCH
-
-    def take(b):
-        here = pl.ds(b * BATCH, BATCH)
-        return pltpu.make_async_copy(raw_ref.at[here, :, pl.ds(0, flat)], raw.at[here], in_sems.at[b])
 
     def give(b):
         here = pl.ds(b * BATCH, BATCH)
         return pltpu.make_async_copy(codes.at[here], codes_ref.at[here], out_sems.at[b])
 
-    take_peaks = pltpu.make_async_copy(raw_ref.at[:, :, pl.ds(flat, LANES)], peaks, peak_sem)
-    take_peaks.start()
-    for b in range(AHEAD):
-        take(b).start()
-    take_peaks.wait()
-    peak = jnp.max(peaks[...].astype(jnp.float32), axis=0)
+    peak = jnp.max(raw_ref[:, :, flat:].astype(jnp.float32), axis=0)
     scale = headroom * jnp.maximum(peak, 1.0) / 127.0
     rows = [jnp.broadcast_to(scale[n : n + 1], (cap, LANES)) for n in range(pl.cdiv(half, LANES))]
     for n, row in enumerate(rows):
@@ -251,19 +217,12 @@
     by_lane = [inverse[:, i * LANES : (i + 1) * LANES] for i in range(tiles)]
 
     def batch(b, totals):
-        take(b).wait()
-
-        @pl.when(b + AHEAD < batches)
-        def _():
-            take(b + AHEAD).start()
-
-
         def group(u, totals):
             totals = list(totals)
             for i in range(tiles):
                 at = pl.ds(pl.multiple_of(u * lanes + i * LANES, LANES), LANES)
                 for s in range(BATCH):
-                    exact = raw[b * BATCH + s, :, at].astype(jnp.float32) * by_lane[i]
+                    exact = raw_ref[b * BATCH + s, :, at].astype(jnp.float32) * by_lane[i]
                     coded = jnp.clip(exact, -127.0, 127.0).astype(jnp.bfloat16)
                     codes[b * BATCH + s, :, at] = coded
                     miss = exact - coded.astype(jnp.float32)
@@ -290,25 +249,21 @@
     sources, cap, size = raw.shape
     flat = size - LANES
     vmem = pl.BlockSpec(memory_space=pltpu.VMEM)
-    hbm = pl.BlockSpec(memory_space=pl.ANY)
     return pl.pallas_call(
         encode_kernel,
         out_shape=[
             jax.ShapeDtypeStruct((sources, cap, flat), jnp.bfloat16),
             jax.ShapeDtypeStruct((1, half), jnp.float32),
-            jax.ShapeDtypeStruct((1, half), jnp.float32),
-        ],
-        in_specs=[hbm],
-        out_specs=[hbm, vmem, vmem],
+            pltpu.VMEM((1, half), jnp.float32),
+        ],
+        in_specs=[vmem],
+        out_specs=[pl.BlockSpec(memory_space=pltpu.HBM), vmem, vmem],
         scratch_shapes=[
-            pltpu.VMEM((sources, cap, LANES), jnp.bfloat16),
-            pltpu.VMEM((sources, cap, flat), jnp.bfloat16),
             pltpu.VMEM((sources, cap, flat), jnp.bfloat16),
             pltpu.VMEM((cap, QUAD * half), jnp.float32),
-            pltpu.SemaphoreType.DMA,
             pltpu.SemaphoreType.DMA((sources // BATCH,)),
-            pltpu.SemaphoreType.DMA((sources // BATCH,)),
-        ],
+        ],
+        compiler_params=pltpu.CompilerParams(vmem_limit_bytes=VMEM_LIMIT),
         cost_estimate=pl.CostEstimate(flops=80_000_000, bytes_accessed=19_000_000, transcendentals=0),
         name="encode",
     )(raw)
@@ -323,11 +278,9 @@
     layers = own_count // SLICES
     tokens, width = block_pool.shape[1:]
     half = width // SLICES
-    selection = (block_pool, sel_index, sel_layer, counts)
-
-    peak = local_peaks(*selection, layers)
+    peak, *found = local_peaks(block_pool, sel_index, sel_layer, counts, layers)
     others = [lax.ppermute(peak, "rep", [(r, (r + k) % rep_count) for r in range(rep_count)]) for k in range(1, rep_count)]
-    sent = lay_out(*selection, layers)
+    sent = lay_out(*found)
     peak = functools.reduce(jnp.maximum, others, peak)
     sent = lax.dynamic_update_slice(sent, peak, (0, 0, tokens * half))
     arrived = lax.all_to_all(sent, "own", split_axis=0, concat_axis=0, tiled=True)

time: 154 us -> 147 us (0.955)
  Pallas kernels: 18.9 us -> 13.3 us
  waiting for transfers between devices: 4.68 us -> 10.1 us
  starting transfers between devices: 9.93 us -> 5.37 us
    ppermute x2, starting transfers between devices: 5.33 us -> 0.77 us  [body(): error = error + lax.ppermute(error, 'rep', pairs)]
    pallas_call x2, Pallas kernels: 9.59 us -> 5.1 us  [the longest x1 2.6 us: lay_out(): pl.pallas_call(lay_out_kernel, out_shape=pltpu.VMEM((layers * SLICES, CAP...]
    ppermute x2, waiting for transfers between devices: 4.67 us -> 7.68 us  [body(): error = error + lax.ppermute(error, 'rep', pairs)]
    ppermute x3, waiting for transfers between devices: 0.01 us -> 2.38 us  [body(): lax.ppermute(peak, 'rep', [(r, (r + k) % rep_count) for r in range(rep_co...]
  transfers between devices with their start and end apart: 5 -> 5, of which waited for: 2 -> 4; matrix products, arithmetic and copies ran while one was open for 0% -> 0% of each run, Pallas kernels for 4% -> 2%
where the time goes in v7:
time: 147 us; the launch traced here: 146 us
  blocking collectives  115 us (78%)
  Pallas kernels  13.3 us (9%)
  waiting for transfers between devices  10.1 us (7%)
  starting transfers between devices  5.37 us (4%)
    all_to_all x1, blocking collectives, body(): lax.all_to_all(sent, 'own', split_axis=0, concat_axis=0, tiled=True)  115 us
    pallas_call x1, Pallas kernels, encode(): pl.pallas_call(encode_kernel, out_shape=[jax.ShapeDtypeStruct((sources, c...  8.23 us
    ppermute x2, waiting for transfers between devices, body(): error = error + lax.ppermute(error, 'rep', pairs)  7.68 us
    ppermute x3, starting transfers between devices, body(): lax.ppermute(peak, 'rep', [(r, (r + k) % rep_count) for r in range(rep_co...  4.6 us
  transfers between devices with their start and end apart: 5, of which 4 were waited for; matrix products, arithmetic and copies ran while one was open for 0% of the time, Pallas kernels for 2%

profile of v7, /device:TPU:32, one launch (start us, length us, event | category | flops | bytes accessed | tf_op | source)
XLA Modules:
  0.0 145.6 jit_solution(17870717963232852425)
XLA Ops:
  1.3 2.5 %peaks.1 = (bf16[32,8,128]{2,1,0:T(8,128)(2,1)S(1)}, bf16[32,64,576]{2,1,0:T(8,128)(2,1)S(1)}, s32[128]{0:T(128)S(4)}, s32[16]{0:T(128)S(4)}) custom-call(s32[32]{0:T(128)} %index_ref.1, s32[32]{0:T(128)} %layer_ref.1, s32[1]{0:T(128)S(6)} %copy.8.count_ref, bf16[64,64,576]{2,1,0:T(8,128)(2,1)} %pool_ref.1), custom_call_target="tpu_custom_call" | custom-call | flops 20000000 | bytes 2500000 | tf_op jit(solution)/shard_map/peaks/pallas_call | solution.py:97
  3.8 3.0 %collective-permute-start.2 = (bf16[32,8,128]{2,1,0:T(8,128)(2,1)S(1)}, bf16[32,8,128]{2,1,0:T(8,128)(2,1)S(1)}, u32[]{:S(2)}, u32[]{:S(2)}) collective-permute-start(bf16[32,8,128]{2,1,0:T(8,128)(2,1)S(1)} %get-tuple-element.13), channel_id=1, source_target_pairs={{0,3},{1,0},{2,1},{3,2},{4,7},{5,4},{6,5},{7,6},{8,11},{9,8},{10,9... | collective-permute-start | bytes 196616 | tf_op jit(solution)/shard_map/ppermute | solution.py:282
  6.8 0.7 collective-permute-start.1
  7.5 0.9 collective-permute-start
  8.4 2.6 %lay_out.1 = bf16[32,8,18560]{2,1,0:T(8,128)(2,1)S(1)} custom-call(s32[128]{0:T(128)S(4)} %get-tuple-element.10.slots, s32[16]{0:T(128)S(4)} %get-tuple-element.11.filled, bf16[32,64,576]{2,1,0:T(8,128)(2,1)S(1)} %get-tuple-element.12.held), custom_call_target="tpu_custom_call" | custom-call | flops 200000000 | bytes 12000000 | tf_op jit(solution)/shard_map/lay_out/pallas_call | solution.py:180
  11.0 0.0 collective-permute-done.2
  11.0 1.7 %collective-permute-done.1 = bf16[32,8,128]{2,1,0:T(8,128)(2,1)S(1)} collective-permute-done((bf16[32,8,128]{2,1,0:T(8,128)(2,1)S(1)}, bf16[32,8,128]{2,1,0:T(8,128)(2,1)S(1)}, u32[]{:S(2)}, u32[]{:S(2)}) %collective-permute-start.1) | collective-permute-done | bytes 65568 | tf_op jit(solution)/shard_map/ppermute | solution.py:282
  12.7 0.7 collective-permute-done
  13.4 0.1 maximum_dynamic-update-slice_fusion
  13.4 114.9 %all_to_all.5.raw_ref = bf16[32,8,18560]{2,1,0:T(8,128)(2,1)S(1)} all-to-all(bf16[32,8,18560]{2,1,0:T(8,128)(2,1)S(1)} %maximum_dynamic-update-slice_fusion), channel_id=1, replica_groups=mesh['own'=32,'rep'=4] {'own'}, dimensions={0} | all-to-all | bytes 19005440 | tf_op jit(solution)/shard_map/all_to_all | solution.py:286
  128.3 8.2 %encode.1 = (bf16[32,8,18432]{2,1,0:T(8,128)(2,1)}, f32[1,288]{1,0:T(1,128)}, f32[1,288]{1,0:T(1,128)S(1)}) custom-call(bf16[32,8,18560]{2,1,0:T(8,128)(2,1)S(1)} %all_to_all.5.raw_ref), custom_call_target="tpu_custom_call" | custom-call | flops 80000000 | bytes 19000000 | tf_op jit(solution)/shard_map/encode/pallas_call | solution.py:252
  136.6 0.1 collective-permute-start.3
  136.7 3.6 %collective-permute-done.3 = f32[1,288]{1,0:T(1,128)S(1)} collective-permute-done((f32[1,288]{1,0:T(1,128)S(1)}, f32[1,288]{1,0:T(1,128)S(1)}, u32[]{:S(2)}, u32[]{:S(2)}) %collective-permute-start.3) | collective-permute-done | bytes 1184 | tf_op jit(solution)/shard_map/ppermute | solution.py:290
  140.2 0.7 collective-permute-start.4
  140.9 4.1 %collective-permute-done.4 = f32[1,288]{1,0:T(1,128)S(1)} collective-permute-done((f32[1,288]{1,0:T(1,128)S(1)}, f32[1,288]{1,0:T(1,128)S(1)}, u32[]{:S(2)}, u32[]{:S(2)}) %collective-permute-start.4) | collective-permute-done | bytes 1184 | tf_op jit(solution)/shard_map/ppermute | solution.py:290
  145.0 0.6 add_multiply_fusion
  (1 shorter events, 0.0 us)
Async XLA Ops:
  3.8 7.2 %collective-permute-start.2 = (bf16[32,8,128]{2,1,0:T(8,128)(2,1)S(1)}, bf16[32,8,128]{2,1,0:T(8,128)(2,1)S(1)}, u32[]{:S(2)}, u32[]{:S(2)}) collective-permute-start(bf16[32,8,128]{2,1,0:T(8,128)(2,1)S(1)} %get-tuple-element.13), channel_id=1, source_target_pairs={{0,3},{1,0},{2,1},{3,2},{4,7},{5,4},{6,5},{7,6},{8,11},{9,8},{10,9... | collective-permute-start | bytes 196616 | tf_op jit(solution)/shard_map/ppermute | solution.py:282
  6.8 5.9 %collective-permute-start.1 = (bf16[32,8,128]{2,1,0:T(8,128)(2,1)S(1)}, bf16[32,8,128]{2,1,0:T(8,128)(2,1)S(1)}, u32[]{:S(2)}, u32[]{:S(2)}) collective-permute-start(bf16[32,8,128]{2,1,0:T(8,128)(2,1)S(1)} %get-tuple-element.13), channel_id=1, source_target_pairs={{0,2},{1,3},{2,0},{3,1},{4,6},{5,7},{6,4},{7,5},{8,10},{9,11},{10,... | collective-permute-start | bytes 196616 | tf_op jit(solution)/shard_map/ppermute | solution.py:282
  7.5 5.9 %collective-permute-start = (bf16[32,8,128]{2,1,0:T(8,128)(2,1)S(1)}, bf16[32,8,128]{2,1,0:T(8,128)(2,1)S(1)}, u32[]{:S(2)}, u32[]{:S(2)}) collective-permute-start(bf16[32,8,128]{2,1,0:T(8,128)(2,1)S(1)} %get-tuple-element.13), channel_id=1, source_target_pairs={{0,1},{1,2},{2,3},{3,0},{4,5},{5,6},{6,7},{7,4},{8,9},{9,10},{10,1... | collective-permute-start | bytes 196616 | tf_op jit(solution)/shard_map/ppermute | solution.py:282
  136.6 3.7 %collective-permute-start.3 = (f32[1,288]{1,0:T(1,128)S(1)}, f32[1,288]{1,0:T(1,128)S(1)}, u32[]{:S(2)}, u32[]{:S(2)}) collective-permute-start(f32[1,288]{1,0:T(1,128)S(1)} %get-tuple-element.16), channel_id=1, source_target_pairs={{0,1},{1,0},{2,3},{3,2},{4,5},{5,4},{6,7},{7,6},{8,9},{9,8},{10,11... | collective-permute-start | bytes 3464 | tf_op jit(solution)/shard_map/ppermute | solution.py:290
  140.2 4.8 %collective-permute-start.4 = (f32[1,288]{1,0:T(1,128)S(1)}, f32[1,288]{1,0:T(1,128)S(1)}, u32[]{:S(2)}, u32[]{:S(2)}) collective-permute-start(f32[1,288]{1,0:T(1,128)S(1)} %add.6), channel_id=1, source_target_pairs={{0,3},{3,0},{1,2},{2,1},{4,7},{7,4},{5,6},{6,5},{8,11},{11,8},{9,1... | collective-permute-start | bytes 3464 | tf_op jit(solution)/shard_map/ppermute | solution.py:290

commit v8 on v7

--- a/solution.py
+++ b/solution.py
@@ -120,7 +120,7 @@
     tokens, width = held.shape[1:]
     half = width // SLICES
     tiles = spread.shape[0]
-    pitch = spread.shape[1] // CAP
+    pitch = spread.shape[1] // (CAP + 1)
     group = QUAD * half
     dirty[0] = CAP
 
@@ -137,7 +137,7 @@
         def _():
             def place(c, carry):
                 values = held[slots[layer * CAP + c]].astype(jnp.float32)
-                rows = pl.ds(pl.multiple_of(c * pitch, 8), tokens)
+                rows = pl.ds(c * pitch, tokens)
                 for i in range(tiles):
                     lanes = min(LANES, width - i * LANES)
                     spread[i, rows, :lanes] = values[:, i * LANES : i * LANES + lanes]
@@ -147,7 +147,7 @@
 
             def blank(c, carry):
                 for i in range(tiles):
-                    spread[i, pl.ds(pl.multiple_of(c * pitch, 8), tokens), :] = jnp.zeros((tokens, LANES), jnp.float32)
+                    spread[i, pl.ds(c * pitch, tokens), :] = jnp.zeros((tokens, LANES), jnp.float32)
                 return carry
 
             lax.fori_loop(held_slots, dirty[0], blank, 0)
@@ -174,7 +174,7 @@
     layers = filled.shape[0]
     _, tokens, width = held.shape
     flat = tokens * (width // SLICES)
-    pitch = tokens + 8
+    pitch = tokens + 1
     smem = pl.BlockSpec(memory_space=pltpu.SMEM)
     vmem = pl.BlockSpec(memory_space=pltpu.VMEM)
     return pl.pallas_call(
@@ -183,7 +183,7 @@
         in_specs=[smem, smem, vmem],
         out_specs=vmem,
         scratch_shapes=[
-            pltpu.VMEM((pl.cdiv(width, LANES), CAP * pitch, LANES), jnp.float32),
+            pltpu.VMEM((pl.cdiv(width, LANES), (CAP + 1) * pitch, LANES), jnp.float32),
             pltpu.SMEM((1,), jnp.int32),
         ],
         compiler_params=pltpu.CompilerParams(vmem_limit_bytes=VMEM_LIMIT),
@@ -219,9 +219,9 @@
     def batch(b, totals):
         def group(u, totals):
             totals = list(totals)
-            for i in range(tiles):
-                at = pl.ds(pl.multiple_of(u * lanes + i * LANES, LANES), LANES)
-                for s in range(BATCH):
+            for s in range(BATCH):
+                for i in range(tiles):
+                    at = pl.ds(pl.multiple_of(u * lanes + i * LANES, LANES), LANES)
                     exact = raw_ref[b * BATCH + s, :, at].astype(jnp.float32) * by_lane[i]
                     coded = jnp.clip(exact, -127.0, 127.0).astype(jnp.bfloat16)
                     codes[b * BATCH + s, :, at] = coded
@@ -229,7 +229,7 @@
                     totals[i] = totals[i] + miss * miss
             return tuple(totals)
 
-        totals = lax.fori_loop(0, flat // lanes, group, totals, unroll=4)
+        totals = lax.fori_loop(0, flat // lanes, group, totals, unroll=flat // lanes)
         give(b).start()
         return totals
 
@@ -269,7 +269,9 @@
     )(raw)
 
 
-NEIGHBOURS = ([(0, 1), (1, 0), (2, 3), (3, 2)], [(0, 3), (3, 0), (1, 2), (2, 1)])
+def from_others(x, axis):
+    count = lax.axis_size(axis)
+    return [lax.ppermute(x, axis, [(r, (r + k) % count) for r in range(count)]) for k in range(1, count)]
 
 
 def body(block_pool, sel_index, sel_layer, counts):
@@ -279,15 +281,14 @@
     tokens, width = block_pool.shape[1:]
     half = width // SLICES
     peak, *found = local_peaks(block_pool, sel_index, sel_layer, counts, layers)
-    others = [lax.ppermute(peak, "rep", [(r, (r + k) % rep_count) for r in range(rep_count)]) for k in range(1, rep_count)]
+    others = from_others(peak, "rep")
     sent = lay_out(*found)
     peak = functools.reduce(jnp.maximum, others, peak)
     sent = lax.dynamic_update_slice(sent, peak, (0, 0, tokens * half))
     arrived = lax.all_to_all(sent, "own", split_axis=0, concat_axis=0, tiled=True)
 
     codes, steps, error = encode(arrived, half)
-    for pairs in NEIGHBOURS:
-        error = error + lax.ppermute(error, "rep", pairs)
+    error = functools.reduce(jnp.add, from_others(error, "rep"), error)
     denominator = float(own_count * rep_count * CAP * tokens)
     return codes[None, None], steps, error / denominator
 

time: 147 us -> 145 us (0.986)
  waiting for transfers between devices: 10.1 us -> 6.82 us
  starting transfers between devices: 5.37 us -> 7.85 us
    ppermute x5 -> x6, waiting for transfers between devices: 10.1 us -> 6.82 us  [from_others(): lax.ppermute(x, axis, [(r, (r + k) % count) for r in range(count)])]
    ppermute x5 -> x6, starting transfers between devices: 5.37 us -> 7.85 us  [from_others(): lax.ppermute(x, axis, [(r, (r + k) % count) for r in range(count)])]
    pallas_call x1, Pallas kernels: 8.23 us -> 6.52 us  [encode(): pl.pallas_call(encode_kernel, out_shape=[jax.ShapeDtypeStruct((sources, c...]
  transfers between devices with their start and end apart: 5 -> 6, of which waited for: 4 -> 5; matrix products, arithmetic and copies ran while one was open for 0% -> 0% of each run, Pallas kernels for 2% -> 2%
where the time goes in v8:
time: 145 us; the launch traced here: 144 us
  blocking collectives  116 us (80%)
  Pallas kernels  11.9 us (8%)
  starting transfers between devices  7.85 us (5%)
  waiting for transfers between devices  6.82 us (5%)
    all_to_all x1, blocking collectives, body(): lax.all_to_all(sent, 'own', split_axis=0, concat_axis=0, tiled=True)  116 us
    ppermute x6, starting transfers between devices, from_others(): lax.ppermute(x, axis, [(r, (r + k) % count) for r in range(count)])  7.85 us
    ppermute x6, waiting for transfers between devices, from_others(): lax.ppermute(x, axis, [(r, (r + k) % count) for r in range(count)])  6.82 us
    pallas_call x1, Pallas kernels, encode(): pl.pallas_call(encode_kernel, out_shape=[jax.ShapeDtypeStruct((sources, c...  6.52 us
  transfers between devices with their start and end apart: 6, of which 5 were waited for; matrix products, arithmetic and copies ran while one was open for 0% of the time, Pallas kernels for 2%

profile of v8, /device:TPU:32, one launch (start us, length us, event | category | flops | bytes accessed | tf_op | source)
XLA Modules:
  0.0 144.1 jit_solution(1163766980326325643)
XLA Ops:
  1.3 2.6 %peaks.1 = (bf16[32,8,128]{2,1,0:T(8,128)(2,1)S(1)}, bf16[32,64,576]{2,1,0:T(8,128)(2,1)S(1)}, s32[128]{0:T(128)S(4)}, s32[16]{0:T(128)S(4)}) custom-call(s32[32]{0:T(128)} %index_ref.1, s32[32]{0:T(128)} %layer_ref.1, s32[1]{0:T(128)S(6)} %copy.8.count_ref, bf16[64,64,576]{2,1,0:T(8,128)(2,1)} %pool_ref.1), custom_call_target="tpu_custom_call" | custom-call | flops 20000000 | bytes 2500000 | tf_op jit(solution)/shard_map/peaks/pallas_call | solution.py:97
  3.8 2.9 %collective-permute-start.2 = (bf16[32,8,128]{2,1,0:T(8,128)(2,1)S(1)}, bf16[32,8,128]{2,1,0:T(8,128)(2,1)S(1)}, u32[]{:S(2)}, u32[]{:S(2)}) collective-permute-start(bf16[32,8,128]{2,1,0:T(8,128)(2,1)S(1)} %get-tuple-element.13), channel_id=1, source_target_pairs={{0,3},{1,0},{2,1},{3,2},{4,7},{5,4},{6,5},{7,6},{8,11},{9,8},{10,9... | collective-permute-start | bytes 196616 | tf_op jit(solution)/shard_map/ppermute | solution.py:274
  6.8 0.6 collective-permute-start.1
  7.4 1.0 collective-permute-start
  8.4 2.8 %lay_out.1 = bf16[32,8,18560]{2,1,0:T(8,128)(2,1)S(1)} custom-call(s32[128]{0:T(128)S(4)} %get-tuple-element.10.slots, s32[16]{0:T(128)S(4)} %get-tuple-element.11.filled, bf16[32,64,576]{2,1,0:T(8,128)(2,1)S(1)} %get-tuple-element.12.held), custom_call_target="tpu_custom_call" | custom-call | flops 200000000 | bytes 12000000 | tf_op jit(solution)/shard_map/lay_out/pallas_call | solution.py:180
  11.2 0.0 collective-permute-done.2
  11.2 1.3 collective-permute-done.1
  12.6 0.7 collective-permute-done
  13.3 0.1 maximum_dynamic-update-slice_fusion
  13.3 115.6 %all_to_all.5.raw_ref = bf16[32,8,18560]{2,1,0:T(8,128)(2,1)S(1)} all-to-all(bf16[32,8,18560]{2,1,0:T(8,128)(2,1)S(1)} %maximum_dynamic-update-slice_fusion), channel_id=1, replica_groups=mesh['own'=32,'rep'=4] {'own'}, dimensions={0} | all-to-all | bytes 19005440 | tf_op jit(solution)/shard_map/all_to_all | solution.py:288
  128.9 6.5 %encode.1 = (bf16[32,8,18432]{2,1,0:T(8,128)(2,1)}, f32[1,288]{1,0:T(1,128)}, f32[1,288]{1,0:T(1,128)S(1)}) custom-call(bf16[32,8,18560]{2,1,0:T(8,128)(2,1)S(1)} %all_to_all.5.raw_ref), custom_call_target="tpu_custom_call" | custom-call | flops 80000000 | bytes 19000000 | tf_op jit(solution)/shard_map/encode/pallas_call | solution.py:252
  135.4 1.2 collective-permute-start.5
  136.6 2.1 %collective-permute-start.4 = (f32[1,288]{1,0:T(1,128)S(1)}, f32[1,288]{1,0:T(1,128)S(1)}, u32[]{:S(2)}, u32[]{:S(2)}) collective-permute-start(f32[1,288]{1,0:T(1,128)S(1)} %get-tuple-element.16), channel_id=1, source_target_pairs={{0,2},{1,3},{2,0},{3,1},{4,6},{5,7},{6,4},{7,5},{8,10},{9,11},{10,... | collective-permute-start | bytes 3464 | tf_op jit(solution)/shard_map/ppermute | solution.py:274
  138.7 0.0 collective-permute-start.3
  138.7 0.3 collective-permute-done.5
  139.1 2.6 %collective-permute-done.4 = f32[1,288]{1,0:T(1,128)S(1)} collective-permute-done((f32[1,288]{1,0:T(1,128)S(1)}, f32[1,288]{1,0:T(1,128)S(1)}, u32[]{:S(2)}, u32[]{:S(2)}) %collective-permute-start.4) | collective-permute-done | bytes 1184 | tf_op jit(solution)/shard_map/ppermute | solution.py:274
  141.7 1.8 %collective-permute-done.3 = f32[1,288]{1,0:T(1,128)S(1)} collective-permute-done((f32[1,288]{1,0:T(1,128)S(1)}, f32[1,288]{1,0:T(1,128)S(1)}, u32[]{:S(2)}, u32[]{:S(2)}) %collective-permute-start.3) | collective-permute-done | bytes 1184 | tf_op jit(solution)/shard_map/ppermute | solution.py:274
  143.5 0.6 add_multiply_fusion
Async XLA Ops:
  3.8 7.4 %collective-permute-start.2 = (bf16[32,8,128]{2,1,0:T(8,128)(2,1)S(1)}, bf16[32,8,128]{2,1,0:T(8,128)(2,1)S(1)}, u32[]{:S(2)}, u32[]{:S(2)}) collective-permute-start(bf16[32,8,128]{2,1,0:T(8,128)(2,1)S(1)} %get-tuple-element.13), channel_id=1, source_target_pairs={{0,3},{1,0},{2,1},{3,2},{4,7},{5,4},{6,5},{7,6},{8,11},{9,8},{10,9... | collective-permute-start | bytes 196616 | tf_op jit(solution)/shard_map/ppermute | solution.py:274
  6.8 5.8 %collective-permute-start.1 = (bf16[32,8,128]{2,1,0:T(8,128)(2,1)S(1)}, bf16[32,8,128]{2,1,0:T(8,128)(2,1)S(1)}, u32[]{:S(2)}, u32[]{:S(2)}) collective-permute-start(bf16[32,8,128]{2,1,0:T(8,128)(2,1)S(1)} %get-tuple-element.13), channel_id=1, source_target_pairs={{0,2},{1,3},{2,0},{3,1},{4,6},{5,7},{6,4},{7,5},{8,10},{9,11},{10,... | collective-permute-start | bytes 196616 | tf_op jit(solution)/shard_map/ppermute | solution.py:274
  7.4 5.8 %collective-permute-start = (bf16[32,8,128]{2,1,0:T(8,128)(2,1)S(1)}, bf16[32,8,128]{2,1,0:T(8,128)(2,1)S(1)}, u32[]{:S(2)}, u32[]{:S(2)}) collective-permute-start(bf16[32,8,128]{2,1,0:T(8,128)(2,1)S(1)} %get-tuple-element.13), channel_id=1, source_target_pairs={{0,1},{1,2},{2,3},{3,0},{4,5},{5,6},{6,7},{7,4},{8,9},{9,10},{10,1... | collective-permute-start | bytes 196616 | tf_op jit(solution)/shard_map/ppermute | solution.py:274
  135.4 3.6 %collective-permute-start.5 = (f32[1,288]{1,0:T(1,128)S(1)}, f32[1,288]{1,0:T(1,128)S(1)}, u32[]{:S(2)}, u32[]{:S(2)}) collective-permute-start(f32[1,288]{1,0:T(1,128)S(1)} %get-tuple-element.16), channel_id=1, source_target_pairs={{0,3},{1,0},{2,1},{3,2},{4,7},{5,4},{6,5},{7,6},{8,11},{9,8},{10,9... | collective-permute-start | bytes 3464 | tf_op jit(solution)/shard_map/ppermute | solution.py:274
  136.6 5.1 %collective-permute-start.4 = (f32[1,288]{1,0:T(1,128)S(1)}, f32[1,288]{1,0:T(1,128)S(1)}, u32[]{:S(2)}, u32[]{:S(2)}) collective-permute-start(f32[1,288]{1,0:T(1,128)S(1)} %get-tuple-element.16), channel_id=1, source_target_pairs={{0,2},{1,3},{2,0},{3,1},{4,6},{5,7},{6,4},{7,5},{8,10},{9,11},{10,... | collective-permute-start | bytes 3464 | tf_op jit(solution)/shard_map/ppermute | solution.py:274
  138.7 4.8 %collective-permute-start.3 = (f32[1,288]{1,0:T(1,128)S(1)}, f32[1,288]{1,0:T(1,128)S(1)}, u32[]{:S(2)}, u32[]{:S(2)}) collective-permute-start(f32[1,288]{1,0:T(1,128)S(1)} %get-tuple-element.16), channel_id=1, source_target_pairs={{0,1},{1,2},{2,3},{3,0},{4,5},{5,6},{6,7},{7,4},{8,9},{9,10},{10,1... | collective-permute-start | bytes 3464 | tf_op jit(solution)/shard_map/ppermute | solution.py:274

commit v9 on v8

--- a/solution.py
+++ b/solution.py
@@ -195,8 +195,9 @@
 BATCH = 2
 
 
-def encode_kernel(raw_ref, codes_ref, steps_ref, error_ref, codes, inverse, out_sems):
-    sources, cap, flat = codes.shape
+def encode_kernel(raw_ref, codes_ref, steps_ref, error_ref, inverse, codes, out_sems):
+    sources = raw_ref.shape[0]
+    first, cap, flat = codes.shape
     lanes = inverse.shape[1]
     half = lanes // QUAD
     tiles = lanes // LANES
@@ -216,7 +217,7 @@
         inverse[:, i * LANES : (i + 1) * LANES] = 1.0 / tile
     by_lane = [inverse[:, i * LANES : (i + 1) * LANES] for i in range(tiles)]
 
-    def batch(b, totals):
+    def batch(b, totals, coding):
         def group(u, totals):
             totals = list(totals)
             for s in range(BATCH):
@@ -224,28 +225,30 @@
                     at = pl.ds(pl.multiple_of(u * lanes + i * LANES, LANES), LANES)
                     exact = raw_ref[b * BATCH + s, :, at].astype(jnp.float32) * by_lane[i]
                     coded = jnp.clip(exact, -127.0, 127.0).astype(jnp.bfloat16)
-                    codes[b * BATCH + s, :, at] = coded
+                    if coding:
+                        codes[b * BATCH + s, :, at] = coded
                     miss = exact - coded.astype(jnp.float32)
                     totals[i] = totals[i] + miss * miss
             return tuple(totals)
 
         totals = lax.fori_loop(0, flat // lanes, group, totals, unroll=flat // lanes)
-        give(b).start()
+        if coding:
+            give(b).start()
         return totals
 
-    totals = lax.fori_loop(
-        0, batches, batch, tuple(jnp.zeros((cap, LANES), jnp.float32) for _ in range(tiles))
-    )
+    totals = tuple(jnp.zeros((cap, LANES), jnp.float32) for _ in range(tiles))
+    totals = lax.fori_loop(0, first // BATCH, functools.partial(batch, coding=True), totals)
+    totals = lax.fori_loop(first // BATCH, batches, functools.partial(batch, coding=False), totals)
     whole = jnp.concatenate([jnp.sum(t, axis=0, keepdims=True) for t in totals], axis=1)
     error = whole[:, :half]
     for q in range(1, QUAD):
         error = error + whole[:, q * half : (q + 1) * half]
     error_ref[...] = error
-    for b in range(batches):
+    for b in range(first // BATCH):
         give(b).wait()
 
 
-def encode(raw, half):
+def encode(raw, half, first):
     sources, cap, size = raw.shape
     flat = size - LANES
     vmem = pl.BlockSpec(memory_space=pltpu.VMEM)
@@ -255,18 +258,62 @@
             jax.ShapeDtypeStruct((sources, cap, flat), jnp.bfloat16),
             jax.ShapeDtypeStruct((1, half), jnp.float32),
             pltpu.VMEM((1, half), jnp.float32),
+            pltpu.VMEM((cap, QUAD * half), jnp.float32),
         ],
         in_specs=[vmem],
-        out_specs=[pl.BlockSpec(memory_space=pltpu.HBM), vmem, vmem],
+        out_specs=[pl.BlockSpec(memory_space=pltpu.HBM), vmem, vmem, vmem],
         scratch_shapes=[
-            pltpu.VMEM((sources, cap, flat), jnp.bfloat16),
-            pltpu.VMEM((cap, QUAD * half), jnp.float32),
-            pltpu.SemaphoreType.DMA((sources // BATCH,)),
+            pltpu.VMEM((first, cap, flat), jnp.bfloat16),
+            pltpu.SemaphoreType.DMA((first // BATCH,)),
         ],
         compiler_params=pltpu.CompilerParams(vmem_limit_bytes=VMEM_LIMIT),
         cost_estimate=pl.CostEstimate(flops=80_000_000, bytes_accessed=19_000_000, transcendentals=0),
         name="encode",
     )(raw)
+
+
+def encode_rest_kernel(raw_ref, inverse, _, codes_ref, codes, out_sems):
+    count, _, flat = codes.shape
+    first = raw_ref.shape[0] - count
+    lanes = inverse.shape[1]
+    by_lane = [inverse[:, i : i + LANES] for i in range(0, lanes, LANES)]
+
+    def give(b):
+        here = pl.ds(b * BATCH, BATCH)
+        return pltpu.make_async_copy(codes.at[here], codes_ref.at[pl.ds(first + b * BATCH, BATCH)], out_sems.at[b])
+
+    def batch(b, carry):
+        for s in range(BATCH):
+            for i in range(flat // LANES):
+                at = slice(i * LANES, (i + 1) * LANES)
+                exact = raw_ref[first + b * BATCH + s, :, at].astype(jnp.float32) * by_lane[i % len(by_lane)]
+                codes[b * BATCH + s, :, at] = jnp.clip(exact, -127.0, 127.0).astype(jnp.bfloat16)
+        give(b).start()
+        return carry
+
+    lax.fori_loop(0, count // BATCH, batch, 0)
+    for b in range(count // BATCH):
+        give(b).wait()
+
+
+def encode_rest(raw, inverse, codes, first):
+    rest = raw.shape[0] - first
+    vmem = pl.BlockSpec(memory_space=pltpu.VMEM)
+    hbm = pl.BlockSpec(memory_space=pltpu.HBM)
+    return pl.pallas_call(
+        encode_rest_kernel,
+        out_shape=jax.ShapeDtypeStruct(codes.shape, codes.dtype),
+        in_specs=[vmem, vmem, hbm],
+        out_specs=hbm,
+        scratch_shapes=[
+            pltpu.VMEM((rest, *codes.shape[1:]), codes.dtype),
+            pltpu.SemaphoreType.DMA((rest // BATCH,)),
+        ],
+        input_output_aliases={2: 0},
+        compiler_params=pltpu.CompilerParams(vmem_limit_bytes=VMEM_LIMIT),
+        cost_estimate=pl.CostEstimate(flops=200_000_000, bytes_accessed=5_000_000, transcendentals=0),
+        name="encode_rest",
+    )(raw, inverse, codes)
 
 
 def from_others(x, axis):
@@ -287,8 +334,11 @@
     sent = lax.dynamic_update_slice(sent, peak, (0, 0, tokens * half))
     arrived = lax.all_to_all(sent, "own", split_axis=0, concat_axis=0, tiled=True)
 
-    codes, steps, error = encode(arrived, half)
-    error = functools.reduce(jnp.add, from_others(error, "rep"), error)
+    first = own_count * 3 // 4
+    codes, steps, error, inverse = encode(arrived, half, first)
+    others = from_others(error, "rep")
+    codes = encode_rest(arrived, inverse, codes, first)
+    error = functools.reduce(jnp.add, others, error)
     denominator = float(own_count * rep_count * CAP * tokens)
     return codes[None, None], steps, error / denominator
 

time: 145 us -> 145 us (level)
  Pallas kernels: 11.9 us -> 14.3 us
  waiting for transfers between devices: 6.82 us -> 4.58 us
    ppermute x6, waiting for transfers between devices: 6.82 us -> 4.58 us  [from_others(): lax.ppermute(x, axis, [(r, (r + k) % count) for r in range(count)])]
    pallas_call x0 -> x1, Pallas kernels: none -> 1.59 us  [encode_rest(): pl.pallas_call(encode_rest_kernel, out_shape=jax.ShapeDtypeStruct(codes.s...]
  transfers between devices with their start and end apart: 6 -> 6, of which waited for: 5 -> 4; matrix products, arithmetic and copies ran while one was open for 0% -> 0% of each run, Pallas kernels for 2% -> 4%
where the time goes in v9:
time: 145 us; the launch traced here: 143 us
  blocking collectives  115 us (79%)
  Pallas kernels  14.3 us (10%)
  starting transfers between devices  7.5 us (5%)
  waiting for transfers between devices  4.58 us (3%)
    all_to_all x1, blocking collectives, body(): lax.all_to_all(sent, 'own', split_axis=0, concat_axis=0, tiled=True)  115 us
    ppermute x6, starting transfers between devices, from_others(): lax.ppermute(x, axis, [(r, (r + k) % count) for r in range(count)])  7.5 us
    pallas_call x1, Pallas kernels, encode(): pl.pallas_call(encode_kernel, out_shape=[jax.ShapeDtypeStruct((sources, c...  5.79 us
    ppermute x6, waiting for transfers between devices, from_others(): lax.ppermute(x, axis, [(r, (r + k) % count) for r in range(count)])  4.58 us
    pallas_call x1, Pallas kernels, lay_out(): pl.pallas_call(lay_out_kernel, out_shape=pltpu.VMEM((layers * SLICES, CAP...  3.91 us
    pallas_call x1, Pallas kernels, local_peaks(): pl.pallas_call(peak_kernel, out_shape=[pltpu.VMEM((layers * SLICES, CAP,...  3.01 us
  transfers between devices with their start and end apart: 6, of which 4 were waited for; matrix products, arithmetic and copies ran while one was open for 0% of the time, Pallas kernels for 4%

profile of v9, /device:TPU:32, one launch (start us, length us, event | category | flops | bytes accessed | tf_op | source)
XLA Modules:
  0.0 143.1 jit_solution(16121547843153111108)
XLA Ops:
  1.3 3.0 %peaks.1 = (bf16[32,8,128]{2,1,0:T(8,128)(2,1)S(1)}, bf16[32,64,576]{2,1,0:T(8,128)(2,1)S(1)}, s32[128]{0:T(128)S(4)}, s32[16]{0:T(128)S(4)}) custom-call(s32[32]{0:T(128)} %index_ref.1, s32[32]{0:T(128)} %layer_ref.1, s32[1]{0:T(128)S(6)} %copy.10.count_ref, bf16[64,64,576]{2,1,0:T(8,128)(2,1)} %pool_ref.1), custom_call_target="tpu_custom_call" | custom-call | flops 20000000 | bytes 2500000 | tf_op jit(solution)/shard_map/peaks/pallas_call | solution.py:97
  4.3 2.6 %collective-permute-start.2 = (bf16[32,8,128]{2,1,0:T(8,128)(2,1)S(1)}, bf16[32,8,128]{2,1,0:T(8,128)(2,1)S(1)}, u32[]{:S(2)}, u32[]{:S(2)}) collective-permute-start(bf16[32,8,128]{2,1,0:T(8,128)(2,1)S(1)} %get-tuple-element.14), channel_id=1, source_target_pairs={{0,3},{1,0},{2,1},{3,2},{4,7},{5,4},{6,5},{7,6},{8,11},{9,8},{10,9... | collective-permute-start | bytes 196616 | tf_op jit(solution)/shard_map/ppermute | solution.py:321
  6.9 0.5 collective-permute-start.1
  7.4 0.9 collective-permute-start
  8.3 3.9 %lay_out.1 = bf16[32,8,18560]{2,1,0:T(8,128)(2,1)S(1)} custom-call(s32[128]{0:T(128)S(4)} %get-tuple-element.11.slots, s32[16]{0:T(128)S(4)} %get-tuple-element.12.filled, bf16[32,64,576]{2,1,0:T(8,128)(2,1)S(1)} %get-tuple-element.13.held), custom_call_target="tpu_custom_call" | custom-call | flops 200000000 | bytes 12000000 | tf_op jit(solution)/shard_map/lay_out/pallas_call | solution.py:180
  12.2 0.0 collective-permute-done.2
  12.3 1.0 collective-permute-done.1
  13.2 0.4 collective-permute-done
  13.7 0.1 maximum_dynamic-update-slice_fusion
  13.7 114.8 %all_to_all.5.raw_ref = bf16[32,8,18560]{2,1,0:T(8,128)(2,1)S(1)} all-to-all(bf16[32,8,18560]{2,1,0:T(8,128)(2,1)S(1)} %maximum_dynamic-update-slice_fusion), channel_id=1, replica_groups=mesh['own'=32,'rep'=4] {'own'}, dimensions={0} | all-to-all | bytes 19005440 | tf_op jit(solution)/shard_map/all_to_all | solution.py:335
  128.5 5.8 %encode.1 = (bf16[32,8,18432]{2,1,0:T(8,128)(2,1)}, f32[1,288]{1,0:T(1,128)}, f32[1,288]{1,0:T(1,128)S(1)}, f32[8,1152]{1,0:T(8,128)S(1)}) custom-call(bf16[32,8,18560]{2,1,0:T(8,128)(2,1)S(1)} %all_to_all.5.raw_ref), custom_call_target="tpu_custom_call" | custom-call | flops 80000000 | bytes 19000000 | tf_op jit(solution)/shard_map/encode/pallas_call | solution.py:255
  134.3 0.6 collective-permute-start.5
  134.9 2.8 %collective-permute-start.4 = (f32[1,288]{1,0:T(1,128)S(1)}, f32[1,288]{1,0:T(1,128)S(1)}, u32[]{:S(2)}, u32[]{:S(2)}) collective-permute-start(f32[1,288]{1,0:T(1,128)S(1)} %get-tuple-element.18), channel_id=1, source_target_pairs={{0,2},{1,3},{2,0},{3,1},{4,6},{5,7},{6,4},{7,5},{8,10},{9,11},{10,... | collective-permute-start | bytes 3464 | tf_op jit(solution)/shard_map/ppermute | solution.py:321
  137.7 0.0 collective-permute-start.3
  137.7 1.6 %encode_rest.1 = bf16[32,8,18432]{2,1,0:T(8,128)(2,1)} custom-call(bf16[32,8,18560]{2,1,0:T(8,128)(2,1)S(1)} %all_to_all.5.raw_ref, f32[8,1152]{1,0:T(8,128)S(1)} %get-tuple-element.15.inverse, bf16[32,8,18432]{2,1,0:T(8,128)(2,1)} %get-tuple-element.16._), custom_call_target="tpu_custom_call", output_to_operand_aliasing={{}: (2, {})} | custom-call | flops 200000000 | bytes 5000000 | tf_op jit(solution)/shard_map/encode_rest/pallas_call | solution.py:303
  139.3 0.0 collective-permute-done.5
  139.4 0.6 collective-permute-done.4
  140.0 2.5 %collective-permute-done.3 = f32[1,288]{1,0:T(1,128)S(1)} collective-permute-done((f32[1,288]{1,0:T(1,128)S(1)}, f32[1,288]{1,0:T(1,128)S(1)}, u32[]{:S(2)}, u32[]{:S(2)}) %collective-permute-start.3) | collective-permute-done | bytes 1184 | tf_op jit(solution)/shard_map/ppermute | solution.py:321
  142.5 0.6 add_multiply_fusion
Async XLA Ops:
  4.3 8.0 %collective-permute-start.2 = (bf16[32,8,128]{2,1,0:T(8,128)(2,1)S(1)}, bf16[32,8,128]{2,1,0:T(8,128)(2,1)S(1)}, u32[]{:S(2)}, u32[]{:S(2)}) collective-permute-start(bf16[32,8,128]{2,1,0:T(8,128)(2,1)S(1)} %get-tuple-element.14), channel_id=1, source_target_pairs={{0,3},{1,0},{2,1},{3,2},{4,7},{5,4},{6,5},{7,6},{8,11},{9,8},{10,9... | collective-permute-start | bytes 196616 | tf_op jit(solution)/shard_map/ppermute | solution.py:321
  6.9 6.3 %collective-permute-start.1 = (bf16[32,8,128]{2,1,0:T(8,128)(2,1)S(1)}, bf16[32,8,128]{2,1,0:T(8,128)(2,1)S(1)}, u32[]{:S(2)}, u32[]{:S(2)}) collective-permute-start(bf16[32,8,128]{2,1,0:T(8,128)(2,1)S(1)} %get-tuple-element.14), channel_id=1, source_target_pairs={{0,2},{1,3},{2,0},{3,1},{4,6},{5,7},{6,4},{7,5},{8,10},{9,11},{10,... | collective-permute-start | bytes 196616 | tf_op jit(solution)/shard_map/ppermute | solution.py:321
  7.4 6.2 %collective-permute-start = (bf16[32,8,128]{2,1,0:T(8,128)(2,1)S(1)}, bf16[32,8,128]{2,1,0:T(8,128)(2,1)S(1)}, u32[]{:S(2)}, u32[]{:S(2)}) collective-permute-start(bf16[32,8,128]{2,1,0:T(8,128)(2,1)S(1)} %get-tuple-element.14), channel_id=1, source_target_pairs={{0,1},{1,2},{2,3},{3,0},{4,5},{5,6},{6,7},{7,4},{8,9},{9,10},{10,1... | collective-permute-start | bytes 196616 | tf_op jit(solution)/shard_map/ppermute | solution.py:321
  134.3 5.1 %collective-permute-start.5 = (f32[1,288]{1,0:T(1,128)S(1)}, f32[1,288]{1,0:T(1,128)S(1)}, u32[]{:S(2)}, u32[]{:S(2)}) collective-permute-start(f32[1,288]{1,0:T(1,128)S(1)} %get-tuple-element.18), channel_id=1, source_target_pairs={{0,3},{1,0},{2,1},{3,2},{4,7},{5,4},{6,5},{7,6},{8,11},{9,8},{10,9... | collective-permute-start | bytes 3464 | tf_op jit(solution)/shard_map/ppermute | solution.py:321
  134.9 5.1 %collective-permute-start.4 = (f32[1,288]{1,0:T(1,128)S(1)}, f32[1,288]{1,0:T(1,128)S(1)}, u32[]{:S(2)}, u32[]{:S(2)}) collective-permute-start(f32[1,288]{1,0:T(1,128)S(1)} %get-tuple-element.18), channel_id=1, source_target_pairs={{0,2},{1,3},{2,0},{3,1},{4,6},{5,7},{6,4},{7,5},{8,10},{9,11},{10,... | collective-permute-start | bytes 3464 | tf_op jit(solution)/shard_map/ppermute | solution.py:321
  137.7 4.8 %collective-permute-start.3 = (f32[1,288]{1,0:T(1,128)S(1)}, f32[1,288]{1,0:T(1,128)S(1)}, u32[]{:S(2)}, u32[]{:S(2)}) collective-permute-start(f32[1,288]{1,0:T(1,128)S(1)} %get-tuple-element.18), channel_id=1, source_target_pairs={{0,1},{1,2},{2,3},{3,0},{4,5},{5,6},{6,7},{7,4},{8,9},{9,10},{10,1... | collective-permute-start | bytes 3464 | tf_op jit(solution)/shard_map/ppermute | solution.py:321

commit v10 on v8

--- a/solution.py
+++ b/solution.py
@@ -271,7 +271,8 @@
 
 def from_others(x, axis):
     count = lax.axis_size(axis)
-    return [lax.ppermute(x, axis, [(r, (r + k) % count) for r in range(count)]) for k in range(1, count)]
+    hops = sorted(range(1, count), key=lambda k: min(k, count - k))
+    return [lax.ppermute(x, axis, [(r, (r + k) % count) for r in range(count)]) for k in hops]
 
 
 def body(block_pool, sel_index, sel_layer, counts):

time: 145 us -> 145 us (level)
  transfers between devices with their start and end apart: 6 -> 6, of which waited for: 5 -> 3; matrix products, arithmetic and copies ran while one was open for 0% -> 0% of each run, Pallas kernels for 2% -> 2%
where the time goes in v10:
time: 145 us; the launch traced here: 143 us
  blocking collectives  115 us (79%)
  Pallas kernels  11.3 us (8%)
  starting transfers between devices  8.16 us (6%)
  waiting for transfers between devices  6.39 us (4%)
    all_to_all x1, blocking collectives, body(): lax.all_to_all(sent, 'own', split_axis=0, concat_axis=0, tiled=True)  115 us
    ppermute x6, starting transfers between devices, from_others(): lax.ppermute(x, axis, [(r, (r + k) % count) for r in range(count)])  8.16 us
    pallas_call x1, Pallas kernels, encode(): pl.pallas_call(encode_kernel, out_shape=[jax.ShapeDtypeStruct((sources, c...  6.52 us
    ppermute x6, waiting for transfers between devices, from_others(): lax.ppermute(x, axis, [(r, (r + k) % count) for r in range(count)])  6.39 us
  transfers between devices with their start and end apart: 6, of which 3 were waited for; matrix products, arithmetic and copies ran while one was open for 0% of the time, Pallas kernels for 2%

profile of v10, /device:TPU:32, one launch (start us, length us, event | category | flops | bytes accessed | tf_op | source)
XLA Modules:
  0.0 143.0 jit_solution(15300588213159300731)
XLA Ops:
  1.3 2.5 %peaks.1 = (bf16[32,8,128]{2,1,0:T(8,128)(2,1)S(1)}, bf16[32,64,576]{2,1,0:T(8,128)(2,1)S(1)}, s32[128]{0:T(128)S(4)}, s32[16]{0:T(128)S(4)}) custom-call(s32[32]{0:T(128)} %index_ref.1, s32[32]{0:T(128)} %layer_ref.1, s32[1]{0:T(128)S(6)} %copy.8.count_ref, bf16[64,64,576]{2,1,0:T(8,128)(2,1)} %pool_ref.1), custom_call_target="tpu_custom_call" | custom-call | flops 20000000 | bytes 2500000 | tf_op jit(solution)/shard_map/peaks/pallas_call | solution.py:97
  3.8 3.8 %collective-permute-start.2 = (bf16[32,8,128]{2,1,0:T(8,128)(2,1)S(1)}, bf16[32,8,128]{2,1,0:T(8,128)(2,1)S(1)}, u32[]{:S(2)}, u32[]{:S(2)}) collective-permute-start(bf16[32,8,128]{2,1,0:T(8,128)(2,1)S(1)} %get-tuple-element.13), channel_id=1, source_target_pairs={{0,2},{1,3},{2,0},{3,1},{4,6},{5,7},{6,4},{7,5},{8,10},{9,11},{10,... | collective-permute-start | bytes 196616 | tf_op jit(solution)/shard_map/ppermute | solution.py:275
  7.6 0.4 collective-permute-start.1
  8.0 1.6 %collective-permute-start = (bf16[32,8,128]{2,1,0:T(8,128)(2,1)S(1)}, bf16[32,8,128]{2,1,0:T(8,128)(2,1)S(1)}, u32[]{:S(2)}, u32[]{:S(2)}) collective-permute-start(bf16[32,8,128]{2,1,0:T(8,128)(2,1)S(1)} %get-tuple-element.13), channel_id=1, source_target_pairs={{0,1},{1,2},{2,3},{3,0},{4,5},{5,6},{6,7},{7,4},{8,9},{9,10},{10,1... | collective-permute-start | bytes 196616 | tf_op jit(solution)/shard_map/ppermute | solution.py:275
  9.6 2.2 %lay_out.1 = bf16[32,8,18560]{2,1,0:T(8,128)(2,1)S(1)} custom-call(s32[128]{0:T(128)S(4)} %get-tuple-element.10.slots, s32[16]{0:T(128)S(4)} %get-tuple-element.11.filled, bf16[32,64,576]{2,1,0:T(8,128)(2,1)S(1)} %get-tuple-element.12.held), custom_call_target="tpu_custom_call" | custom-call | flops 200000000 | bytes 12000000 | tf_op jit(solution)/shard_map/lay_out/pallas_call | solution.py:180
  11.8 0.0 collective-permute-done.2
  11.8 0.0 collective-permute-done.1
  11.9 1.6 %collective-permute-done = bf16[32,8,128]{2,1,0:T(8,128)(2,1)S(1)} collective-permute-done((bf16[32,8,128]{2,1,0:T(8,128)(2,1)S(1)}, bf16[32,8,128]{2,1,0:T(8,128)(2,1)S(1)}, u32[]{:S(2)}, u32[]{:S(2)}) %collective-permute-start) | collective-permute-done | bytes 65568 | tf_op jit(solution)/shard_map/ppermute | solution.py:275
  13.5 0.1 maximum_dynamic-update-slice_fusion
  13.5 115.2 %all_to_all.5.raw_ref = bf16[32,8,18560]{2,1,0:T(8,128)(2,1)S(1)} all-to-all(bf16[32,8,18560]{2,1,0:T(8,128)(2,1)S(1)} %maximum_dynamic-update-slice_fusion), channel_id=1, replica_groups=mesh['own'=32,'rep'=4] {'own'}, dimensions={0} | all-to-all | bytes 19005440 | tf_op jit(solution)/shard_map/all_to_all | solution.py:289
  128.8 6.5 %encode.1 = (bf16[32,8,18432]{2,1,0:T(8,128)(2,1)}, f32[1,288]{1,0:T(1,128)}, f32[1,288]{1,0:T(1,128)S(1)}) custom-call(bf16[32,8,18560]{2,1,0:T(8,128)(2,1)S(1)} %all_to_all.5.raw_ref), custom_call_target="tpu_custom_call" | custom-call | flops 80000000 | bytes 19000000 | tf_op jit(solution)/shard_map/encode/pallas_call | solution.py:252
  135.3 0.3 collective-permute-start.5
  135.6 2.0 %collective-permute-start.4 = (f32[1,288]{1,0:T(1,128)S(1)}, f32[1,288]{1,0:T(1,128)S(1)}, u32[]{:S(2)}, u32[]{:S(2)}) collective-permute-start(f32[1,288]{1,0:T(1,128)S(1)} %get-tuple-element.16), channel_id=1, source_target_pairs={{0,3},{1,0},{2,1},{3,2},{4,7},{5,4},{6,5},{7,6},{8,11},{9,8},{10,9... | collective-permute-start | bytes 3464 | tf_op jit(solution)/shard_map/ppermute | solution.py:275
  137.7 0.0 collective-permute-start.3
  137.7 2.8 %collective-permute-done.5 = f32[1,288]{1,0:T(1,128)S(1)} collective-permute-done((f32[1,288]{1,0:T(1,128)S(1)}, f32[1,288]{1,0:T(1,128)S(1)}, u32[]{:S(2)}, u32[]{:S(2)}) %collective-permute-start.5) | collective-permute-done | bytes 1184 | tf_op jit(solution)/shard_map/ppermute | solution.py:275
  140.5 0.0 collective-permute-done.4
  140.5 2.0 %collective-permute-done.3 = f32[1,288]{1,0:T(1,128)S(1)} collective-permute-done((f32[1,288]{1,0:T(1,128)S(1)}, f32[1,288]{1,0:T(1,128)S(1)}, u32[]{:S(2)}, u32[]{:S(2)}) %collective-permute-start.3) | collective-permute-done | bytes 1184 | tf_op jit(solution)/shard_map/ppermute | solution.py:275
  142.5 0.6 add_multiply_fusion
Async XLA Ops:
  3.8 8.0 %collective-permute-start.2 = (bf16[32,8,128]{2,1,0:T(8,128)(2,1)S(1)}, bf16[32,8,128]{2,1,0:T(8,128)(2,1)S(1)}, u32[]{:S(2)}, u32[]{:S(2)}) collective-permute-start(bf16[32,8,128]{2,1,0:T(8,128)(2,1)S(1)} %get-tuple-element.13), channel_id=1, source_target_pairs={{0,2},{1,3},{2,0},{3,1},{4,6},{5,7},{6,4},{7,5},{8,10},{9,11},{10,... | collective-permute-start | bytes 196616 | tf_op jit(solution)/shard_map/ppermute | solution.py:275
  7.6 4.3 %collective-permute-start.1 = (bf16[32,8,128]{2,1,0:T(8,128)(2,1)S(1)}, bf16[32,8,128]{2,1,0:T(8,128)(2,1)S(1)}, u32[]{:S(2)}, u32[]{:S(2)}) collective-permute-start(bf16[32,8,128]{2,1,0:T(8,128)(2,1)S(1)} %get-tuple-element.13), channel_id=1, source_target_pairs={{0,3},{1,0},{2,1},{3,2},{4,7},{5,4},{6,5},{7,6},{8,11},{9,8},{10,9... | collective-permute-start | bytes 196616 | tf_op jit(solution)/shard_map/ppermute | solution.py:275
  8.0 5.5 %collective-permute-start = (bf16[32,8,128]{2,1,0:T(8,128)(2,1)S(1)}, bf16[32,8,128]{2,1,0:T(8,128)(2,1)S(1)}, u32[]{:S(2)}, u32[]{:S(2)}) collective-permute-start(bf16[32,8,128]{2,1,0:T(8,128)(2,1)S(1)} %get-tuple-element.13), channel_id=1, source_target_pairs={{0,1},{1,2},{2,3},{3,0},{4,5},{5,6},{6,7},{7,4},{8,9},{9,10},{10,1... | collective-permute-start | bytes 196616 | tf_op jit(solution)/shard_map/ppermute | solution.py:275
  135.3 5.2 %collective-permute-start.5 = (f32[1,288]{1,0:T(1,128)S(1)}, f32[1,288]{1,0:T(1,128)S(1)}, u32[]{:S(2)}, u32[]{:S(2)}) collective-permute-start(f32[1,288]{1,0:T(1,128)S(1)} %get-tuple-element.16), channel_id=1, source_target_pairs={{0,2},{1,3},{2,0},{3,1},{4,6},{5,7},{6,4},{7,5},{8,10},{9,11},{10,... | collective-permute-start | bytes 3464 | tf_op jit(solution)/shard_map/ppermute | solution.py:275
  135.6 4.8 %collective-permute-start.4 = (f32[1,288]{1,0:T(1,128)S(1)}, f32[1,288]{1,0:T(1,128)S(1)}, u32[]{:S(2)}, u32[]{:S(2)}) collective-permute-start(f32[1,288]{1,0:T(1,128)S(1)} %get-tuple-element.16), channel_id=1, source_target_pairs={{0,3},{1,0},{2,1},{3,2},{4,7},{5,4},{6,5},{7,6},{8,11},{9,8},{10,9... | collective-permute-start | bytes 3464 | tf_op jit(solution)/shard_map/ppermute | solution.py:275
  137.7 4.8 %collective-permute-start.3 = (f32[1,288]{1,0:T(1,128)S(1)}, f32[1,288]{1,0:T(1,128)S(1)}, u32[]{:S(2)}, u32[]{:S(2)}) collective-permute-start(f32[1,288]{1,0:T(1,128)S(1)} %get-tuple-element.16), channel_id=1, source_target_pairs={{0,1},{1,2},{2,3},{3,0},{4,5},{5,6},{6,7},{7,4},{8,9},{9,10},{10,1... | collective-permute-start | bytes 3464 | tf_op jit(solution)/shard_map/ppermute | solution.py:275

commit v11 on v9

--- a/solution.py
+++ b/solution.py
@@ -63,8 +63,13 @@
     def wait(j, carry):
         fetch(j).wait()
         layer = layer_ref[j]
-        values = jnp.abs(held[j].astype(jnp.float32)).reshape(tokens // 8, 8, width)
-        acc[layer] = jnp.maximum(acc[layer], jnp.max(values, axis=0))
+        values = jnp.abs(held[j])
+        rows = tokens
+        while rows > 16:
+            rows //= 2
+            values = jnp.maximum(values[:rows], values[rows:])
+        values = values.astype(jnp.float32)
+        acc[layer] = jnp.maximum(acc[layer], jnp.maximum(values[:8], values[8:]))
         return carry
 
     lax.fori_loop(0, live, wait, 0)
@@ -334,7 +339,7 @@
     sent = lax.dynamic_update_slice(sent, peak, (0, 0, tokens * half))
     arrived = lax.all_to_all(sent, "own", split_axis=0, concat_axis=0, tiled=True)
 
-    first = own_count * 3 // 4
+    first = own_count * 7 // 8
     codes, steps, error, inverse = encode(arrived, half, first)
     others = from_others(error, "rep")
     codes = encode_rest(arrived, inverse, codes, first)

time: 145 us -> 144 us (level)
  Pallas kernels: 14.3 us -> 11.9 us
    pallas_call x1, Pallas kernels: 3.91 us -> 2.34 us  [lay_out(): pl.pallas_call(lay_out_kernel, out_shape=pltpu.VMEM((layers * SLICES, CAP...]
  transfers between devices with their start and end apart: 6 -> 6, of which waited for: 4 -> 4; matrix products, arithmetic and copies ran while one was open for 0% -> 0% of each run, Pallas kernels for 4% -> 2%
where the time goes in v11:
time: 144 us; the launch traced here: 142 us
  blocking collectives  115 us (80%)
  Pallas kernels  11.9 us (8%)
  starting transfers between devices  8.02 us (6%)
  waiting for transfers between devices  4.48 us (3%)
    all_to_all x1, blocking collectives, body(): lax.all_to_all(sent, 'own', split_axis=0, concat_axis=0, tiled=True)  115 us
    ppermute x6, starting transfers between devices, from_others(): lax.ppermute(x, axis, [(r, (r + k) % count) for r in range(count)])  8.02 us
    pallas_call x1, Pallas kernels, encode(): pl.pallas_call(encode_kernel, out_shape=[jax.ShapeDtypeStruct((sources, c...  5.9 us
    ppermute x6, waiting for transfers between devices, from_others(): lax.ppermute(x, axis, [(r, (r + k) % count) for r in range(count)])  4.48 us
  transfers between devices with their start and end apart: 6, of which 4 were waited for; matrix products, arithmetic and copies ran while one was open for 0% of the time, Pallas kernels for 2%

profile of v11, /device:TPU:32, one launch (start us, length us, event | category | flops | bytes accessed | tf_op | source)
XLA Modules:
  0.0 141.7 jit_solution(14126603134588560143)
XLA Ops:
  1.3 2.5 %peaks.1 = (bf16[32,8,128]{2,1,0:T(8,128)(2,1)S(1)}, bf16[32,64,576]{2,1,0:T(8,128)(2,1)S(1)}, s32[128]{0:T(128)S(4)}, s32[16]{0:T(128)S(4)}) custom-call(s32[32]{0:T(128)} %index_ref.1, s32[32]{0:T(128)} %layer_ref.1, s32[1]{0:T(128)S(6)} %copy.10.count_ref, bf16[64,64,576]{2,1,0:T(8,128)(2,1)} %pool_ref.1), custom_call_target="tpu_custom_call" | custom-call | flops 20000000 | bytes 2500000 | tf_op jit(solution)/shard_map/peaks/pallas_call | solution.py:102
  3.8 2.9 %collective-permute-start.2 = (bf16[32,8,128]{2,1,0:T(8,128)(2,1)S(1)}, bf16[32,8,128]{2,1,0:T(8,128)(2,1)S(1)}, u32[]{:S(2)}, u32[]{:S(2)}) collective-permute-start(bf16[32,8,128]{2,1,0:T(8,128)(2,1)S(1)} %get-tuple-element.14), channel_id=1, source_target_pairs={{0,3},{1,0},{2,1},{3,2},{4,7},{5,4},{6,5},{7,6},{8,11},{9,8},{10,9... | collective-permute-start | bytes 196616 | tf_op jit(solution)/shard_map/ppermute | solution.py:326
  6.8 0.9 collective-permute-start.1
  7.6 1.3 collective-permute-start
  9.0 2.3 %lay_out.1 = bf16[32,8,18560]{2,1,0:T(8,128)(2,1)S(1)} custom-call(s32[128]{0:T(128)S(4)} %get-tuple-element.11.slots, s32[16]{0:T(128)S(4)} %get-tuple-element.12.filled, bf16[32,64,576]{2,1,0:T(8,128)(2,1)S(1)} %get-tuple-element.13.held), custom_call_target="tpu_custom_call" | custom-call | flops 200000000 | bytes 12000000 | tf_op jit(solution)/shard_map/lay_out/pallas_call | solution.py:185
  11.3 0.0 collective-permute-done.2
  11.3 1.3 collective-permute-done.1
  12.6 0.7 collective-permute-done
  13.3 0.1 maximum_dynamic-update-slice_fusion
  13.4 115.3 %all_to_all.5.raw_ref = bf16[32,8,18560]{2,1,0:T(8,128)(2,1)S(1)} all-to-all(bf16[32,8,18560]{2,1,0:T(8,128)(2,1)S(1)} %maximum_dynamic-update-slice_fusion), channel_id=1, replica_groups=mesh['own'=32,'rep'=4] {'own'}, dimensions={0} | all-to-all | bytes 19005440 | tf_op jit(solution)/shard_map/all_to_all | solution.py:340
  128.6 5.9 %encode.1 = (bf16[32,8,18432]{2,1,0:T(8,128)(2,1)}, f32[1,288]{1,0:T(1,128)}, f32[1,288]{1,0:T(1,128)S(1)}, f32[8,1152]{1,0:T(8,128)S(1)}) custom-call(bf16[32,8,18560]{2,1,0:T(8,128)(2,1)S(1)} %all_to_all.5.raw_ref), custom_call_target="tpu_custom_call" | custom-call | flops 80000000 | bytes 19000000 | tf_op jit(solution)/shard_map/encode/pallas_call | solution.py:260
  134.5 1.1 collective-permute-start.5
  135.7 0.6 collective-permute-start.4
  136.3 1.1 collective-permute-start.3
  137.4 1.2 encode_rest.1
  138.6 0.0 collective-permute-done.5
  138.6 2.2 %collective-permute-done.4 = f32[1,288]{1,0:T(1,128)S(1)} collective-permute-done((f32[1,288]{1,0:T(1,128)S(1)}, f32[1,288]{1,0:T(1,128)S(1)}, u32[]{:S(2)}, u32[]{:S(2)}) %collective-permute-start.4) | collective-permute-done | bytes 1184 | tf_op jit(solution)/shard_map/ppermute | solution.py:326
  140.7 0.3 collective-permute-done.3
  141.1 0.6 add_multiply_fusion
Async XLA Ops:
  3.8 7.5 %collective-permute-start.2 = (bf16[32,8,128]{2,1,0:T(8,128)(2,1)S(1)}, bf16[32,8,128]{2,1,0:T(8,128)(2,1)S(1)}, u32[]{:S(2)}, u32[]{:S(2)}) collective-permute-start(bf16[32,8,128]{2,1,0:T(8,128)(2,1)S(1)} %get-tuple-element.14), channel_id=1, source_target_pairs={{0,3},{1,0},{2,1},{3,2},{4,7},{5,4},{6,5},{7,6},{8,11},{9,8},{10,9... | collective-permute-start | bytes 196616 | tf_op jit(solution)/shard_map/ppermute | solution.py:326
  6.8 5.8 %collective-permute-start.1 = (bf16[32,8,128]{2,1,0:T(8,128)(2,1)S(1)}, bf16[32,8,128]{2,1,0:T(8,128)(2,1)S(1)}, u32[]{:S(2)}, u32[]{:S(2)}) collective-permute-start(bf16[32,8,128]{2,1,0:T(8,128)(2,1)S(1)} %get-tuple-element.14), channel_id=1, source_target_pairs={{0,2},{1,3},{2,0},{3,1},{4,6},{5,7},{6,4},{7,5},{8,10},{9,11},{10,... | collective-permute-start | bytes 196616 | tf_op jit(solution)/shard_map/ppermute | solution.py:326
  7.6 5.7 %collective-permute-start = (bf16[32,8,128]{2,1,0:T(8,128)(2,1)S(1)}, bf16[32,8,128]{2,1,0:T(8,128)(2,1)S(1)}, u32[]{:S(2)}, u32[]{:S(2)}) collective-permute-start(bf16[32,8,128]{2,1,0:T(8,128)(2,1)S(1)} %get-tuple-element.14), channel_id=1, source_target_pairs={{0,1},{1,2},{2,3},{3,0},{4,5},{5,6},{6,7},{7,4},{8,9},{9,10},{10,1... | collective-permute-start | bytes 196616 | tf_op jit(solution)/shard_map/ppermute | solution.py:326
  134.5 4.0 %collective-permute-start.5 = (f32[1,288]{1,0:T(1,128)S(1)}, f32[1,288]{1,0:T(1,128)S(1)}, u32[]{:S(2)}, u32[]{:S(2)}) collective-permute-start(f32[1,288]{1,0:T(1,128)S(1)} %get-tuple-element.18), channel_id=1, source_target_pairs={{0,3},{1,0},{2,1},{3,2},{4,7},{5,4},{6,5},{7,6},{8,11},{9,8},{10,9... | collective-permute-start | bytes 3464 | tf_op jit(solution)/shard_map/ppermute | solution.py:326
  135.7 5.1 %collective-permute-start.4 = (f32[1,288]{1,0:T(1,128)S(1)}, f32[1,288]{1,0:T(1,128)S(1)}, u32[]{:S(2)}, u32[]{:S(2)}) collective-permute-start(f32[1,288]{1,0:T(1,128)S(1)} %get-tuple-element.18), channel_id=1, source_target_pairs={{0,2},{1,3},{2,0},{3,1},{4,6},{5,7},{6,4},{7,5},{8,10},{9,11},{10,... | collective-permute-start | bytes 3464 | tf_op jit(solution)/shard_map/ppermute | solution.py:326
  136.3 4.8 %collective-permute-start.3 = (f32[1,288]{1,0:T(1,128)S(1)}, f32[1,288]{1,0:T(1,128)S(1)}, u32[]{:S(2)}, u32[]{:S(2)}) collective-permute-start(f32[1,288]{1,0:T(1,128)S(1)} %get-tuple-element.18), channel_id=1, source_target_pairs={{0,1},{1,2},{2,3},{3,0},{4,5},{5,6},{6,7},{7,4},{8,9},{9,10},{10,1... | collective-permute-start | bytes 3464 | tf_op jit(solution)/shard_map/ppermute | solution.py:326

commit v12 on v8

--- a/solution.py
+++ b/solution.py
@@ -63,8 +63,13 @@
     def wait(j, carry):
         fetch(j).wait()
         layer = layer_ref[j]
-        values = jnp.abs(held[j].astype(jnp.float32)).reshape(tokens // 8, 8, width)
-        acc[layer] = jnp.maximum(acc[layer], jnp.max(values, axis=0))
+        values = jnp.abs(held[j])
+        rows = tokens
+        while rows > 16:
+            rows //= 2
+            values = jnp.maximum(values[:rows], values[rows:])
+        values = values.astype(jnp.float32)
+        acc[layer] = jnp.maximum(acc[layer], jnp.maximum(values[:8], values[8:]))
         return carry
 
     lax.fori_loop(0, live, wait, 0)

time: 145 us -> 145 us (level); the launches traced: 144 us -> 142 us
  transfers between devices with their start and end apart: 6 -> 6, of which waited for: 5 -> 5; matrix products, arithmetic and copies ran while one was open for 0% -> 0% of each run, Pallas kernels for 2% -> 1%
where the time goes in v12:
time: 145 us; the launch traced here: 142 us
  blocking collectives  115 us (79%)
  Pallas kernels  10.9 us (8%)
  starting transfers between devices  7.73 us (5%)
  waiting for transfers between devices  6.52 us (4%)
    all_to_all x1, blocking collectives, body(): lax.all_to_all(sent, 'own', split_axis=0, concat_axis=0, tiled=True)  115 us
    ppermute x6, starting transfers between devices, from_others(): lax.ppermute(x, axis, [(r, (r + k) % count) for r in range(count)])  7.73 us
    pallas_call x1, Pallas kernels, encode(): pl.pallas_call(encode_kernel, out_shape=[jax.ShapeDtypeStruct((sources, c...  6.52 us
    ppermute x6, waiting for transfers between devices, from_others(): lax.ppermute(x, axis, [(r, (r + k) % count) for r in range(count)])  6.52 us
  transfers between devices with their start and end apart: 6, of which 5 were waited for; matrix products, arithmetic and copies ran while one was open for 0% of the time, Pallas kernels for 1%

profile of v12, /device:TPU:32, one launch (start us, length us, event | category | flops | bytes accessed | tf_op | source)
XLA Modules:
  0.0 142.4 jit_solution(9725405546779260190)
XLA Ops:
  1.3 2.4 %peaks.1 = (bf16[32,8,128]{2,1,0:T(8,128)(2,1)S(1)}, bf16[32,64,576]{2,1,0:T(8,128)(2,1)S(1)}, s32[128]{0:T(128)S(4)}, s32[16]{0:T(128)S(4)}) custom-call(s32[32]{0:T(128)} %index_ref.1, s32[32]{0:T(128)} %layer_ref.1, s32[1]{0:T(128)S(6)} %copy.8.count_ref, bf16[64,64,576]{2,1,0:T(8,128)(2,1)} %pool_ref.1), custom_call_target="tpu_custom_call" | custom-call | flops 20000000 | bytes 2500000 | tf_op jit(solution)/shard_map/peaks/pallas_call | solution.py:102
  3.7 3.2 %collective-permute-start.2 = (bf16[32,8,128]{2,1,0:T(8,128)(2,1)S(1)}, bf16[32,8,128]{2,1,0:T(8,128)(2,1)S(1)}, u32[]{:S(2)}, u32[]{:S(2)}) collective-permute-start(bf16[32,8,128]{2,1,0:T(8,128)(2,1)S(1)} %get-tuple-element.13), channel_id=1, source_target_pairs={{0,3},{1,0},{2,1},{3,2},{4,7},{5,4},{6,5},{7,6},{8,11},{9,8},{10,9... | collective-permute-start | bytes 196616 | tf_op jit(solution)/shard_map/ppermute | solution.py:279
  6.9 0.5 collective-permute-start.1
  7.5 1.0 collective-permute-start
  8.5 1.9 %lay_out.1 = bf16[32,8,18560]{2,1,0:T(8,128)(2,1)S(1)} custom-call(s32[128]{0:T(128)S(4)} %get-tuple-element.10.slots, s32[16]{0:T(128)S(4)} %get-tuple-element.11.filled, bf16[32,64,576]{2,1,0:T(8,128)(2,1)S(1)} %get-tuple-element.12.held), custom_call_target="tpu_custom_call" | custom-call | flops 200000000 | bytes 12000000 | tf_op jit(solution)/shard_map/lay_out/pallas_call | solution.py:185
  10.4 0.0 collective-permute-done.2
  10.4 2.3 %collective-permute-done.1 = bf16[32,8,128]{2,1,0:T(8,128)(2,1)S(1)} collective-permute-done((bf16[32,8,128]{2,1,0:T(8,128)(2,1)S(1)}, bf16[32,8,128]{2,1,0:T(8,128)(2,1)S(1)}, u32[]{:S(2)}, u32[]{:S(2)}) %collective-permute-start.1) | collective-permute-done | bytes 65568 | tf_op jit(solution)/shard_map/ppermute | solution.py:279
  12.7 0.7 collective-permute-done
  13.4 0.1 maximum_dynamic-update-slice_fusion
  13.5 115.3 %all_to_all.5.raw_ref = bf16[32,8,18560]{2,1,0:T(8,128)(2,1)S(1)} all-to-all(bf16[32,8,18560]{2,1,0:T(8,128)(2,1)S(1)} %maximum_dynamic-update-slice_fusion), channel_id=1, replica_groups=mesh['own'=32,'rep'=4] {'own'}, dimensions={0} | all-to-all | bytes 19005440 | tf_op jit(solution)/shard_map/all_to_all | solution.py:293
  128.8 6.5 %encode.1 = (bf16[32,8,18432]{2,1,0:T(8,128)(2,1)}, f32[1,288]{1,0:T(1,128)}, f32[1,288]{1,0:T(1,128)S(1)}) custom-call(bf16[32,8,18560]{2,1,0:T(8,128)(2,1)S(1)} %all_to_all.5.raw_ref), custom_call_target="tpu_custom_call" | custom-call | flops 80000000 | bytes 19000000 | tf_op jit(solution)/shard_map/encode/pallas_call | solution.py:257
  135.3 1.2 collective-permute-start.5
  136.5 0.5 collective-permute-start.4
  137.0 1.3 collective-permute-start.3
  138.3 0.7 collective-permute-done.5
  139.0 2.7 %collective-permute-done.4 = f32[1,288]{1,0:T(1,128)S(1)} collective-permute-done((f32[1,288]{1,0:T(1,128)S(1)}, f32[1,288]{1,0:T(1,128)S(1)}, u32[]{:S(2)}, u32[]{:S(2)}) %collective-permute-start.4) | collective-permute-done | bytes 1184 | tf_op jit(solution)/shard_map/ppermute | solution.py:279
  141.6 0.2 collective-permute-done.3
  141.8 0.6 add_multiply_fusion
Async XLA Ops:
  3.7 6.7 %collective-permute-start.2 = (bf16[32,8,128]{2,1,0:T(8,128)(2,1)S(1)}, bf16[32,8,128]{2,1,0:T(8,128)(2,1)S(1)}, u32[]{:S(2)}, u32[]{:S(2)}) collective-permute-start(bf16[32,8,128]{2,1,0:T(8,128)(2,1)S(1)} %get-tuple-element.13), channel_id=1, source_target_pairs={{0,3},{1,0},{2,1},{3,2},{4,7},{5,4},{6,5},{7,6},{8,11},{9,8},{10,9... | collective-permute-start | bytes 196616 | tf_op jit(solution)/shard_map/ppermute | solution.py:279
  6.9 5.8 %collective-permute-start.1 = (bf16[32,8,128]{2,1,0:T(8,128)(2,1)S(1)}, bf16[32,8,128]{2,1,0:T(8,128)(2,1)S(1)}, u32[]{:S(2)}, u32[]{:S(2)}) collective-permute-start(bf16[32,8,128]{2,1,0:T(8,128)(2,1)S(1)} %get-tuple-element.13), channel_id=1, source_target_pairs={{0,2},{1,3},{2,0},{3,1},{4,6},{5,7},{6,4},{7,5},{8,10},{9,11},{10,... | collective-permute-start | bytes 196616 | tf_op jit(solution)/shard_map/ppermute | solution.py:279
  7.5 5.9 %collective-permute-start = (bf16[32,8,128]{2,1,0:T(8,128)(2,1)S(1)}, bf16[32,8,128]{2,1,0:T(8,128)(2,1)S(1)}, u32[]{:S(2)}, u32[]{:S(2)}) collective-permute-start(bf16[32,8,128]{2,1,0:T(8,128)(2,1)S(1)} %get-tuple-element.13), channel_id=1, source_target_pairs={{0,1},{1,2},{2,3},{3,0},{4,5},{5,6},{6,7},{7,4},{8,9},{9,10},{10,1... | collective-permute-start | bytes 196616 | tf_op jit(solution)/shard_map/ppermute | solution.py:279
  135.3 3.6 %collective-permute-start.5 = (f32[1,288]{1,0:T(1,128)S(1)}, f32[1,288]{1,0:T(1,128)S(1)}, u32[]{:S(2)}, u32[]{:S(2)}) collective-permute-start(f32[1,288]{1,0:T(1,128)S(1)} %get-tuple-element.16), channel_id=1, source_target_pairs={{0,3},{1,0},{2,1},{3,2},{4,7},{5,4},{6,5},{7,6},{8,11},{9,8},{10,9... | collective-permute-start | bytes 3464 | tf_op jit(solution)/shard_map/ppermute | solution.py:279
  136.5 5.1 %collective-permute-start.4 = (f32[1,288]{1,0:T(1,128)S(1)}, f32[1,288]{1,0:T(1,128)S(1)}, u32[]{:S(2)}, u32[]{:S(2)}) collective-permute-start(f32[1,288]{1,0:T(1,128)S(1)} %get-tuple-element.16), channel_id=1, source_target_pairs={{0,2},{1,3},{2,0},{3,1},{4,6},{5,7},{6,4},{7,5},{8,10},{9,11},{10,... | collective-permute-start | bytes 3464 | tf_op jit(solution)/shard_map/ppermute | solution.py:279
  137.0 4.8 %collective-permute-start.3 = (f32[1,288]{1,0:T(1,128)S(1)}, f32[1,288]{1,0:T(1,128)S(1)}, u32[]{:S(2)}, u32[]{:S(2)}) collective-permute-start(f32[1,288]{1,0:T(1,128)S(1)} %get-tuple-element.16), channel_id=1, source_target_pairs={{0,1},{1,2},{2,3},{3,0},{4,5},{5,6},{6,7},{7,4},{8,9},{9,10},{10,1... | collective-permute-start | bytes 3464 | tf_op jit(solution)/shard_map/ppermute | solution.py:279
